TPU v7x, 64 devices: a 2x2x8 block of a 4x4x8 slice. The times are simulated.
64 devices in a mesh: dp: 4 (over x, y), sp: 16 (over z, core).
Axes of the slice: x: 2, y: 2, z: 8, core: 2. Of those that a mesh axis runs over, the one named last changes fastest.
The devices are a block of a 4x4x8 slice.
Arguments:
- x_in: bfloat16 [4, 4096, 2048], P('dp', 'sp'), parts along dimension 0
- grad_y: bfloat16 [4, 4096, 2048], P('dp', 'sp'), parts along dimension 0
- positions: int32 [4, 4096], P('dp', 'sp'), parts along dimension 0
- g_norm: bfloat16 [2048], replicated
- w_query: bfloat16 [2048, 2048], replicated
- w_key: bfloat16 [2048, 2048], replicated
- w_value: bfloat16 [2048, 2048], replicated
- w_out: bfloat16 [2048, 2048], replicated
- g_query: bfloat16 [2048], replicated
- g_key: bfloat16 [2048], replicated
Outputs:
- output 1: bfloat16 [4, 4096, 2048], P('dp', 'sp'), parts along dimension 0
- output 2: bfloat16 [4, 4096, 2048], P('dp', 'sp'), parts along dimension 0
- output 3: float32 [8192], P(('dp', 'sp')), parts along dimension 0
- output 4: float32 [8192, 2048], P(('dp', 'sp')), parts along dimension 0
- output 5: float32 [8192, 2048], P(('dp', 'sp')), parts along dimension 0
- output 6: float32 [8192, 2048], P(('dp', 'sp')), parts along dimension 0
- output 7: float32 [8192, 2048], P(('dp', 'sp')), parts along dimension 0
- output 8: float32 [8192], P(('dp', 'sp')), parts along dimension 0
- output 9: float32 [8192], P(('dp', 'sp')), parts along dimension 0
There are 4 independent parts. A program takes and returns all parts, laid end to end along the dimension named above; an argument that names none is the same for every part.
All inputs are finite; a program needn't handle non-finite values.
Results may differ from a plain program's by a relative error of at most 0.0111848.
Values are sent between devices in bfloat16 or wider.
A program may use at most 768 MiB of HBM per device.

v0:
```python
import functools
import jax
import jax.numpy as jnp
from jax import lax
from jax.sharding import PartitionSpec as P

HEAD_DIM = 128
QUERY_BLOCK = 128
NORM_EPS = 1e-5
ROPE_BASE = 10000.0
NEG_BIG = -1e30


def rope_tables(positions):
    half_dim = HEAD_DIM // 2
    inv_freq = ROPE_BASE ** (-jnp.arange(half_dim, dtype=jnp.float32) * (2.0 / HEAD_DIM))
    angles = positions.astype(jnp.float32)[..., None] * inv_freq
    return jnp.cos(angles)[:, :, None, :], jnp.sin(angles)[:, :, None, :]


def rope_apply(values, cos_t, sin_t):
    half_dim = values.shape[-1] // 2
    first_half = values[..., :half_dim]
    second_half = values[..., half_dim:]
    return jnp.concatenate([first_half * cos_t - second_half * sin_t, second_half * cos_t + first_half * sin_t], axis=-1)


def rope_revert(grads_in, cos_t, sin_t):
    half_dim = grads_in.shape[-1] // 2
    first_half = grads_in[..., :half_dim]
    second_half = grads_in[..., half_dim:]
    return jnp.concatenate([first_half * cos_t + second_half * sin_t, second_half * cos_t - first_half * sin_t], axis=-1)


def rms_forward(values, gain_vec):
    inv_rms = lax.rsqrt(jnp.mean(values * values, axis=-1, keepdims=True) + NORM_EPS)
    normed = values * inv_rms
    return normed * gain_vec.astype(jnp.float32), normed, inv_rms


def rms_backward(d_out, normed, inv_rms, gain_vec):
    d_normed = d_out * gain_vec.astype(jnp.float32)
    d_in = inv_rms * (d_normed - normed * jnp.mean(d_normed * normed, axis=-1, keepdims=True))
    return d_in, d_out * normed


def project(values, weight):
    return jnp.einsum('bsd,de->bse', values, weight, preferred_element_type=jnp.float32)


def project_back(grads_in, weight):
    return jnp.einsum('bse,de->bsd', grads_in, weight, preferred_element_type=jnp.float32)


def weight_grad(values, grads_in):
    return jnp.einsum('bsd,bse->de', values, grads_in, preferred_element_type=jnp.float32)


def block_front(x_in, positions, g_norm, w_query, w_key, w_value, g_query, g_key):
    n_batch, seq_len, d_model = x_in.shape
    head_shape = (n_batch, seq_len, d_model // HEAD_DIM, HEAD_DIM)
    cos_t, sin_t = rope_tables(positions)
    x_f = x_in.astype(jnp.float32)
    hid_f, x_hat, x_inv = rms_forward(x_f, g_norm)
    hidden = hid_f.astype(jnp.bfloat16)
    q_nrm, q_hat, q_inv = rms_forward(project(hidden, w_query), g_query)
    k_nrm, k_hat, k_inv = rms_forward(project(hidden, w_key), g_key)
    q_rot = rope_apply(q_nrm.reshape(head_shape), cos_t, sin_t).astype(jnp.bfloat16)
    k_rot = rope_apply(k_nrm.reshape(head_shape), cos_t, sin_t).astype(jnp.bfloat16)
    v_val = project(hidden, w_value).astype(jnp.bfloat16).reshape(head_shape)
    saved_fwd = (x_f, x_hat, x_inv, hidden, q_hat, q_inv, k_hat, k_inv, cos_t, sin_t)
    return q_rot, k_rot, v_val, saved_fwd


def block_back(saved_fwd, d_q, d_k, d_v, grad_y, g_norm, w_query, w_key, w_value, g_query, g_key):
    x_f, x_hat, x_inv, hidden, q_hat, q_inv, k_hat, k_inv, cos_t, sin_t = saved_fwd
    flat_shape = hidden.shape
    dq_rot = rope_revert(d_q.astype(jnp.float32), cos_t, sin_t).reshape(flat_shape)
    dk_rot = rope_revert(d_k.astype(jnp.float32), cos_t, sin_t).reshape(flat_shape)
    dq_raw, q_terms = rms_backward(dq_rot, q_hat, q_inv, g_query)
    dk_raw, k_terms = rms_backward(dk_rot, k_hat, k_inv, g_key)
    dq_bf = dq_raw.astype(jnp.bfloat16)
    dk_bf = dk_raw.astype(jnp.bfloat16)
    dv_bf = d_v.reshape(flat_shape)
    d_hidden = project_back(dq_bf, w_query) + project_back(dk_bf, w_key) + project_back(dv_bf, w_value)
    dx_norm, n_terms = rms_backward(d_hidden, x_hat, x_inv, g_norm)
    grad_x = (grad_y.astype(jnp.float32) + dx_norm).astype(jnp.bfloat16)
    return grad_x, (dq_bf, dk_bf, dv_bf), (n_terms, q_terms, k_terms)


def attend_forward(q_all, k_all, v_all, q_offset):
    q_len = q_all.shape[1]
    key_pos = jnp.arange(k_all.shape[1])
    blk_len = min(QUERY_BLOCK, q_len)
    qk_scale = q_all.shape[-1] ** -0.5

    def block_step(blk_idx, loop_state):
        out_buf, lse_buf = loop_state
        q_start = blk_idx * blk_len
        q_blk = lax.dynamic_slice_in_dim(q_all, q_start, blk_len, axis=1)
        scores = jnp.einsum('bqhd,bkhd->bhqk', q_blk, k_all, preferred_element_type=jnp.float32) * qk_scale
        q_pos = q_offset + q_start + jnp.arange(blk_len)
        scores = jnp.where(q_pos[:, None] >= key_pos[None, :], scores, NEG_BIG)
        row_max = jnp.max(scores, axis=-1, keepdims=True)
        exp_scores = jnp.exp(scores - row_max)
        row_sum = jnp.sum(exp_scores, axis=-1, keepdims=True)
        prob_bf = (exp_scores / row_sum).astype(jnp.bfloat16)
        out_blk = jnp.einsum('bhqk,bkhd->bqhd', prob_bf, v_all, preferred_element_type=jnp.float32)
        lse_blk = (row_max + jnp.log(row_sum))[..., 0]
        out_buf = lax.dynamic_update_slice_in_dim(out_buf, out_blk.astype(jnp.bfloat16), q_start, axis=1)
        lse_buf = lax.dynamic_update_slice_in_dim(lse_buf, lse_blk, q_start, axis=2)
        return out_buf, lse_buf

    init_state = (jnp.zeros(q_all.shape, jnp.bfloat16), jnp.zeros((q_all.shape[0], q_all.shape[2], q_len), jnp.float32))
    return lax.fori_loop(0, q_len // blk_len, block_step, init_state)


def attend_backward(q_all, k_all, v_all, lse_all, dout_all, q_offset):
    q_len = q_all.shape[1]
    key_pos = jnp.arange(k_all.shape[1])
    blk_len = min(QUERY_BLOCK, q_len)
    qk_scale = q_all.shape[-1] ** -0.5

    def block_step(blk_idx, loop_state):
        dq_buf, dk_acc, dv_acc = loop_state
        q_start = blk_idx * blk_len
        q_blk = lax.dynamic_slice_in_dim(q_all, q_start, blk_len, axis=1)
        do_blk = lax.dynamic_slice_in_dim(dout_all, q_start, blk_len, axis=1)
        lse_blk = lax.dynamic_slice_in_dim(lse_all, q_start, blk_len, axis=2)
        scores = jnp.einsum('bqhd,bkhd->bhqk', q_blk, k_all, preferred_element_type=jnp.float32) * qk_scale
        q_pos = q_offset + q_start + jnp.arange(blk_len)
        scores = jnp.where(q_pos[:, None] >= key_pos[None, :], scores, NEG_BIG)
        prob_f = jnp.exp(scores - lse_blk[..., None])
        d_prob = jnp.einsum('bqhd,bkhd->bhqk', do_blk, v_all, preferred_element_type=jnp.float32)
        row_dot = jnp.sum(prob_f * d_prob, axis=-1, keepdims=True)
        ds_bf = (prob_f * (d_prob - row_dot) * qk_scale).astype(jnp.bfloat16)
        prob_bf = prob_f.astype(jnp.bfloat16)
        dv_acc = dv_acc + jnp.einsum('bhqk,bqhd->bkhd', prob_bf, do_blk, preferred_element_type=jnp.float32)
        dk_acc = dk_acc + jnp.einsum('bhqk,bqhd->bkhd', ds_bf, q_blk, preferred_element_type=jnp.float32)
        dq_blk = jnp.einsum('bhqk,bkhd->bqhd', ds_bf, k_all, preferred_element_type=jnp.float32)
        dq_buf = lax.dynamic_update_slice_in_dim(dq_buf, dq_blk.astype(jnp.bfloat16), q_start, axis=1)
        return dq_buf, dk_acc, dv_acc

    init_state = (jnp.zeros(q_all.shape, jnp.bfloat16), jnp.zeros(k_all.shape, jnp.float32), jnp.zeros(v_all.shape, jnp.float32))
    return lax.fori_loop(0, q_len // blk_len, block_step, init_state)


def solution(mesh):
    to_heads = functools.partial(lax.all_to_all, axis_name='sp', split_axis=2, concat_axis=1, tiled=True)
    to_tokens = functools.partial(lax.all_to_all, axis_name='sp', split_axis=1, concat_axis=2, tiled=True)

    def sum_rows(partial_sum):
        return lax.psum_scatter(partial_sum, 'sp', scatter_dimension=0, tiled=True)

    def device_step(x_loc, grad_y, positions, g_norm, w_query, w_key, w_value, w_out, g_query, g_key):
        n_batch, loc_len, d_model = x_loc.shape
        q_loc, k_loc, v_loc, saved_fwd = block_front(x_loc, positions, g_norm, w_query, w_key, w_value, g_query, g_key)
        q_all = to_heads(q_loc)
        k_all = to_heads(k_loc)
        v_all = to_heads(v_loc)
        out_all, lse_all = attend_forward(q_all, k_all, v_all, 0)
        attended = to_tokens(out_all).reshape(n_batch, loc_len, d_model)
        y_out = (saved_fwd[0] + project(attended, w_out)).astype(jnp.bfloat16)
        grad_w_out = weight_grad(attended, grad_y)
        d_attn = project_back(grad_y, w_out).astype(jnp.bfloat16).reshape(q_loc.shape)
        dq_all, dk_acc, dv_acc = attend_backward(q_all, k_all, v_all, lse_all, to_heads(d_attn), 0)
        d_q = to_tokens(dq_all)
        d_k = to_tokens(dk_acc.astype(jnp.bfloat16))
        d_v = to_tokens(dv_acc.astype(jnp.bfloat16))
        grad_x, proj_grads, gain_terms = block_back(saved_fwd, d_q, d_k, d_v, grad_y, g_norm, w_query, w_key, w_value, g_query, g_key)
        hidden = saved_fwd[3]
        return (y_out, grad_x, sum_rows(jnp.sum(gain_terms[0], axis=(0, 1))), sum_rows(weight_grad(hidden, proj_grads[0])), sum_rows(weight_grad(hidden, proj_grads[1])), sum_rows(weight_grad(hidden, proj_grads[2])), sum_rows(grad_w_out), sum_rows(jnp.sum(gain_terms[1], axis=(0, 1))), sum_rows(jnp.sum(gain_terms[2], axis=(0, 1))))

    seq_spec = P('dp', 'sp', None)
    mat_rep = P(None, None)
    vec_rep = P(None)
    row_spec = P(('dp', 'sp'), None)
    vec_spec = P(('dp', 'sp'))
    return jax.shard_map(device_step, mesh=mesh, in_specs=(seq_spec, seq_spec, P('dp', 'sp'), vec_rep, mat_rep, mat_rep, mat_rep, mat_rep, vec_rep, vec_rep), out_specs=(seq_spec, seq_spec, vec_spec, row_spec, row_spec, row_spec, row_spec, vec_spec, vec_spec), check_vma=False)
```

profile of v0, /device:TPU:21, one launch (start us, length us, event | category | flops | bytes accessed | tf_op | source)
XLA Modules:
  0.0 1226.0 jit_solution(13161109988643414062)
XLA Ops:
  10.3 6.3 multiply_reduce_fusion.3
  29.9 11.3 all-to-all-start
  42.8 26.1 %all-to-all-done = bf16[1,256,16,128]{3,1,0,2:T(8,128)(2,1)} async-done(((bf16[1,256,16,128]{3,1,0,2:T(8,128)(2,1)}), bf16[1,256,16,128]{3,1,0,2:T(8,128)(2,1)}, u32[]{:S(2)}, u32[]{:S(2)}) %all-to-all-start) | async-done | bytes 1048608 | tf_op jit(solution)/shard_map/all_to_all | solution.py:158
  72.7 5.8 fusion.54
  80.0 20.3 %all-to-all-done.1 = bf16[1,256,16,128]{3,1,0,2:T(8,128)(2,1)S(1)} async-done(((bf16[1,256,16,128]{3,1,0,2:T(8,128)(2,1)}), bf16[1,256,16,128]{3,1,0,2:T(8,128)(2,1)S(1)}, u32[]{:S(2)}, u32[]{:S(2)}) %all-to-all-start.1) | async-done | bytes 1048608 | tf_op jit(solution)/shard_map/all_to_all | solution.py:159
  100.2 4.4 all-to-all-start.2
  104.7 5.7 fusion.55
  111.9 19.6 %all-to-all-done.2 = bf16[1,256,16,128]{3,1,0,2:T(8,128)(2,1)} async-done(((bf16[1,256,16,128]{3,1,0,2:T(8,128)(2,1)}), bf16[1,256,16,128]{3,1,0,2:T(8,128)(2,1)}, u32[]{:S(2)}, u32[]{:S(2)}) %all-to-all-start.2) | async-done | bytes 1048608 | tf_op jit(solution)/shard_map/all_to_all | solution.py:160
  131.5 4.7 all-to-all-start.4
  136.4 118.0 %while.34 = (s32[]{:T(128)}, bf16[1,4096,1,128]{3,1,2,0:T(8,128)(2,1)S(1)}, f32[1,1,4096]{2,1,0:T(1,128)S(1)}, bf16[1,4096,1,128]{3,1,2,0:T(8,128)(2,1)}, bf16[1...) while((s32[]{:T(128)}, ...), condition=%wide.region_6.7_spmd.clone, body=%wide.region_3.6_spmd.clone.sunk | while | flops 273170432 | bytes 8459435 | solution.py:115
  255.8 400.6 %while.35 = (s32[]{:T(128)}, bf16[1,4096,1,128]{3,1,2,0:T(8,128)(2,1)}, f32[1,4096,1,128]{1,3,2,0:T(8,128)}, f32[1,4096,1,128]{1,3,2,0:T(8,128)}, bf16[1,4096,1,...) while((s32[]{:T(128)}, ...), condition=%wide.region_9.10_spmd.clone, body=%wide.region_7.9_spmd.clone.sunk | while | flops 678969344 | bytes 48402220 | solution.py:145
  661.4 22.4 %reduce.27 = bf16[4096,128]{1,0:T(8,128)(2,1)S(1)} reduce(bf16[4096,1,1,128]{3,2,1,0:T(2,128)(2,1)S(1)} %bitcast.254, bf16[]{:T(256)} %broadcast.228), dimensions={1,2}, to_apply=%bitcast.165.reduce_sub_computation | reduce | bytes 2097154
  684.9 7.6 all-to-all-start.6
  695.7 23.4 %reduce.28 = bf16[4096,128]{1,0:T(8,128)(2,1)} reduce(bf16[4096,1,1,128]{3,2,1,0:T(2,128)(2,1)S(1)} %bitcast.256, bf16[]{:T(256)} %broadcast.228), dimensions={1,2}, to_apply=%bitcast.203.reduce_sub_computation | reduce | bytes 2097154
  721.2 7.2 all-to-all-start.5
  735.9 20.5 %all-to-all-done.5 = bf16[16,2,16384]{2,1,0:T(2,128)(2,1)} async-done(((bf16[16,2,16384]{2,1,0:T(2,128)(2,1)}), bf16[16,2,16384]{2,1,0:T(2,128)(2,1)}, u32[]{:S(2)}, u32[]{:S(2)}) %all-to-all-start.5) | async-done | bytes 1048608 | tf_op jit(solution)/shard_map/all_to_all | solution.py:167
  756.4 5.8 reshape.521
  774.2 8.2 fusion.64
  790.8 8.2 fusion.62
  801.7 5.0 copy.58
  806.7 23.4 %reduce.29 = bf16[4096,128]{1,0:T(8,128)(2,1)} reduce(bf16[4096,1,1,128]{3,2,1,0:T(2,128)(2,1)S(1)} %bitcast.257, bf16[]{:T(256)} %broadcast.228), dimensions={1,2}, to_apply=%bitcast.167.reduce_sub_computation | reduce | bytes 2097154
  831.5 37.5 %all_to_all.120 = bf16[16,2,16384]{2,1,0:T(2,128)(2,1)} all-to-all(bf16[16,2,16384]{2,1,0:T(2,128)(2,1)S(1)} %reshape.524), channel_id=1, replica_groups=mesh['dp'=4,'sp'=16] {'sp'}, dimensions={0} | all-to-all | bytes 2097152 | tf_op jit(solution)/shard_map/all_to_all | solution.py:169
  875.9 8.2 fusion.60
  887.4 23.4 %reduce.26 = bf16[4096,128]{1,0:T(8,128)(2,1)} reduce(bf16[4096,1,1,128]{3,2,1,0:T(2,128)(2,1)S(1)} %bitcast.255, bf16[]{:T(256)} %broadcast.228), dimensions={1,2}, to_apply=%bitcast.204.reduce_sub_computation | reduce | bytes 2097154
  912.1 37.3 %all_to_all.121 = bf16[16,2,16384]{2,1,0:T(2,128)(2,1)} all-to-all(bf16[16,2,16384]{2,1,0:T(2,128)(2,1)S(1)} %reshape.518), channel_id=1, replica_groups=mesh['dp'=4,'sp'=16] {'sp'}, dimensions={0} | all-to-all | bytes 2097152 | tf_op jit(solution)/shard_map/all_to_all | solution.py:162
  956.4 8.1 fusion.57
  966.4 6.2 fusion.74
  972.6 5.9 convolution_add_fusion.1
  982.7 43.4 %all-reduce.3 = (f32[2048]{0:T(1024)S(1)}, f32[2048]{0:T(1024)S(1)}, f32[2048]{0:T(1024)S(1)}) all-reduce(f32[2048]{0:T(1024)S(1)} %get-tuple-element.360, f32[2048]{0:T(1024)S(1)} %get-tuple-element.358, f32[2048]{0:T(1024)S(1)} %get-tuple-element.356), channel_id=2, replica_groups=mesh['dp'=4,'sp'=16] {'sp'}, use_global_device_ids=true, to_apply=%region_14.15.clone | all-reduce | flops 6144 | bytes 49152
  1031.1 6.7 fusion.43
  1037.8 82.6 %reduce-scatter.9.cloned.1.call-done = f32[128,2048]{1,0:T(8,128)} async-done(((f32[2048,2048]{1,0:T(8,128)}), f32[128,2048]{1,0:T(8,128)}) %reduce-scatter.9.cloned.1.call-update) | async-done | bytes 1048592 | tf_op jit(solution)/shard_map/reduce_scatter | solution.py:153
  1120.4 98.8 %reduce-scatter.11.cloned.1.call-done = f32[128,2048]{1,0:T(8,128)} async-done(((f32[2048,2048]{1,0:T(8,128)}), f32[128,2048]{1,0:T(8,128)}) %reduce-scatter.11.cloned.1.call-update) | async-done | bytes 1048592 | tf_op jit(solution)/shard_map/reduce_scatter | solution.py:153
  (734 shorter events, 613.9 us)
Async XLA Ops:
  7.9 10.4 slice-start
  10.3 8.1 slice-start.1
  29.9 38.9 %all-to-all-start = ((bf16[1,256,16,128]{3,1,0,2:T(8,128)(2,1)}), bf16[1,256,16,128]{3,1,0,2:T(8,128)(2,1)}, u32[]{:S(2)}, u32[]{:S(2)}) async-start(bf16[1,256,16,128]{3,1,0,2:T(8,128)(2,1)} %pad_maximum_fusion.2), calls=%async_computation | async-start | bytes 2097152 | tf_op jit(solution)/shard_map/all_to_all | solution.py:158
  68.9 31.3 %all-to-all-start.1 = ((bf16[1,256,16,128]{3,1,0,2:T(8,128)(2,1)}), bf16[1,256,16,128]{3,1,0,2:T(8,128)(2,1)S(1)}, u32[]{:S(2)}, u32[]{:S(2)}) async-start(bf16[1,256,16,128]{3,1,0,2:T(8,128)(2,1)} %pad_maximum_fusion.3), calls=%async_computation.1 | async-start | bytes 2097152 | tf_op jit(solution)/shard_map/all_to_all | solution.py:159
  78.7 26.0 %copy-start.11 = (bf16[1,256,2048]{2,1,0:T(8,128)(2,1)S(1)}, bf16[1,256,2048]{2,1,0:T(8,128)(2,1)}, u32[]{:S(2)}) copy-start(bf16[1,256,2048]{2,1,0:T(8,128)(2,1)} %param.15) | copy-start | bytes 3145732
  100.2 31.3 %all-to-all-start.2 = ((bf16[1,256,16,128]{3,1,0,2:T(8,128)(2,1)}), bf16[1,256,16,128]{3,1,0,2:T(8,128)(2,1)}, u32[]{:S(2)}, u32[]{:S(2)}) async-start(bf16[1,256,16,128]{3,1,0,2:T(8,128)(2,1)} %copy.50), calls=%async_computation.2 | async-start | bytes 2097152 | tf_op jit(solution)/shard_map/all_to_all | solution.py:160
  131.5 122.9 %all-to-all-start.4 = ((bf16[1,256,16,128]{3,1,0,2:T(8,128)(2,1)}), bf16[1,256,16,128]{3,1,0,2:T(8,128)(2,1)}, u32[]{:S(2)}, u32[]{:S(2)}) async-start(bf16[1,256,16,128]{3,1,0,2:T(8,128)(2,1)} %copy.53), calls=%async_computation.4 | async-start | bytes 2097152 | tf_op jit(solution)/shard_map/all_to_all | solution.py:166
  273.5 3.8 copy-start.1
  286.0 3.8 copy-start.1
  298.5 3.8 copy-start.1
  311.1 3.8 copy-start.1
  323.6 3.8 copy-start.1
  336.2 3.8 copy-start.1
  348.7 3.8 copy-start.1
  361.2 3.8 copy-start.1
  373.8 3.8 copy-start.1
  386.3 3.8 copy-start.1
  398.9 3.8 copy-start.1
  411.4 3.8 copy-start.1
  423.9 3.8 copy-start.1
  524.2 3.8 copy-start.1
  684.9 36.3 %all-to-all-start.6 = ((bf16[16,2,16384]{2,1,0:T(2,128)(2,1)}), bf16[16,2,16384]{2,1,0:T(2,128)(2,1)S(1)}, u32[]{:S(2)}, u32[]{:S(2)}) async-start(bf16[16,2,16384]{2,1,0:T(2,128)(2,1)} %reshape.522), calls=%async_computation.6 | async-start | bytes 2097152 | tf_op jit(solution)/shard_map/all_to_all | solution.py:168
  721.2 35.2 %all-to-all-start.5 = ((bf16[16,2,16384]{2,1,0:T(2,128)(2,1)}), bf16[16,2,16384]{2,1,0:T(2,128)(2,1)}, u32[]{:S(2)}, u32[]{:S(2)}) async-start(bf16[16,2,16384]{2,1,0:T(2,128)(2,1)} %reshape.520), calls=%async_computation.5 | async-start | bytes 2097152 | tf_op jit(solution)/shard_map/all_to_all | solution.py:167
  728.4 309.4 %reduce-scatter.5.cloned.1.call-start = ((), (), s32[]{:S(2)}) async-start(), calls=%async_computation.12 | async-start | bytes 17825792 | tf_op jit(solution)/shard_map/reduce_scatter | solution.py:153
  782.5 255.3 %reduce-scatter.7.cloned.1.call-start = ((), (), s32[]{:S(2)}) async-start(), calls=%async_computation.13 | async-start | bytes 17825792 | tf_op jit(solution)/shard_map/reduce_scatter | solution.py:153
  799.1 321.4 %reduce-scatter.9.cloned.1.call-start = ((), (), s32[]{:S(2)}) async-start(), calls=%async_computation.14 | async-start | bytes 17825792 | tf_op jit(solution)/shard_map/reduce_scatter | solution.py:153
  875.9 8.2 copy-start.16
  884.2 335.1 %reduce-scatter.11.cloned.1.call-start = ((), (), s32[]{:S(2)}) async-start(), calls=%async_computation.15 | async-start | bytes 17825792 | tf_op jit(solution)/shard_map/reduce_scatter | solution.py:153
  966.3 6.2 copy-start.15
  966.4 12.2 slice-start.2
  972.6 6.0 copy-start.17
  972.6 6.0 slice-start.3
  (97 other events, 163.0 us)
Sparse Core Ops, SparseCore 0:
  782.6 116.2 reduce-scatter.4
  901.9 119.0 reduce-scatter.6
  1023.9 96.4 reduce-scatter.8
  1123.2 95.9 reduce-scatter.10
where the time goes:
time: 1240 us; the launch traced here: 1230 us
  matrix products  490 us (40%)
  waiting for transfers between devices  268 us (22%)
  other arithmetic  154 us (12%)
  local copies, waits for them, and re-layouts  138 us (11%)
  blocking collectives  118 us (10%)
  starting transfers between devices  39.7 us (3%)
  between operations  15.2 us (1%)
    reduce_scatter x4, waiting for transfers between devices, sum_rows(): return lax.psum_scatter(partial_sum, 'sp', scatter_dimension=0, tiled=True)  181 us
    dot_general x32, matrix products, block_step(): jnp.einsum('bhqk,bqhd->bkhd', ds_bf, q_blk, preferred_element_type=jnp.fl...  122 us
    dot_general x64, matrix products, block_step(): jnp.einsum('bqhd,bkhd->bhqk', q_blk, k_all, preferred_element_type=jnp.fl...  97.5 us
    unnamed x10, other arithmetic  93 us
    while x192, local copies, waits for them, and re-layouts  73.3 us
    dot_general x32, matrix products, block_step(): jnp.einsum('bhqk,bkhd->bqhd', prob_bf, v_all, preferred_element_type=jnp....  58.8 us
    dot_general x32, matrix products, block_step(): jnp.einsum('bqhd,bkhd->bhqk', do_blk, v_all, preferred_element_type=jnp.f...  53.6 us
    dot_general x32, matrix products, block_step(): jnp.einsum('bhqk,bqhd->bkhd', prob_bf, do_blk, preferred_element_type=jnp...  48.2 us
  transfers between devices with their start and end apart: 10, of which 6 were waited for; matrix products, arithmetic and copies ran while one was open for 24% of the time, Pallas kernels for 0%

commit v1 on v0

v1 whole, which is shorter than its diff:
```python
import functools
import jax
import jax.numpy as jnp
from jax import lax
from jax.experimental import pallas as pl
from jax.experimental.pallas import tpu as pltpu
from jax.sharding import PartitionSpec as P

HEAD=128
NT=(((1,),(1,)),((),()))
TN=(((0,),(0,)),((),()))
LOG2E=1.4426950408889634

def dotf(a,b,dims):
    return lax.dot_general(a,b,dims,preferred_element_type=jnp.float32)

def fwd_kernel(bq,bk,q_ref,k_ref,v_ref,o_ref,of_ref,lse_ref):
    j=pl.program_id(0)
    c=HEAD**-0.5*LOG2E
    q=q_ref[...]
    def step(kb,carry,masked):
        m,l,acc=carry
        ks=pl.multiple_of(kb*bk,bk)
        s=dotf(q,k_ref[pl.ds(ks,bk),:],NT)
        if masked:
            r=lax.broadcasted_iota(jnp.int32,(bq,bk),0)+j*bq
            cc=lax.broadcasted_iota(jnp.int32,(bq,bk),1)+ks
            s=jnp.where(r>=cc,s,-1e30)
        mn=jnp.maximum(m,jnp.max(s,axis=1,keepdims=True))
        al=jnp.exp2((m-mn)*c)
        p=jnp.exp2((s-mn)*c)
        l=l*al+jnp.sum(p,axis=1,keepdims=True)
        acc=acc*al+dotf(p.astype(jnp.bfloat16),v_ref[pl.ds(ks,bk),:],(((1,),(0,)),((),())))
        return mn,l,acc
    init=(jnp.full((bq,1),-1e30,jnp.float32),jnp.zeros((bq,1),jnp.float32),jnp.zeros((bq,HEAD),jnp.float32))
    nfull=j*(bq//bk)
    carry=lax.fori_loop(0,nfull,functools.partial(step,masked=False),init)
    for t in range(bq//bk):
        carry=step(nfull+t,carry,True)
    m,l,acc=carry
    o=acc/l
    of_ref[...]=o
    o_ref[...]=o.astype(jnp.bfloat16)
    lse=m*c+jnp.log2(l)
    lse_ref[...]=jnp.broadcast_to(jnp.broadcast_to(lse,(bq,HEAD)).T[0:1,:],(8,bq))

def attn_fwd(q,k,v,bq=512,bk=512):
    n=q.shape[0]
    full=pl.BlockSpec((n,HEAD),lambda j:(0,0))
    return pl.pallas_call(functools.partial(fwd_kernel,bq,bk),grid=(n//bq,),
      in_specs=[pl.BlockSpec((bq,HEAD),lambda j:(j,0)),full,full],
      out_specs=[pl.BlockSpec((bq,HEAD),lambda j:(j,0)),pl.BlockSpec((bq,HEAD),lambda j:(j,0)),pl.BlockSpec((8,bq),lambda j:(0,j))],
      out_shape=[jax.ShapeDtypeStruct((n,HEAD),jnp.bfloat16),jax.ShapeDtypeStruct((n,HEAD),jnp.float32),jax.ShapeDtypeStruct((8,n),jnp.float32)],
      name="attn_fwd")(q,k,v)

def bwd_kernel(bq,bk,q_ref,k_ref,v_ref,do_ref,lse_ref,dl_ref,dq_ref,dk_ref,dv_ref,dqa):
    j=pl.program_id(0)
    n=q_ref.shape[0]
    c=HEAD**-0.5*LOG2E
    scale=HEAD**-0.5
    @pl.when(j==0)
    def _(): dqa[...]=jnp.zeros_like(dqa)
    k=k_ref[...]; v=v_ref[...]
    def step(qb,carry,masked):
        dk,dv=carry
        qs=pl.multiple_of(qb*bq,bq)
        q=q_ref[pl.ds(qs,bq),:]; do=do_ref[pl.ds(qs,bq),:]
        st=dotf(k,q,NT)
        p=jnp.exp2(st*c-lse_ref[0:1,pl.ds(qs,bq)])
        if masked:
            r=lax.broadcasted_iota(jnp.int32,(bk,bq),0)+j*bk
            cc=lax.broadcasted_iota(jnp.int32,(bk,bq),1)+qs
            p=jnp.where(cc>=r,p,0.0)
        dp=dotf(v,do,NT)
        ds=(p*(dp-dl_ref[0:1,pl.ds(qs,bq)])).astype(jnp.bfloat16)
        dv=dv+dotf(p.astype(jnp.bfloat16),do,(((1,),(0,)),((),())))
        dk=dk+dotf(ds,q,(((1,),(0,)),((),())))
        dqa[pl.ds(qs,bq),:]+=dotf(ds,k,TN)
        return dk,dv
    z=jnp.zeros((bk,HEAD),jnp.float32)
    carry=(z,z)
    for t in range(bk//bq):
        carry=step(j*(bk//bq)+t,carry,True)
    dk,dv=lax.fori_loop((j+1)*(bk//bq),n//bq,functools.partial(step,masked=False),carry)
    dk_ref[...]=(dk*scale).astype(jnp.bfloat16); dv_ref[...]=dv.astype(jnp.bfloat16)
    @pl.when(j==pl.num_programs(0)-1)
    def _(): dq_ref[...]=(dqa[...]*scale).astype(jnp.bfloat16)

def attn_bwd(q,k,v,do,lse,dl,bq=512,bk=512):
    n=q.shape[0]
    full=pl.BlockSpec((n,HEAD),lambda j:(0,0))
    row=pl.BlockSpec((8,n),lambda j:(0,0))
    blk=pl.BlockSpec((bk,HEAD),lambda j:(j,0))
    o=jax.ShapeDtypeStruct((n,HEAD),jnp.bfloat16)
    return pl.pallas_call(functools.partial(bwd_kernel,bq,bk),grid=(n//bk,),
      in_specs=[full,blk,blk,full,row,row],out_specs=[full,blk,blk],out_shape=[o,o,o],
      scratch_shapes=[pltpu.VMEM((n,HEAD),jnp.float32)],name="attn_bwd")(q,k,v,do,lse,dl)

NORM_EPS = 1e-5
ROPE_BASE = 10000.0
MESH = pl.DeviceIdType.MESH
f32 = jnp.float32
bf16 = jnp.bfloat16


def spread_kernel(n, gather, x_ref, o_ref, send_sem, recv_sem):
    me = lax.axis_index('sp')
    barrier = pltpu.get_barrier_semaphore()
    for d in range(1, n):
        pl.semaphore_signal(barrier, inc=1, device_id={'sp': lax.rem(me + d, n)}, device_id_type=MESH)
    pl.semaphore_wait(barrier, n - 1)
    copies = []
    for d in range(1, n):
        to = lax.rem(me + d, n)
        src = x_ref if gather else x_ref.at[to]
        cp = pltpu.make_async_remote_copy(src_ref=src, dst_ref=o_ref.at[me], send_sem=send_sem.at[d], recv_sem=recv_sem.at[d], device_id={'sp': to}, device_id_type=MESH)
        cp.start()
        copies.append(cp)
    o_ref[me] = x_ref[...] if gather else x_ref[me]
    for cp in copies:
        cp.wait()


def spread(x, n, gather, cid):
    shape = (n,) + x.shape if gather else x.shape
    return pl.pallas_call(functools.partial(spread_kernel, n, gather), out_shape=jax.ShapeDtypeStruct(shape, x.dtype),
        in_specs=[pl.BlockSpec(memory_space=pltpu.VMEM)], out_specs=pl.BlockSpec(memory_space=pltpu.VMEM),
        scratch_shapes=[pltpu.SemaphoreType.DMA((n,)), pltpu.SemaphoreType.DMA((n,))],
        compiler_params=pltpu.CompilerParams(collective_id=cid, has_side_effects=True), name='spread%d' % cid)(x)


def rope_tables(positions):
    half = HEAD // 2
    inv_freq = ROPE_BASE ** (-jnp.arange(half, dtype=f32) * (2.0 / HEAD))
    ang = positions.astype(f32)[:, None] * inv_freq
    return jnp.cos(ang), jnp.sin(ang)


def rope(x, cos, sin):
    a, b = x[..., :HEAD // 2], x[..., HEAD // 2:]
    return jnp.concatenate([a * cos - b * sin, b * cos + a * sin], -1)


def unrope(x, cos, sin):
    a, b = x[..., :HEAD // 2], x[..., HEAD // 2:]
    return jnp.concatenate([a * cos + b * sin, b * cos - a * sin], -1)


def mm(a, b, dims=(((1,), (0,)), ((), ()))):
    return lax.dot_general(a, b, dims, preferred_element_type=f32)


def solution(mesh):
    n = mesh.shape['sp']

    def device_step(x_in, grad_y, positions, g_norm, wq, wk, wv, wo, gq, gk):
        me = lax.axis_index('sp')
        x = x_in[0].astype(f32)
        gy = grad_y[0]
        t_loc, d = x.shape
        t_all = t_loc * n
        hd = d // n
        nh = n
        gn_f, gq_f, gk_f = g_norm.astype(f32), gq.astype(f32), gk.astype(f32)
        x_inv = lax.rsqrt(jnp.mean(x * x, -1, keepdims=True) + NORM_EPS)
        x_hat = x * x_inv
        hid = (x_hat * gn_f).astype(bf16)
        h_all = lax.all_gather(hid, 'sp', axis=0, tiled=True)
        gy_all = lax.all_gather(gy, 'sp', axis=0, tiled=True)
        q1l = mm(hid, wq)
        k1l = mm(hid, wk)
        q_inv = lax.rsqrt(jnp.mean(q1l * q1l, -1) + NORM_EPS)
        k_inv = lax.rsqrt(jnp.mean(k1l * k1l, -1) + NORM_EPS)
        pos = positions[0]
        st = spread(jnp.stack([q_inv, k_inv, pos.astype(f32), q_inv, q_inv, q_inv, q_inv, q_inv]), n, True, 1)
        st = jnp.swapaxes(st, 0, 1).reshape(8, t_all)
        qi, ki = st[0][:, None], st[1][:, None]
        cos, sin = rope_tables(st[2])
        sl = lambda w: lax.dynamic_slice_in_dim(w, me * hd, hd, w.ndim - 1)
        gq_h, gk_h = sl(gq_f), sl(gk_f)
        qkv = mm(h_all, jnp.concatenate([sl(wq), sl(wk), sl(wv)], 1))
        q_hat, k_hat = qkv[:, :hd] * qi, qkv[:, hd:2 * hd] * ki
        q = rope(q_hat * gq_h, cos, sin).astype(bf16)
        k = rope(k_hat * gk_h, cos, sin).astype(bf16)
        v = qkv[:, 2 * hd:].astype(bf16)
        o, o_f, lse = attn_fwd(q, k, v)
        att = lax.all_to_all(o, 'sp', split_axis=0, concat_axis=1, tiled=True)
        wo_h = lax.dynamic_slice_in_dim(wo, me * hd, hd, 0)
        do = mm(gy_all, wo_h, (((1,), (1,)), ((), ()))).astype(bf16)
        delta = jnp.broadcast_to(jnp.sum(o_f * do.astype(f32), -1)[None], (8, t_all))
        dwo = mm(o, gy_all, (((0,), (0,)), ((), ())))
        y = (x + mm(att, wo)).astype(bf16)
        dq, dk, dv = attn_bwd(q, k, v, do, lse, delta)
        to_tok = lambda z: lax.all_to_all(z, 'sp', split_axis=0, concat_axis=1, tiled=True)
        dqt, dkt, dvt = to_tok(dq), to_tok(dk), to_tok(dv)
        cl, sn = rope_tables(pos)
        cl, sn = cl[:, None], sn[:, None]
        revert = lambda z: unrope(z.astype(f32).reshape(t_loc, nh, HEAD), cl, sn).reshape(t_loc, d)
        qh_l, kh_l = q1l * q_inv[:, None], k1l * k_inv[:, None]
        dqn, dkn = revert(dqt) * gq_f, revert(dkt) * gk_f
        mq, mk = jnp.mean(dqn * qh_l, -1), jnp.mean(dkn * kh_l, -1)
        ms = spread(jnp.stack([mq, mk, mq, mq, mq, mq, mq, mq]), n, True, 2)
        ms = jnp.swapaxes(ms, 0, 1).reshape(8, t_all)
        dq_rot, dk_rot = unrope(dq.astype(f32), cos, sin), unrope(dk.astype(f32), cos, sin)
        ggq, ggk = jnp.sum(dq_rot * q_hat, 0), jnp.sum(dk_rot * k_hat, 0)
        dq_raw = (qi * (dq_rot * gq_h - q_hat * ms[0][:, None])).astype(bf16)
        dk_raw = (ki * (dk_rot * gk_h - k_hat * ms[1][:, None])).astype(bf16)
        dw = mm(h_all, jnp.concatenate([dq_raw, dk_raw, dv], 1), (((0,), (0,)), ((), ())))
        dw = lax.all_to_all(dw.reshape(n, d // n, 3 * hd), 'sp', split_axis=0, concat_axis=0, tiled=True)
        dw = jnp.transpose(dw.reshape(n, d // n, 3, hd), (2, 1, 0, 3)).reshape(3, d // n, d)
        dq_l = (q_inv[:, None] * (dqn - qh_l * mq[:, None])).astype(bf16)
        dk_l = (k_inv[:, None] * (dkn - kh_l * mk[:, None])).astype(bf16)
        nt = (((1,), (1,)), ((), ()))
        d_hid = mm(dq_l, wq, nt) + mm(dk_l, wk, nt) + mm(dvt, wv, nt)
        d_hid = d_hid.astype(bf16).astype(f32)
        dxn = d_hid * gn_f
        gx = (gy.astype(f32) + x_inv * (dxn - x_hat * jnp.mean(dxn * x_hat, -1, keepdims=True))).astype(bf16)
        gn_part = jnp.sum(d_hid * x_hat, 0).reshape(n, 1, d // n)
        gn = jnp.sum(spread(jnp.broadcast_to(gn_part, (n, 8, d // n)), n, False, 3)[:, 0], 0)
        return (y[None], gx[None], gn, dw[0], dw[1], dw[2], dwo, ggq, ggk)

    seq_spec = P('dp', 'sp', None)
    rep2, rep1 = P(None, None), P(None)
    row_spec, vec_spec = P(('dp', 'sp'), None), P(('dp', 'sp'))
    return jax.shard_map(device_step, mesh=mesh, in_specs=(seq_spec, seq_spec, P('dp', 'sp'), rep1, rep2, rep2, rep2, rep2, rep1, rep1), out_specs=(seq_spec, seq_spec, vec_spec, row_spec, row_spec, row_spec, row_spec, vec_spec, vec_spec), check_vma=False)
```

time: 1240 us -> 499 us (0.40)
  matrix products: 490 us -> 87.7 us
  waiting for transfers between devices: 268 us -> 110 us
  Pallas kernels: 0 us -> 154 us
  local copies, waits for them, and re-layouts: 138 us -> 24.7 us
  other arithmetic: 154 us -> 52 us
  blocking collectives: 118 us -> 32 us
  starting transfers between devices: 39.7 us -> 18.3 us
    dot_general x236 -> x10, matrix products: 490 us -> 87.7 us  [mm(): return lax.dot_general(a, b, dims, preferred_element_type=f32)]
    reduce_scatter x4 -> x0, waiting for transfers between devices: 181 us -> none  [sum_rows(): return lax.psum_scatter(partial_sum, 'sp', scatter_dimension=0, tiled=True)]
    pallas_call x0 -> x5, Pallas kernels: none -> 154 us  [the longest x3 89.4 us: spread(): pl.pallas_call(functools.partial(spread_kernel, n, gather), out_shape=jax...]
    all_gather x0 -> x2, waiting for transfers between devices: none -> 99.7 us  [the longest x1 62.9 us: device_step(): h_all = lax.all_gather(hid, 'sp', axis=0, tiled=True)]
    unnamed x10 -> x0, other arithmetic: 93 us -> none
    while x194 -> x0, local copies, waits for them, and re-layouts: 79.6 us -> none
    all_to_all x6 -> x4, waiting for transfers between devices: 86.5 us -> 9.68 us  [the longest x2 9.67 us: device_step(): lax.all_to_all(z, 'sp', split_axis=0, concat_axis=1, tiled=True)]
    unnamed x1 -> x0, blocking collectives: 43.4 us -> none
  transfers between devices with their start and end apart: 10 -> 6, of which waited for: 6 -> 4; matrix products, arithmetic and copies ran while one was open for 24% -> 28% of each run, Pallas kernels for 0% -> 24%
where the time goes in v1:
time: 499 us; the launch traced here: 494 us
  Pallas kernels  154 us (31%)
  waiting for transfers between devices  110 us (22%)
  matrix products  87.7 us (18%)
  other arithmetic  52 us (10%)
  blocking collectives  32 us (6%)
  local copies, waits for them, and re-layouts  24.7 us (5%)
  starting transfers between devices  18.3 us (4%)
  between operations  14.7 us (3%)
    pallas_call x3, Pallas kernels, spread(): pl.pallas_call(functools.partial(spread_kernel, n, gather), out_shape=jax...  89.4 us
    dot_general x10, matrix products, mm(): return lax.dot_general(a, b, dims, preferred_element_type=f32)  87.7 us
    all_gather x1, waiting for transfers between devices, device_step(): h_all = lax.all_gather(hid, 'sp', axis=0, tiled=True)  62.9 us
    pallas_call x1, Pallas kernels, attn_bwd(): pl.pallas_call(functools.partial(bwd_kernel, bq, bk), grid=(n // bk,), in...  37.1 us
    all_gather x1, waiting for transfers between devices, device_step(): gy_all = lax.all_gather(gy, 'sp', axis=0, tiled=True)  36.8 us
    all_to_all x1, blocking collectives, device_step(): lax.all_to_all(z, 'sp', split_axis=0, concat_axis=1, tiled=True)  32 us
    pallas_call x1, Pallas kernels, attn_fwd(): pl.pallas_call(functools.partial(fwd_kernel, bq, bk), grid=(n // bq,), in...  27.8 us
    add x2, other arithmetic, unrope(): return jnp.concatenate([a * cos + b * sin, b * cos - a * sin], -1)  13.9 us
  transfers between devices with their start and end apart: 6, of which 4 were waited for; matrix products, arithmetic and copies ran while one was open for 28% of the time, Pallas kernels for 24%

profile of v1, /device:TPU:21, one launch (start us, length us, event | category | flops | bytes accessed | tf_op | source)
XLA Modules:
  0.0 493.7 jit_solution(17811836310230028173)
XLA Ops:
  9.5 2.5 fusion.55
  13.2 7.1 %multiply_reduce_fusion.5 = (f32[256]{0:T(256)S(1)}, f32[256,2048]{1,0:T(8,128)}) fusion(bf16[256,2048]{1,0:T(8,128)(2,1)S(1)} %copy-done.19, bf16[2048,2048]{1,0:T(8,128)(2,1)} %param.15), kind=kOutput, calls=%fused_computation.87 | convolution fusion | flops 2148531968 | bytes 11535360 | tf_op jit(solution)/shard_map/dot_general | solution.py:150
  20.3 7.1 %multiply_reduce_fusion.6 = (f32[256]{0:T(256)S(1)}, f32[256,2048]{1,0:T(8,128)}) fusion(bf16[256,2048]{1,0:T(8,128)(2,1)S(1)} %copy-done.19, bf16[2048,2048]{1,0:T(8,128)(2,1)} %param.14), kind=kOutput, calls=%fused_computation.88 | convolution fusion | flops 2148531968 | bytes 11535360 | tf_op jit(solution)/shard_map/dot_general | solution.py:150
  28.1 17.6 %spread1.1 = f32[16,8,256]{2,1,0:T(8,128)} custom-call(f32[8,256]{1,0:T(8,128)} %stack.4.x_ref), custom_call_target="tpu_custom_call" | custom-call | tf_op jit(solution)/shard_map/spread1/pallas_call | solution.py:126
  49.2 62.9 %all-gather.4.cloned.1.call-done = bf16[4096,2048]{1,0:T(8,128)(2,1)} async-done(((bf16[256,2048]{1,0:T(8,128)(2,1)}), bf16[4096,2048]{1,0:T(8,128)(2,1)}) %all-gather.4.cloned.1.call-update) | async-done | bytes 16777232 | tf_op jit(solution)/shard_map/all_gather | solution.py:168
  112.1 12.3 %fusion.61 = f32[4096,384]{1,0:T(8,128)S(1)} fusion(bf16[4096,2048]{1,0:T(8,128)(2,1)} %all-gather.4.cloned.1.call-done, bf16[2048,128]{1,0:T(8,128)(2,1)S(1)} %get-tuple-element.73, bf16[2048,128]{1,0:T(8,128)(2,1)S(1)} %get-tuple-element.74, bf16[2048,128]{1,0:T(8,128)(2,1)S(1)} %constant_dynamic-slice_fusion.2), kind=kOutput, calls=%fused_computation.91 | convolution fusion | flops 6447169536 | bytes 24641536 | tf_op jit(solution)/shard_map/dot_general | solution.py:150
  127.3 9.3 %fusion.48 = (bf16[4096,64]{1,0:T(8,128)(2,1)S(1)}, bf16[4096,64]{1,0:T(8,128)(2,1)S(1)}, bf16[4096,64]{1,0:T(8,128)(2,1)S(1)}, bf16[4096,64]{1,0:T(8,128)(2,1)S(1)}) fusion(f32[4096,128]{1,0:T(8,128)S(1)} %get-tuple-element.36, f32[64]{0:T(128)S(1)} %multiply_power_fusion, f32[4096]{0:T(1024)S(1)} %bitcast.113, f32[4096,128]{1,0:T(8,128)S(1)} %get-tuple-element.37), kind=kLoop, calls=%fused_computation.52 | loop fusion | flops 4456448 | bytes 6308096 | tf_op jit(solution)/shard_map/convert.4
  139.7 27.8 %attn_fwd.1 = (bf16[4096,128]{1,0:T(8,128)(2,1)}, f32[4096,128]{1,0:T(8,128)}, f32[8,4096]{1,0:T(8,128)}) custom-call(bf16[4096,128]{1,0:T(8,128)(2,1)} %pad_maximum_fusion.2.q_ref, bf16[4096,128]{1,0:T(8,128)(2,1)} %pad_maximum_fusion.3.k_ref, bf16[4096,128]{1,0:T(8,128)(2,1)} %slice.168.v_ref), custom_call_target="tpu_custom_call" | custom-call | tf_op jit(solution)/shard_map/attn_fwd/pallas_call | solution.py:50
  167.5 36.8 %all-gather.6.cloned.1.call-done = bf16[1,4096,2048]{2,1,0:T(8,128)(2,1)} async-done(((bf16[1,256,2048]{2,1,0:T(8,128)(2,1)}), bf16[1,4096,2048]{2,1,0:T(8,128)(2,1)}) %all-gather.6.cloned.1.call-update) | async-done | bytes 16777232 | tf_op jit(solution)/shard_map/all_gather | solution.py:169
  204.3 12.0 %multiply_reduce_fusion.4 = (f32[4096]{0:T(1024)S(1)}, bf16[4096,128]{1,0:T(8,128)(2,1)}) fusion(f32[4096,128]{1,0:T(8,128)} %get-tuple-element.17, bf16[1,4096,2048]{2,1,0:T(8,128)(2,1)} %all-gather.6.cloned.1.call-done, bf16[2048,2048]{1,0:T(8,128)(2,1)} %param.17, s32[]{:T(128)S(6)} %select_n.2), kind=kOutput, calls=%fused_computation.86 | convolution fusion | flops 2149576704 | bytes 20463620 | tf_op jit(solution)/shard_map/dot_general | solution.py:150
  217.0 37.1 %attn_bwd.1 = (bf16[4096,128]{1,0:T(8,128)(2,1)}, bf16[4096,128]{1,0:T(8,128)(2,1)}, bf16[4096,128]{1,0:T(8,128)(2,1)}) custom-call(bf16[4096,128]{1,0:T(8,128)(2,1)} %pad_maximum_fusion.2.q_ref, bf16[4096,128]{1,0:T(8,128)(2,1)} %pad_maximum_fusion.3.k_ref, bf16[4096,128]{1,0:T(8,128)(2,1)} %slice.168.v_ref, bf16[4096,128]{1,0:T(8,128)(2,1)} %get-tuple-element.71.do_ref, ...), custom_call_target="tpu_custom_call" | custom-call | tf_op jit(solution)/shard_map/attn_bwd/pallas_call | solution.py:95
  254.0 32.0 %all_to_all.69 = bf16[16,256,128]{2,1,0:T(8,128)(2,1)} all-to-all(bf16[16,256,128]{2,1,0:T(8,128)(2,1)} %bitcast.101), channel_id=1, replica_groups=mesh['dp'=4,'sp'=16] {'sp'}, dimensions={0} | all-to-all | bytes 2097152 | tf_op jit(solution)/shard_map/all_to_all | solution.py:194
  286.0 4.5 all-to-all-start.2
  291.3 2.8 convert_element_type.112
  295.4 2.3 copy.33
  297.6 12.0 %fusion.51 = (f32[4096,64]{1,0:T(8,128)}, f32[4096,64]{1,0:T(8,128)}, f32[4096,64]{1,0:T(8,128)}, f32[4096,64]{1,0:T(8,128)}) fusion(f32[4096,128]{1,0:T(8,128)S(1)} %convert_element_type.110, f32[64]{0:T(128)S(1)} %multiply_power_fusion, f32[4096]{0:T(1024)S(1)} %bitcast.114, f32[4096,128]{1,0:T(8,128)} %convert_element_type.112), kind=kLoop, calls=%fused_computation.55 | loop fusion | flops 3407872 | bytes 8405248 | tf_op jit(solution)/shard_map/add | solution.py:146
  311.2 7.4 %all-to-all-done.2 = bf16[16,256,128]{2,1,0:T(8,128)(2,1)} async-done(((bf16[16,256,128]{2,1,0:T(8,128)(2,1)}), bf16[16,256,128]{2,1,0:T(8,128)(2,1)}, u32[]{:S(2)}, u32[]{:S(2)}) %all-to-all-start.2) | async-done | bytes 1048608 | tf_op jit(solution)/shard_map/all_to_all | solution.py:194
  318.6 3.8 all-to-all-start
  330.9 23.7 %spread2.1 = f32[16,8,256]{2,1,0:T(8,128)} custom-call(f32[8,256]{1,0:T(8,128)} %stack.5.x_ref), custom_call_target="tpu_custom_call" | custom-call | tf_op jit(solution)/shard_map/spread2/pallas_call | solution.py:126
  355.7 4.5 all-to-all-start.3
  360.2 8.1 %multiply_reduce_fusion = (f32[128]{0:T(128)}, f32[128]{0:T(128)}, bf16[4096,128]{1,0:T(8,128)(2,1)S(1)}, bf16[4096,128]{1,0:T(8,128)(2,1)S(1)}) fusion(f32[4096,384]{1,0:T(8,128)} %copy-done.8, f32[4096]{0:T(1024)S(1)} %bitcast.110, f32[4096,64]{1,0:T(8,128)} %get-tuple-element.60, f32[4096,64]{1,0:T(8,128)} %get-tuple-element.61, f32[4096]{0:T(1024)S(1)} %bitcast.112, ...), kind=kLoop, calls=%fused_computation.74 | loop fusion | flops 9436928 | bytes 10553344 | tf_op jit(solution)/shard_map/reduce_sum | solution.py:205
  368.3 13.7 %fusion.10 = f32[2048,384]{1,0:T(8,128)} fusion(bf16[4096,2048]{1,0:T(8,128)(2,1)} %all-gather.4.cloned.1.call-done, bf16[4096,128]{1,0:T(8,128)(2,1)S(1)} %copy-done.21, bf16[4096,128]{1,0:T(8,128)(2,1)S(1)} %get-tuple-element.35, bf16[4096,128]{1,0:T(8,128)(2,1)S(1)} %get-tuple-element.34), kind=kOutput, calls=%fused_computation.6 | convolution fusion | flops 6451888128 | bytes 23068672 | tf_op jit(solution)/shard_map/dot_general | solution.py:150
  382.0 3.5 copy.34
  385.5 2.3 all-to-all-done.3
  387.8 5.3 %all-to-all-start.4 = ((f32[16,128,384]{1,2,0:T(8,128)}), f32[16,128,384]{1,2,0:T(8,128)}, u32[]{:S(2)}, u32[]{:S(2)}) async-start(f32[16,128,384]{1,2,0:T(8,128)} %copy.34), calls=%async_computation.4 | async-start | bytes 6291456 | tf_op jit(solution)/shard_map/all_to_all | solution.py:209
  393.2 9.3 %fusion = f32[128,2048]{1,0:T(8,128)} fusion(bf16[4096,128]{1,0:T(8,128)(2,1)S(1)} %copy-done.16, bf16[1,4096,2048]{2,1,0:T(8,128)(2,1)} %all-gather.6.cloned.1.call-done), kind=kOutput, calls=%fused_computation | convolution fusion | flops 2147483648 | bytes 18874368 | tf_op jit(solution)/shard_map/dot_general | solution.py:150
  402.5 6.4 %fusion.67 = f32[256,2048]{1,0:T(8,128)S(1)} fusion(bf16[2048,2048]{1,0:T(8,128)(2,1)} %param.14, f32[256,2048]{1,0:T(8,128)S(1)} %copy-done.12, f32[256]{0:T(256)S(1)} %broadcast_multiply_fusion.2, f32[2048]{0:T(1024)S(1)} %convert_element_type.93, f32[256]{0:T(256)S(1)} %add_rsqrt_fusion.1, f32[256,16,64]{2,0,1:T(8,128)S(1)} %copy-done.4, ...), kind=kOutput, calls=%fused_computation.97 | convolution fusion | flops 2151153664 | bytes 14690304 | tf_op jit(solution)/shard_map/dot_general | solution.py:150
  408.9 6.3 %convolution_add_fusion.1 = f32[256,2048]{1,0:T(8,128)S(1)} fusion(f32[256,2048]{1,0:T(8,128)S(1)} %fusion.67, bf16[2048,2048]{1,0:T(8,128)(2,1)} %param.15, f32[256,2048]{1,0:T(8,128)S(1)} %copy-done.10, f32[256]{0:T(256)S(1)} %broadcast_multiply_fusion.1, f32[2048]{0:T(1024)S(1)} %convert_element_type.94, f32[256]{0:T(256)S(1)} %add_rsqrt_fusion, ...), kind=kOutput, calls=%fused_computation.39 | convolution fusion | flops 2151677952 | bytes 16787456 | tf_op jit(solution)/shard_map/dot_general | solution.py:150
  415.2 6.7 %fusion.57 = (f32[2048]{0:T(1024)S(1)}, f32[256]{0:T(256)S(1)}, bf16[256,2048]{1,0:T(8,128)(2,1)S(1)}) fusion(bf16[1,256,2048]{2,1,0:T(8,128)(2,1)S(1)} %copy-done.7, f32[256]{0:T(256)S(1)} %add_rsqrt_fusion.2, f32[2048]{0:T(1024)S(1)} %convert_element_type.90, f32[256,2048]{1,0:T(8,128)S(1)} %convolution_add_fusion.1, bf16[256,2048]{0,1:T(8,128)(2,1)} %bitcast.22, ...), kind=kOutput, calls=%fused_computation.61 | convolution fusion | flops 2152724224 | bytes 13649920 | tf_op jit(solution)/shard_map/dot_general | solution.py:150
  422.6 48.0 %spread3.1 = f32[16,8,128]{2,1,0:T(8,128)} custom-call(f32[16,8,128]{2,1,0:T(8,128)} %broadcast_in_dim.14.x_ref), custom_call_target="tpu_custom_call" | custom-call | tf_op jit(solution)/shard_map/spread3/pallas_call | solution.py:126
  473.7 6.9 %fusion.39 = bf16[1,256,2048]{2,1,0:T(8,128)(2,1)} fusion(bf16[256,2048]{0,1:T(8,128)(2,1)S(1)} %bitcast.99, bf16[2048,2048]{1,0:T(8,128)(2,1)} %param.17, bf16[1,256,2048]{2,1,0:T(8,128)(2,1)S(1)} %copy-done.7), kind=kOutput, calls=%fused_computation.43 | convolution fusion | flops 2149056512 | bytes 11534336 | tf_op jit(solution)/shard_map/dot_general | solution.py:150
  480.7 2.1 fusion.79
  (95 shorter events, 35.1 us)
Async XLA Ops:
  7.2 104.9 %all-gather.4.cloned.1.call-start = ((), (), s32[]{:S(2)}) async-start(), calls=%async_computation.5 | async-start | bytes 17825792 | tf_op jit(solution)/shard_map/all_gather | solution.py:168
  9.5 3.4 copy-start.22
  9.5 3.5 copy-start.23
  9.5 3.6 copy-start.24
  12.0 1.2 copy-start.19
  12.1 192.2 %all-gather.6.cloned.1.call-start = ((), (), s32[]{:S(2)}) async-start(), calls=%async_computation.6 | async-start | bytes 17825792 | tf_op jit(solution)/shard_map/all_gather | solution.py:169
  124.3 3.0 copy-start.8
  254.0 37.1 %copy-start.18 = (bf16[4096,128]{1,0:T(8,128)(2,1)S(1)}, bf16[4096,128]{1,0:T(8,128)(2,1)}, u32[]{:S(2)}) copy-start(bf16[4096,128]{1,0:T(8,128)(2,1)} %get-tuple-element.18) | copy-start | bytes 3145732
  286.0 32.5 %all-to-all-start.2 = ((bf16[16,256,128]{2,1,0:T(8,128)(2,1)}), bf16[16,256,128]{2,1,0:T(8,128)(2,1)}, u32[]{:S(2)}, u32[]{:S(2)}) async-start(bf16[16,256,128]{2,1,0:T(8,128)(2,1)} %bitcast.18), calls=%async_computation.2 | async-start | bytes 2097152 | tf_op jit(solution)/shard_map/all_to_all | solution.py:194
  291.3 2.8 copy-start.15
  297.6 12.0 %copy-start.17 = (bf16[16,256,128]{2,1,0:T(8,128)(2,1)S(1)}, bf16[16,256,128]{2,1,0:T(8,128)(2,1)}, u32[]{:S(2)}) copy-start(bf16[16,256,128]{2,1,0:T(8,128)(2,1)} %all_to_all.69) | copy-start | bytes 3145732
  318.6 37.1 %all-to-all-start = ((bf16[16,256,128]{1,2,0:T(8,128)(2,1)}), bf16[16,256,128]{1,2,0:T(8,128)(2,1)S(1)}, u32[]{:S(2)}, u32[]{:S(2)}) async-start(bf16[16,256,128]{1,2,0:T(8,128)(2,1)} %copy.29), calls=%async_computation | async-start | bytes 2097152 | tf_op jit(solution)/shard_map/all_to_all | solution.py:187
  322.4 1.9 copy-start.2
  324.3 1.9 copy-start.9
  326.2 1.3 copy-start
  326.2 2.1 copy-start.3
  326.2 2.8 copy-start.5
  326.2 3.2 copy-start.11
  355.7 12.6 %copy-start.13 = (bf16[16,256,128]{1,2,0:T(8,128)(2,1)}, bf16[16,256,128]{1,2,0:T(8,128)(2,1)S(1)}, u32[]{:S(2)}) copy-start(bf16[16,256,128]{1,2,0:T(8,128)(2,1)S(1)} %all-to-all-done) | copy-start | bytes 3145732
  355.7 32.1 %all-to-all-start.3 = ((bf16[16,256,128]{1,2,0:T(8,128)(2,1)}), bf16[16,256,128]{1,2,0:T(8,128)(2,1)}, u32[]{:S(2)}, u32[]{:S(2)}) async-start(bf16[16,256,128]{1,2,0:T(8,128)(2,1)} %copy.33), calls=%async_computation.3 | async-start | bytes 2097152 | tf_op jit(solution)/shard_map/all_to_all | solution.py:194
  360.2 8.1 %copy-start.21 = (bf16[4096,128]{1,0:T(8,128)(2,1)S(1)}, bf16[4096,128]{1,0:T(8,128)(2,1)}, u32[]{:S(2)}) copy-start(bf16[4096,128]{1,0:T(8,128)(2,1)} %get-tuple-element.20) | copy-start | bytes 3145732
  385.5 7.7 %copy-start.16 = (bf16[4096,128]{1,0:T(8,128)(2,1)S(1)}, bf16[4096,128]{1,0:T(8,128)(2,1)}, u32[]{:S(2)}) copy-start(bf16[4096,128]{1,0:T(8,128)(2,1)} %get-tuple-element.15) | copy-start | bytes 3145732
  387.8 92.9 %all-to-all-start.4 = ((f32[16,128,384]{1,2,0:T(8,128)}), f32[16,128,384]{1,2,0:T(8,128)}, u32[]{:S(2)}, u32[]{:S(2)}) async-start(f32[16,128,384]{1,2,0:T(8,128)} %copy.34), calls=%async_computation.4 | async-start | bytes 6291456 | tf_op jit(solution)/shard_map/all_to_all | solution.py:209
  393.2 9.3 %copy-start.4 = (f32[256,16,64]{2,0,1:T(8,128)S(1)}, f32[256,16,64]{2,0,1:T(8,128)}, u32[]{:S(2)}) copy-start(f32[256,16,64]{2,0,1:T(8,128)} %copy-done.3) | copy-start | bytes 3145732
  393.2 9.3 %copy-start.6 = (f32[256,16,64]{2,0,1:T(8,128)S(1)}, f32[256,16,64]{2,0,1:T(8,128)}, u32[]{:S(2)}) copy-start(f32[256,16,64]{2,0,1:T(8,128)} %copy-done.5) | copy-start | bytes 3145732
  393.2 9.3 %copy-start.12 = (f32[256,2048]{1,0:T(8,128)S(1)}, f32[256,2048]{1,0:T(8,128)}, u32[]{:S(2)}) copy-start(f32[256,2048]{1,0:T(8,128)} %get-tuple-element.67) | copy-start | bytes 6291460
  402.4 6.4 %copy-start.1 = (f32[256,16,64]{2,0,1:T(8,128)S(1)}, f32[256,16,64]{2,0,1:T(8,128)}, u32[]{:S(2)}) copy-start(f32[256,16,64]{2,0,1:T(8,128)} %copy-done) | copy-start | bytes 3145732
  402.5 6.4 %copy-start.10 = (f32[256,2048]{1,0:T(8,128)S(1)}, f32[256,2048]{1,0:T(8,128)}, u32[]{:S(2)}) copy-start(f32[256,2048]{1,0:T(8,128)} %get-tuple-element.69) | copy-start | bytes 6291460
  408.9 6.3 %copy-start.7 = (bf16[1,256,2048]{2,1,0:T(8,128)(2,1)S(1)}, bf16[1,256,2048]{2,1,0:T(8,128)(2,1)}, u32[]{:S(2)}) copy-start(bf16[1,256,2048]{2,1,0:T(8,128)(2,1)} %param.10) | copy-start | bytes 3145732
  415.2 56.8 %copy-start.20 = (bf16[1,256,2048]{2,1,0:T(8,128)(2,1)S(1)}, bf16[1,256,2048]{2,1,0:T(8,128)(2,1)}, u32[]{:S(2)}) copy-start(bf16[1,256,2048]{2,1,0:T(8,128)(2,1)} %param.11) | copy-start | bytes 3145732
  472.0 1.7 copy-start.14
Sparse Core Ops, SparseCore 0:
  12.2 99.8 all-gather.3
  113.7 90.5 all-gather.5

commit v2 on v1

v2 whole, which is shorter than its diff:
```python
import contextlib
import functools
import jax
import jax.numpy as jnp
from jax import lax
from jax.experimental import pallas as pl
from jax.experimental.pallas import tpu as pltpu
from jax.sharding import PartitionSpec as P

HEAD=128
NORM_EPS = 1e-5
ROPE_BASE = 10000.0

NT=(((1,),(1,)),((),()))
TN=(((0,),(0,)),((),()))
LOG2E=1.4426950408889634

def dotf(a,b,dims):
    return lax.dot_general(a,b,dims,preferred_element_type=jnp.float32)

def fwd_kernel(bq,bk,q_ref,k_ref,v_ref,o_ref,of_ref,lse_ref):
    j=pl.program_id(0)
    c=HEAD**-0.5*LOG2E
    q=q_ref[...]
    def step(kb,carry,masked):
        m,l,acc=carry
        ks=pl.multiple_of(kb*bk,bk)
        s=dotf(q,k_ref[pl.ds(ks,bk),:],NT)
        if masked:
            r=lax.broadcasted_iota(jnp.int32,(bq,bk),0)+j*bq
            cc=lax.broadcasted_iota(jnp.int32,(bq,bk),1)+ks
            s=jnp.where(r>=cc,s,-1e30)
        mn=jnp.maximum(m,jnp.max(s,axis=1,keepdims=True))
        al=jnp.exp2((m-mn)*c)
        p=jnp.exp2((s-mn)*c)
        l=l*al+jnp.sum(p,axis=1,keepdims=True)
        acc=acc*al+dotf(p.astype(jnp.bfloat16),v_ref[pl.ds(ks,bk),:],(((1,),(0,)),((),())))
        return mn,l,acc
    init=(jnp.full((bq,1),-1e30,jnp.float32),jnp.zeros((bq,1),jnp.float32),jnp.zeros((bq,HEAD),jnp.float32))
    nfull=j*(bq//bk)
    carry=lax.fori_loop(0,nfull,functools.partial(step,masked=False),init)
    for t in range(bq//bk):
        carry=step(nfull+t,carry,True)
    m,l,acc=carry
    o=acc/l
    of_ref[...]=o
    o_ref[...]=o.astype(jnp.bfloat16)
    lse=m*c+jnp.log2(l)
    lse_ref[...]=jnp.broadcast_to(jnp.broadcast_to(lse,(bq,HEAD)).T[0:1,:],(8,bq))

def attn_fwd(q,k,v,bq=512,bk=512):
    n=q.shape[0]
    full=pl.BlockSpec((n,HEAD),lambda j:(0,0))
    return pl.pallas_call(functools.partial(fwd_kernel,bq,bk),grid=(n//bq,),
      in_specs=[pl.BlockSpec((bq,HEAD),lambda j:(j,0)),full,full],
      out_specs=[pl.BlockSpec((bq,HEAD),lambda j:(j,0)),pl.BlockSpec((bq,HEAD),lambda j:(j,0)),pl.BlockSpec((8,bq),lambda j:(0,j))],
      out_shape=[jax.ShapeDtypeStruct((n,HEAD),jnp.bfloat16),jax.ShapeDtypeStruct((n,HEAD),jnp.float32),jax.ShapeDtypeStruct((8,n),jnp.float32)],
      name="attn_fwd")(q,k,v)

f32 = jnp.float32
bf16 = jnp.bfloat16
MESH = pl.DeviceIdType.MESH
PROF = 0
scope = jax.named_scope if PROF else (lambda name: contextlib.nullcontext())
NN = (((1,), (0,)), ((), ()))


def greet(n, me):
    barrier = pltpu.get_barrier_semaphore()
    for d in range(1, n):
        pl.semaphore_signal(barrier, inc=1, device_id={'sp': lax.rem(me + d, n)}, device_id_type=MESH)
    pl.semaphore_wait(barrier, n - 1)


def remote(src, dst, ss, rs, to):
    return pltpu.make_async_remote_copy(src_ref=src, dst_ref=dst, send_sem=ss, recv_sem=rs, device_id={'sp': to}, device_id_type=MESH)


def back_kernel(n, q_ref, k_ref, v_ref, do_ref, o_ref, lse_ref, dl_ref, x_ref, wo_ref, gy_ref, h_ref,
                dq_ref, dkv_ref, tq_ref, tkv_ref, y_ref, dwo_ref, dwv_ref,
                dqa, att, dt, tile, wtile, s_o, r_o, s_kv, r_kv, s_q, r_q, s_t, s_w):
    me = lax.axis_index('sp')
    t_all = q_ref.shape[0]
    t_loc = t_all // n
    d = x_ref.shape[1]
    blk = 2 * t_loc
    nb = t_all // blk
    z = me // 2
    c = HEAD ** -0.5 * LOG2E
    scale = HEAD ** -0.5
    cw = tile.shape[2]
    nt = d // cw
    cols = pl.ds(pl.multiple_of(me * HEAD, HEAD), HEAD)

    def tile_copy(t):
        cs = pl.ds(pl.multiple_of(lax.rem(t, nt) * cw, cw), cw)
        return cs

    def gy_copy(t):
        return pltpu.make_async_copy(gy_ref.at[:, tile_copy(t)], tile.at[lax.rem(t, 2)], s_t.at[lax.rem(t, 2)])

    def h_copy(t):
        return pltpu.make_async_copy(h_ref.at[:, tile_copy(t)], tile.at[lax.rem(t, 2)], s_t.at[lax.rem(t, 2)])

    def w_copy(t):
        return pltpu.make_async_copy(wo_ref.at[:, tile_copy(t)], wtile.at[lax.rem(t, 2)], s_w.at[lax.rem(t, 2)])

    gy_copy(0).start()
    w_copy(0).start()
    with scope('greet'):
        greet(n, me)

    def rows(i):
        return pl.ds(pl.multiple_of(i * t_loc, t_loc), t_loc)

    def o_send(e):
        to = lax.rem(me + e, n)
        return remote(o_ref.at[rows(to), :], att.at[:, cols], s_o.at[e], r_o.at[e], to)

    def q_send(e):
        to = lax.rem(me + e, n)
        return remote(dq_ref.at[rows(to), :], tq_ref.at[:, cols], s_q.at[e], r_q.at[e], to)

    def kv_send(to):
        e = lax.rem(to + n - me, n)
        return remote(dkv_ref.at[to], tkv_ref.at[:, :, cols], s_kv.at[e], r_kv.at[e], to)

    for e in range(1, n):
        o_send(e).start()
    att[:, cols] = o_ref[rows(me), :]
    dqa[...] = jnp.zeros_like(dqa)

    def step(s, _):
        kb = lax.rem(z + 1 + s, nb)
        ks = pl.ds(pl.multiple_of(kb * blk, blk), blk)
        k = k_ref[ks, :]
        v = v_ref[ks, :]

        def unit(qb, carry, masked):
            dk, dv = carry
            qs = pl.ds(pl.multiple_of(qb * blk, blk), blk)
            q = q_ref[qs, :]
            do = do_ref[qs, :]
            st = dotf(k, q, NT)
            p = jnp.exp2(st * c - lse_ref[0:1, qs])
            if masked:
                r = lax.broadcasted_iota(jnp.int32, (blk, blk), 0)
                cc = lax.broadcasted_iota(jnp.int32, (blk, blk), 1)
                p = jnp.where(cc >= r, p, 0.0)
            dp = dotf(v, do, NT)
            ds = (p * (dp - dl_ref[0:1, qs])).astype(bf16)
            dv = dv + dotf(p.astype(bf16), do, NN)
            dk = dk + dotf(ds, q, NN)
            dqa[qs, :] += dotf(ds, k, TN)
            return dk, dv

        zero = jnp.zeros((blk, HEAD), f32)
        carry = unit(kb, (zero, zero), True)
        dk, dv = lax.fori_loop(kb + 1, nb, functools.partial(unit, masked=False), carry)
        dk = (dk * scale).astype(bf16)
        dv = dv.astype(bf16)
        for u in range(2):
            to = 2 * kb + u
            dkv_ref[to, 0] = dk[u * t_loc:(u + 1) * t_loc]
            dkv_ref[to, 1] = dv[u * t_loc:(u + 1) * t_loc]

        @pl.when(kb != z)
        def _():
            for u in range(2):
                kv_send(2 * kb + u).start()

        @pl.when(kb == z)
        def _():
            kv_send(me + 1 - 2 * lax.rem(me, 2)).start()
        return 0

    with scope('bwd'):
        lax.fori_loop(0, nb, step, 0)
    with scope('dqsend'):
        dq_ref[...] = (dqa[...] * scale).astype(bf16)
        for e in range(1, n):
            q_send(e).start()
        tq_ref[:, cols] = dq_ref[rows(me), :]
        tkv_ref[:, :, cols] = dkv_ref[me]

    def flip(i, _):
        dt[:, rows(i)] = o_ref[rows(i), :].T
        return 0

    with scope('flip'):
        lax.fori_loop(0, n, flip, 0)

    def dwo_step(t, _):
        gy_copy(t).wait()

        @pl.when(t + 1 < nt)
        def _():
            gy_copy(t + 1).start()

        @pl.when(t + 1 == nt)
        def _():
            h_copy(t + 1).start()
        dwo_ref[:, tile_copy(t)] = dotf(dt[...], tile[lax.rem(t, 2)], NN)
        return 0

    with scope('dwo'):
        lax.fori_loop(0, nt, dwo_step, 0)

    def flip2(i, _):
        dt[:, rows(i)] = dkv_ref[i, 1].T
        return 0

    with scope('flip2'):
        lax.fori_loop(0, n, flip2, 0)

    def dwv_step(t, _):
        h_copy(t).wait()

        @pl.when(t + 1 < 2 * nt)
        def _():
            h_copy(t + 1).start()
        r = dotf(dt[...], tile[lax.rem(t, 2)], NN)
        for u in range(2):
            dwv_ref[2 * (t - nt) + u] = r[:, u * HEAD:(u + 1) * HEAD].T
        return 0

    with scope('dwv'):
        lax.fori_loop(nt, 2 * nt, dwv_step, 0)
    with scope('waito'):
        for e in range(1, n):
            o_send(e).wait()

    def y_step(t, _):
        w_copy(t).wait()

        @pl.when(t + 1 < nt)
        def _():
            w_copy(t + 1).start()
        y_ref[:, tile_copy(t)] = (x_ref[:, tile_copy(t)].astype(f32) + dotf(att[...], wtile[lax.rem(t, 2)], NN)).astype(bf16)
        return 0

    with scope('y'):
        lax.fori_loop(0, nt, y_step, 0)
    for e in range(1, n):
        kv_send(lax.rem(me + e, n)).wait()
        q_send(e).wait()


def back(n, q, k, v, do, o, lse, dl, x, wo, gy, h, cid):
    t_all, d = h.shape
    t_loc = t_all // n
    vm = pl.BlockSpec(memory_space=pltpu.VMEM)
    hb = pl.BlockSpec(memory_space=pl.ANY)
    S = jax.ShapeDtypeStruct
    sem = pltpu.SemaphoreType.DMA
    return pl.pallas_call(functools.partial(back_kernel, n),
        in_specs=[vm] * 8 + [hb] * 3, out_specs=[vm] * 7,
        out_shape=[S((t_all, HEAD), bf16), S((n, 2, t_loc, HEAD), bf16), S((t_loc, d), bf16), S((2, t_loc, d), bf16), S((t_loc, d), bf16), S((HEAD, d), f32), S((n, d // n, HEAD), f32)],
        scratch_shapes=[pltpu.VMEM((t_all, HEAD), f32), pltpu.VMEM((t_loc, d), bf16), pltpu.VMEM((HEAD, t_all), bf16), pltpu.VMEM((2, t_all, 2 * HEAD), bf16), pltpu.VMEM((2, d, 2 * HEAD), bf16)]
        + [sem((n,))] * 6 + [sem((2,))] * 2,
        compiler_params=pltpu.CompilerParams(collective_id=cid, has_side_effects=True, vmem_limit_bytes=60 * 1024 * 1024), name='back')(q, k, v, do, o, lse, dl, x, wo, gy, h)


def last_kernel(n, dq_ref, dkv_ref, tq_ref, tkv_ref, bv_ref, qt_ref, kt_ref, iv_ref, cs_ref, gc_ref,
                ql_ref, kl_ref, il_ref, cl_ref, sl_ref, g_ref, x_ref, gy_ref, h_ref, wq_ref, wk_ref, wv_ref,
                gx_ref, dwq_ref, dwk_ref, dwv_ref, gg_ref, gn_ref,
                raw, stage, dloc, dh, mine, mall, gpart, gall, tile, wtile,
                s_v, r_v, s_a, r_a, s_b, r_b, s_m, r_m, s_g, r_g, s_t, s_w):
    me = lax.axis_index('sp')
    t_all = h_ref.shape[0]
    t_loc, d = x_ref.shape
    z = me // 2
    cw = tile.shape[2]
    nt = d // cw
    wr = wtile.shape[2]
    nw = d // wr
    half = HEAD // 2
    cols = pl.ds(pl.multiple_of(me * HEAD, HEAD), HEAD)

    def h_copy(t):
        cs = pl.ds(pl.multiple_of(lax.rem(z + 1 + t, nt) * cw, cw), cw)
        return pltpu.make_async_copy(h_ref.at[:, cs], tile.at[lax.rem(t, 2)], s_t.at[lax.rem(t, 2)])

    def w_copies(t):
        rs = pl.ds(pl.multiple_of(t * wr, wr), wr)
        sl = lax.rem(t, 2)
        return [pltpu.make_async_copy(w.at[rs, :], wtile.at[sl, i], s_w.at[sl, i]) for i, w in enumerate((wq_ref, wk_ref, wv_ref))]

    h_copy(0).start()
    for cp in w_copies(0):
        cp.start()
    with scope('greet'):
        greet(n, me)

    def v_send(e):
        to = lax.rem(me + e, n)
        return remote(bv_ref.at[to], dwv_ref.at[:, cols], s_v.at[e], r_v.at[e], to)

    def a_send(to):
        e = lax.rem(to + n - me, n)
        return remote(stage.at[0, to], dwq_ref.at[:, cols], s_a.at[e], r_a.at[e], to)

    def b_send(to):
        e = lax.rem(to + n - me, n)
        return remote(stage.at[1, to], dwk_ref.at[:, cols], s_b.at[e], r_b.at[e], to)

    def m_send(e):
        to = lax.rem(me + e, n)
        return remote(mine, mall.at[me], s_m.at[e], r_m.at[e], to)

    def g_send(e):
        to = lax.rem(me + e, n)
        return remote(gpart.at[to], gall.at[me], s_g.at[e], r_g.at[e], to)

    cl = cl_ref[...]
    sl = sl_ref[...]

    def back_rope(a):
        a = a.astype(f32)
        return a * cl + pltpu.roll(a, half, 1) * sl

    def hs(i):
        return pl.ds(pl.multiple_of(i * HEAD, HEAD), HEAD)

    def mean_step(i, carry):
        a, b = carry
        a = a + back_rope(tq_ref[:, hs(i)]) * g_ref[0:1, hs(i)] * ql_ref[:, hs(i)]
        b = b + back_rope(tkv_ref[0, :, hs(i)]) * g_ref[1:2, hs(i)] * kl_ref[:, hs(i)]
        return a, b

    zero = jnp.zeros((t_loc, HEAD), f32)
    with scope('mean'):
        a, b = lax.fori_loop(0, d // HEAD, mean_step, (zero, zero))
        mq = jnp.sum(a, axis=1, keepdims=True) * (1.0 / d)
        mk = jnp.sum(b, axis=1, keepdims=True) * (1.0 / d)
    with scope('msend'):
        mine[...] = jnp.zeros_like(mine)
        mine[0:1, :] = jnp.broadcast_to(mq, (t_loc, HEAD)).T[0:1, :]
        mine[1:2, :] = jnp.broadcast_to(mk, (t_loc, HEAD)).T[0:1, :]
        for e in range(1, n):
            m_send(e).start()
        for e in range(1, n):
            v_send(e).start()
        dwv_ref[:, cols] = bv_ref[me]
        mall[me] = mine[...]

    qi = il_ref[:, 0:1]
    ki = il_ref[:, 1:2]

    def loc_step(i, _):
        dloc[0, :, hs(i)] = (qi * (back_rope(tq_ref[:, hs(i)]) * g_ref[0:1, hs(i)] - ql_ref[:, hs(i)] * mq)).astype(bf16)
        dloc[1, :, hs(i)] = (ki * (back_rope(tkv_ref[0, :, hs(i)]) * g_ref[1:2, hs(i)] - kl_ref[:, hs(i)] * mk)).astype(bf16)
        return 0

    with scope('loc'):
        lax.fori_loop(0, d // HEAD, loc_step, 0)
    with scope('mwait'):
        for e in range(1, n):
            m_send(e).wait()

    def head_step(j, carry):
        js = pl.ds(pl.multiple_of(j * t_loc, t_loc), t_loc)
        rs = js
        ct = cs_ref[0, :, js]
        sn = cs_ref[1, :, js]
        out = []
        for u, (src, hat) in enumerate(((dq_ref[rs, :], qt_ref), (dkv_ref[j, 0], kt_ref))):
            w = src.astype(f32).T
            p, r = w[:half], w[half:]
            w = jnp.concatenate([p * ct + r * sn, r * ct - p * sn], axis=0)
            hat = hat[:, js]
            out.append(carry[u] + w * hat)
            raw[u * HEAD:(u + 1) * HEAD, js] = (iv_ref[u:u + 1, js] * (w * gc_ref[:, u:u + 1] - hat * mall[j, u:u + 1, :])).astype(bf16)
        return tuple(out)

    zt = jnp.zeros((HEAD, t_loc), f32)
    with scope('head'):
        aq, ak = lax.fori_loop(0, n, head_step, (zt, zt))
        for u, a in enumerate((aq, ak)):
            col = jnp.sum(a, axis=1, keepdims=True)
            gg_ref[u] = jnp.broadcast_to(col, (HEAD, HEAD)).T[0:8, :]

    def dw_step(t, _):
        h_copy(t).wait()

        @pl.when(t + 1 < nt)
        def _():
            h_copy(t + 1).start()
        nn = lax.rem(z + 1 + t, nt)
        r = dotf(raw[...], tile[lax.rem(t, 2)], NN)
        for u in range(2):
            to = 2 * nn + u
            for w in range(2):
                stage[w, to] = r[w * HEAD:(w + 1) * HEAD, u * HEAD:(u + 1) * HEAD].T

            @pl.when(to != me)
            def _():
                a_send(to).start()
                b_send(to).start()
        return 0

    with scope('dw'):
        lax.fori_loop(0, nt, dw_step, 0)
        dwq_ref[:, cols] = stage[0, me]
        dwk_ref[:, cols] = stage[1, me]

    def dh_step(t, _):
        for cp in w_copies(t):
            cp.wait()

        @pl.when(t + 1 < nw)
        def _():
            for cp in w_copies(t + 1):
                cp.start()
        sl = lax.rem(t, 2)
        r = dotf(dloc[0], wtile[sl, 0], NT) + dotf(dloc[1], wtile[sl, 1], NT) + dotf(tkv_ref[1], wtile[sl, 2], NT)
        dh[:, pl.ds(pl.multiple_of(t * wr, wr), wr)] = r.astype(bf16).astype(f32)
        return 0

    with scope('dh'):
        lax.fori_loop(0, nw, dh_step, 0)

    def ms_step(i, carry):
        sx, sg = carry
        xf = x_ref[:, hs(i)].astype(f32)
        return sx + xf * xf, sg + dh[:, hs(i)] * g_ref[2:3, hs(i)] * xf

    with scope('ms'):
        sx, sg = lax.fori_loop(0, d // HEAD, ms_step, (zero, zero))
        xi = lax.rsqrt(jnp.sum(sx, axis=1, keepdims=True) * (1.0 / d) + NORM_EPS)
        mx = jnp.sum(sg, axis=1, keepdims=True) * xi * (1.0 / d)

    def gx_step(i, _):
        xh = x_ref[:, hs(i)].astype(f32) * xi
        dhh = dh[:, hs(i)]
        gpart[i] = jnp.broadcast_to(jnp.sum(dhh * xh, axis=0, keepdims=True), (8, HEAD))
        gx_ref[:, hs(i)] = (gy_ref[:, hs(i)].astype(f32) + xi * (dhh * g_ref[2:3, hs(i)] - xh * mx)).astype(bf16)
        return 0

    with scope('gx'):
        lax.fori_loop(0, d // HEAD, gx_step, 0)
    with scope('gsend'):
        for e in range(1, n):
            g_send(e).start()
        gall[me] = gpart[me]
        for e in range(1, n):
            g_send(e).wait()
        gn_ref[...] = jnp.sum(gall[...], axis=0)
    for e in range(1, n):
        v_send(e).wait()
        a_send(lax.rem(me + e, n)).wait()
        b_send(lax.rem(me + e, n)).wait()


def last(n, vmem_args, hbm_args, cid):
    t_all, d = hbm_args[0].shape
    t_loc = t_all // n
    vm = pl.BlockSpec(memory_space=pltpu.VMEM)
    hb = pl.BlockSpec(memory_space=pl.ANY)
    S = jax.ShapeDtypeStruct
    V = pltpu.VMEM
    sem = pltpu.SemaphoreType.DMA
    return pl.pallas_call(functools.partial(last_kernel, n),
        in_specs=[vm] * len(vmem_args) + [hb] * 4, out_specs=[vm] * 6,
        out_shape=[S((t_loc, d), bf16)] + [S((d // n, d), f32)] * 3 + [S((2, 8, HEAD), f32), S((8, d // n), f32)],
        scratch_shapes=[V((2 * HEAD, t_all), bf16), V((2, n, d // n, HEAD), f32), V((2, t_loc, d), bf16), V((t_loc, d), f32), V((8, t_loc), f32), V((n, 8, t_loc), f32), V((n, 8, d // n), f32), V((n, 8, d // n), f32), V((2, t_all, 2 * HEAD), bf16), V((2, 3, 256, d), bf16)]
        + [sem((n,))] * 10 + [sem((2,)), sem((2, 3))],
        compiler_params=pltpu.CompilerParams(collective_id=cid, has_side_effects=True, vmem_limit_bytes=63 * 1024 * 1024), name='last')(*vmem_args, *hbm_args)


def spread_kernel(n, gather, x_ref, o_ref, send_sem, recv_sem):
    me = lax.axis_index('sp')
    barrier = pltpu.get_barrier_semaphore()
    for d in range(1, n):
        pl.semaphore_signal(barrier, inc=1, device_id={'sp': lax.rem(me + d, n)}, device_id_type=MESH)
    pl.semaphore_wait(barrier, n - 1)
    copies = []
    for d in range(1, n):
        to = lax.rem(me + d, n)
        src = x_ref if gather else x_ref.at[to]
        cp = pltpu.make_async_remote_copy(src_ref=src, dst_ref=o_ref.at[me], send_sem=send_sem.at[d], recv_sem=recv_sem.at[d], device_id={'sp': to}, device_id_type=MESH)
        cp.start()
        copies.append(cp)
    o_ref[me] = x_ref[...] if gather else x_ref[me]
    for cp in copies:
        cp.wait()


def spread(x, n, gather, cid):
    shape = (n,) + x.shape if gather else x.shape
    return pl.pallas_call(functools.partial(spread_kernel, n, gather), out_shape=jax.ShapeDtypeStruct(shape, x.dtype),
        in_specs=[pl.BlockSpec(memory_space=pltpu.VMEM)], out_specs=pl.BlockSpec(memory_space=pltpu.VMEM),
        scratch_shapes=[pltpu.SemaphoreType.DMA((n,)), pltpu.SemaphoreType.DMA((n,))],
        compiler_params=pltpu.CompilerParams(collective_id=cid, has_side_effects=True), name='spread%d' % cid)(x)


def rope_tables(positions):
    half = HEAD // 2
    inv_freq = ROPE_BASE ** (-jnp.arange(half, dtype=f32) * (2.0 / HEAD))
    ang = positions.astype(f32)[:, None] * inv_freq
    return jnp.cos(ang), jnp.sin(ang)


def rope(x, cos, sin):
    a, b = x[..., :HEAD // 2], x[..., HEAD // 2:]
    return jnp.concatenate([a * cos - b * sin, b * cos + a * sin], -1)


def mm(a, b, dims=(((1,), (0,)), ((), ()))):
    return lax.dot_general(a, b, dims, preferred_element_type=f32)


def solution(mesh):
    n = mesh.shape['sp']

    def device_step(x_in, grad_y, positions, g_norm, wq, wk, wv, wo, gq, gk):
        me = lax.axis_index('sp')
        xb = x_in[0]
        x = xb.astype(f32)
        gy = grad_y[0]
        t_loc, d = x.shape
        t_all = t_loc * n
        hd = d // n
        gn_f, gq_f, gk_f = g_norm.astype(f32), gq.astype(f32), gk.astype(f32)
        x_inv = lax.rsqrt(jnp.mean(x * x, -1, keepdims=True) + NORM_EPS)
        hid = (x * x_inv * gn_f).astype(bf16)
        h_all = lax.all_gather(hid, 'sp', axis=0, tiled=True)
        gy_all = lax.all_gather(gy, 'sp', axis=0, tiled=True)
        q1l = mm(hid, wq)
        k1l = mm(hid, wk)
        q_inv = lax.rsqrt(jnp.mean(q1l * q1l, -1) + NORM_EPS)
        k_inv = lax.rsqrt(jnp.mean(k1l * k1l, -1) + NORM_EPS)
        pos = positions[0]
        st = spread(jnp.stack([q_inv, k_inv, pos.astype(f32), q_inv, q_inv, q_inv, q_inv, q_inv]), n, True, 1)
        st = jnp.swapaxes(st, 0, 1).reshape(8, t_all)
        qi, ki = st[0][:, None], st[1][:, None]
        cos, sin = rope_tables(st[2])
        cs_t = jnp.stack([cos.T, sin.T])
        sl = lambda w: lax.dynamic_slice_in_dim(w, me * hd, hd, w.ndim - 1)
        gq_h, gk_h = sl(gq_f), sl(gk_f)
        qkv = mm(h_all, jnp.concatenate([sl(wq), sl(wk), sl(wv)], 1))
        q_hat, k_hat = qkv[:, :hd] * qi, qkv[:, hd:2 * hd] * ki
        q = rope(q_hat * gq_h, cos, sin).astype(bf16)
        k = rope(k_hat * gk_h, cos, sin).astype(bf16)
        v = qkv[:, 2 * hd:].astype(bf16)
        o, o_f, lse = attn_fwd(q, k, v)
        wo_h = lax.dynamic_slice_in_dim(wo, me * hd, hd, 0)
        do = mm(gy_all, wo_h, (((1,), (1,)), ((), ()))).astype(bf16)
        delta = jnp.broadcast_to(jnp.sum(o_f * do.astype(f32), -1)[None], (8, t_all))
        dq, dkv, tq, tkv, y, dwo, bv = back(n, q, k, v, do, o, lse, delta, xb, wo, gy_all, h_all, 4)
        cl, sn = rope_tables(pos)
        cl, sn = jnp.concatenate([cl, cl], 1), jnp.concatenate([sn, -sn], 1)
        qh_l, kh_l = q1l * q_inv[:, None], k1l * k_inv[:, None]
        gains = jnp.stack([gq_f, gk_f, gn_f] + [gn_f] * 5)
        gx, dwq, dwk, dwv, gg, gn = last(n, [dq, dkv, tq, tkv, bv, q_hat.T, k_hat.T, st, cs_t, jnp.stack([gq_h, gk_h], 1), qh_l, kh_l, jnp.stack([q_inv, k_inv], 1), cl, sn, gains, xb, gy], [h_all, wq, wk, wv], 5)
        return (y[None], gx[None], gn[0], dwq, dwk, dwv, dwo, gg[0, 0], gg[1, 0])

    seq_spec = P('dp', 'sp', None)
    rep2, rep1 = P(None, None), P(None)
    row_spec, vec_spec = P(('dp', 'sp'), None), P(('dp', 'sp'))
    return jax.shard_map(device_step, mesh=mesh, in_specs=(seq_spec, seq_spec, P('dp', 'sp'), rep1, rep2, rep2, rep2, rep2, rep1, rep1), out_specs=(seq_spec, seq_spec, vec_spec, row_spec, row_spec, row_spec, row_spec, vec_spec, vec_spec), check_vma=False)
```

time: 499 us -> 434 us (0.87)
  Pallas kernels: 154 us -> 245 us
  matrix products: 87.7 us -> 35.7 us
  blocking collectives: 32 us -> 0 us
  other arithmetic: 52 us -> 21.3 us
  starting transfers between devices: 18.3 us -> 0.13 us
  waiting for transfers between devices: 110 us -> 93.9 us
    pallas_call x1 -> x2, Pallas kernels: 37.1 us -> 199 us  [the longest x1 105 us: back(): pl.pallas_call(functools.partial(back_kernel, n), in_specs=[vm] * 8 + [hb...]
    pallas_call x3 -> x1, Pallas kernels: 89.4 us -> 17.6 us  [spread(): pl.pallas_call(functools.partial(spread_kernel, n, gather), out_shape=jax...]
    dot_general x10 -> x4, matrix products: 87.7 us -> 35.7 us  [mm(): return lax.dot_general(a, b, dims, preferred_element_type=f32)]
    all_to_all x1 -> x0, blocking collectives: 32 us -> none  [device_step(): lax.all_to_all(z, 'sp', split_axis=0, concat_axis=1, tiled=True)]
    all_to_all x4 -> x0, starting transfers between devices: 18.2 us -> none  [the longest x2 9.03 us: device_step(): lax.all_to_all(z, 'sp', split_axis=0, concat_axis=1, tiled=True)]
    add x2 -> x0, other arithmetic: 13.9 us -> none  [unrope(): return jnp.concatenate([a * cos + b * sin, b * cos - a * sin], -1)]
    all_gather x1, waiting for transfers between devices: 62.9 us -> 51.1 us  [device_step(): h_all = lax.all_gather(hid, 'sp', axis=0, tiled=True)]
    reduce_sum x4 -> x0, other arithmetic: 11.3 us -> none  [the longest x1 8.08 us: device_step(): ggq, ggk = (jnp.sum(dq_rot * q_hat, 0), jnp.sum(dk_rot * k_hat, 0))]
  transfers between devices with their start and end apart: 6 -> 2, of which waited for: 4 -> 2; matrix products, arithmetic and copies ran while one was open for 28% -> 12% of each run, Pallas kernels for 24% -> 10%
where the time goes in v2:
time: 434 us; the launch traced here: 433 us
  Pallas kernels  245 us (56%)
  waiting for transfers between devices  93.9 us (22%)
  matrix products  35.7 us (8%)
  local copies, waits for them, and re-layouts  22.9 us (5%)
  other arithmetic  21.3 us (5%)
  between operations  14.2 us (3%)
    pallas_call x1, Pallas kernels, back(): pl.pallas_call(functools.partial(back_kernel, n), in_specs=[vm] * 8 + [hb...  105 us
    pallas_call x1, Pallas kernels, last(): pl.pallas_call(functools.partial(last_kernel, n), in_specs=[vm] * len(vme...  94.4 us
    all_gather x1, waiting for transfers between devices, device_step(): h_all = lax.all_gather(hid, 'sp', axis=0, tiled=True)  51.1 us
    all_gather x1, waiting for transfers between devices, device_step(): gy_all = lax.all_gather(gy, 'sp', axis=0, tiled=True)  42 us
    dot_general x4, matrix products, mm(): return lax.dot_general(a, b, dims, preferred_element_type=f32)  35.7 us
    pallas_call x1, Pallas kernels, attn_fwd(): pl.pallas_call(functools.partial(fwd_kernel, bq, bk), grid=(n // bq,), in...  27.8 us
    pallas_call x1, Pallas kernels, spread(): pl.pallas_call(functools.partial(spread_kernel, n, gather), out_shape=jax...  17.6 us
    unnamed x27, local copies, waits for them, and re-layouts  9.62 us
  transfers between devices with their start and end apart: 2, of which 2 were waited for; matrix products, arithmetic and copies ran while one was open for 12% of the time, Pallas kernels for 10%

profile of v2, /device:TPU:21, one launch (start us, length us, event | category | flops | bytes accessed | tf_op | source)
XLA Modules:
  0.0 432.8 jit_solution(9338561461931403938)
XLA Ops:
  7.9 1.5 fusion.1
  9.5 2.5 fusion.3
  13.2 5.8 %multiply_reduce_fusion.2 = (f32[256]{0:T(256)S(1)}, f32[256,2048]{1,0:T(8,128)S(1)}) fusion(bf16[256,2048]{1,0:T(8,128)(2,1)S(1)} %copy-done, bf16[2048,2048]{1,0:T(8,128)(2,1)} %wq_ref.1), kind=kOutput, calls=%fused_computation.12 | convolution fusion | flops 2148531968 | bytes 11535360 | tf_op jit(solution)/shard_map/dot_general | solution.py:510
  19.1 7.1 %multiply_reduce_fusion.1 = (f32[256]{0:T(256)S(1)}, f32[256,2048]{1,0:T(8,128)}) fusion(bf16[256,2048]{1,0:T(8,128)(2,1)S(1)} %copy-done, bf16[2048,2048]{1,0:T(8,128)(2,1)} %wk_ref.1), kind=kOutput, calls=%fused_computation.11 | convolution fusion | flops 2148531968 | bytes 11535360 | tf_op jit(solution)/shard_map/dot_general | solution.py:510
  26.8 17.6 %spread1.1 = f32[16,8,256]{2,1,0:T(8,128)} custom-call(f32[8,256]{1,0:T(8,128)} %stack.18.x_ref), custom_call_target="tpu_custom_call" | custom-call | tf_op jit(solution)/shard_map/spread1/pallas_call | solution.py:491
  48.3 1.1 fusion.35
  49.4 1.9 constant_dynamic-slice_fusion.2
  51.3 1.3 constant_dynamic-slice_fusion
  52.5 3.7 multiply_cosine_fusion
  56.2 1.5 pad_maximum_fusion.cs_ref
  57.7 0.9 copy-done.1
  58.6 2.3 broadcast_multiply_fusion
  60.9 51.1 %all-gather.4.cloned.1.call-done.h_ref = bf16[4096,2048]{1,0:T(8,128)(2,1)} async-done(((bf16[256,2048]{1,0:T(8,128)(2,1)}), bf16[4096,2048]{1,0:T(8,128)(2,1)}) %all-gather.4.cloned.1.call-update) | async-done | bytes 16777232 | tf_op jit(solution)/shard_map/all_gather | solution.py:527
  112.0 10.7 %fusion.8 = f32[4096,384]{0,1:T(8,128)S(1)} fusion(bf16[4096,2048]{1,0:T(8,128)(2,1)} %all-gather.4.cloned.1.call-done.h_ref, bf16[2048,128]{1,0:T(8,128)(2,1)S(1)} %get-tuple-element.69, bf16[2048,128]{1,0:T(8,128)(2,1)S(1)} %get-tuple-element.70, bf16[2048,128]{1,0:T(8,128)(2,1)} %constant_dynamic-slice_fusion.2), kind=kOutput, calls=%fused_computation.17 | convolution fusion | flops 6447169536 | bytes 24641536 | tf_op jit(solution)/shard_map/dot_general | solution.py:510
  122.9 2.7 fusion.6
  125.6 4.8 %fusion.27 = (bf16[4096,64]{0,1:T(8,128)(2,1)S(1)}, bf16[4096,64]{0,1:T(8,128)(2,1)S(1)}, bf16[4096,64]{0,1:T(8,128)(2,1)S(1)}, bf16[4096,64]{0,1:T(8,128)(2,1)S(1)}) fusion(f32[4096,128]{0,1:T(8,128)S(1)} %get-tuple-element.42, f32[64]{0:T(128)S(1)} %multiply_power_fusion, f32[4096]{0:T(1024)S(1)} %bitcast.61, f32[4096,128]{0,1:T(8,128)S(1)} %get-tuple-element.45), kind=kLoop, calls=%fused_computation.40 | loop fusion | flops 4456448 | bytes 6308096 | tf_op jit(solution)/shard_map/convert.1
  130.4 1.3 copy.42.k_ref
  131.9 1.3 copy.41.q_ref
  133.2 1.3 copy.46.v_ref
  134.5 27.8 %attn_fwd.1 = (bf16[4096,128]{1,0:T(8,128)(2,1)}, f32[4096,128]{1,0:T(8,128)}, f32[8,4096]{1,0:T(8,128)}) custom-call(bf16[4096,128]{1,0:T(8,128)(2,1)} %copy.41.q_ref, bf16[4096,128]{1,0:T(8,128)(2,1)} %copy.42.k_ref, bf16[4096,128]{1,0:T(8,128)(2,1)} %copy.46.v_ref), custom_call_target="tpu_custom_call" | custom-call | tf_op jit(solution)/shard_map/attn_fwd/pallas_call | solution.py:54
  162.2 42.0 %all-gather.6.cloned.1.call-done = bf16[1,4096,2048]{2,1,0:T(8,128)(2,1)} async-done(((bf16[1,256,2048]{2,1,0:T(8,128)(2,1)}), bf16[1,4096,2048]{2,1,0:T(8,128)(2,1)}) %all-gather.6.cloned.1.call-update) | async-done | bytes 16777232 | tf_op jit(solution)/shard_map/all_gather | solution.py:528
  204.2 12.0 %multiply_reduce_fusion = (f32[4096]{0:T(1024)S(1)}, bf16[4096,128]{1,0:T(8,128)(2,1)}) fusion(f32[4096,128]{1,0:T(8,128)} %get-tuple-element.27, bf16[1,4096,2048]{2,1,0:T(8,128)(2,1)} %all-gather.6.cloned.1.call-done, bf16[2048,2048]{1,0:T(8,128)(2,1)} %wo_ref.1, s32[]{:T(128)S(6)} %select_n.2), kind=kOutput, calls=%fused_computation.10 | convolution fusion | flops 2149576704 | bytes 20463620 | tf_op jit(solution)/shard_map/dot_general | solution.py:510
  216.9 104.9 %back.1 = (bf16[4096,128]{1,0:T(8,128)(2,1)}, bf16[16,2,256,128]{3,2,1,0:T(8,128)(2,1)}, bf16[256,2048]{1,0:T(8,128)(2,1)}, bf16[2,256,2048]{2,1,0:T(8,128)(2,1)...) custom-call(bf16[4096,128]{1,0:T(8,128)(2,1)} %copy.41.q_ref, ...), custom_call_target="tpu_custom_call" | custom-call | tf_op jit(solution)/shard_map/back/pallas_call | solution.py:256
  321.8 94.4 %last.1 = (bf16[256,2048]{1,0:T(8,128)(2,1)}, f32[128,2048]{1,0:T(8,128)}, f32[128,2048]{1,0:T(8,128)}, f32[128,2048]{1,0:T(8,128)}, f32[2,8,128]{2,1,0:T(8,128)}, /*index=5*/f32[8,128]{1,0:T(8,128)}) custom-call(bf16[4096,128]{1,0:T(8,128)(2,1)} %get-tuple-element.29.dq_ref, bf16[16,2,256,128]{3,2,1,0:T(8,128)(2,1)} %get-tuple-element.30.dkv_ref, ...), custom_call_target="tpu_custom_call" | custom-call | tf_op jit(solution)/shard_map/last/pallas_call | solution.py:463
  416.2 1.3 slice_bitcast_fusion
  417.5 1.2 slice_bitcast_fusion.2
  418.7 2.4 copy.53
  421.1 1.0 copy.54
  422.0 1.0 copy.55
  423.0 1.0 copy.56
  424.0 1.0 copy.57
  425.0 1.0 copy.58
  (47 shorter events, 7.4 us)
Async XLA Ops:
  7.2 104.8 %all-gather.4.cloned.1.call-start = ((), (), s32[]{:S(2)}) async-start(), calls=%async_computation | async-start | bytes 17825792 | tf_op jit(solution)/shard_map/all_gather | solution.py:527
  9.5 3.4 copy-start.7
  9.5 3.5 copy-start.8
  9.5 3.6 copy-start.9
  12.0 1.2 copy-start
  12.1 192.1 %all-gather.6.cloned.1.call-start = ((), (), s32[]{:S(2)}) async-start(), calls=%async_computation.1 | async-start | bytes 17825792 | tf_op jit(solution)/shard_map/all_gather | solution.py:528
  56.2 2.4 copy-start.1
  416.2 4.9 %copy-start.6 = (bf16[256,2048]{1,0:T(8,128)(2,1)S(1)}, bf16[256,2048]{1,0:T(8,128)(2,1)}, u32[]{:S(2)}) copy-start(bf16[256,2048]{1,0:T(8,128)(2,1)} %get-tuple-element.34) | copy-start | bytes 3145732
  418.7 3.4 copy-start.5
  421.1 1.9 copy-start.4
  422.0 1.9 copy-start.3
  423.0 1.9 copy-start.2
Sparse Core Ops, SparseCore 0:
  12.2 99.7 all-gather.3
  113.6 90.5 all-gather.5

commit v3 on v0

v3 whole, which is shorter than its diff:
```python
import contextlib
import functools
import jax
import jax.numpy as jnp
import numpy as np
from jax import lax
from jax.experimental import pallas as pl
from jax.experimental.pallas import tpu as pltpu
from jax.sharding import PartitionSpec as P

HEAD = 128
NORM_EPS = 1e-5
ROPE_BASE = 10000.0
LOG2E = 1.4426950408889634
f32 = jnp.float32
bf16 = jnp.bfloat16
MESH = pl.DeviceIdType.MESH
NN = (((1,), (0,)), ((), ()))
NT = (((1,), (1,)), ((), ()))
TN = (((0,), (0,)), ((), ()))
PROF = 0
scope = jax.named_scope if PROF else (lambda name: contextlib.nullcontext())


def dotf(a, b, dims):
    return lax.dot_general(a, b, dims, preferred_element_type=f32)


def remote(src, dst, ss, rs, to):
    return pltpu.make_async_remote_copy(src_ref=src, dst_ref=dst, send_sem=ss, recv_sem=rs, device_id={'sp': to}, device_id_type=MESH)


def ds(i, size):
    return pl.ds(pl.multiple_of(i * size, size), size)


def as_row(col):
    return jnp.broadcast_to(col, (col.shape[0], HEAD)).T[0:1, :]


def loop(lo, hi, body):
    def step(i, carry):
        body(i)
        return carry
    lax.fori_loop(lo, hi, step, 0)


def block_kernel(n, x_hbm, gy_hbm, pos_ref, g_ref, fr_ref, wq_ref, wk_ref, wv_ref, wo_ref,
                 y_out, gx_out, gn_ref, dwq_out, dwk_out, dwv_out, dwo_out, gg_ref, h_all, gy_all,
                 x_ref, gy_ref, hid, wh, woh, raw, xbuf, wtile, tile, wrow, qkl, hatT, csT, q_s, k_s, v_s, do_s, o_s, lse, dl,
                 dq_s, dkv, tq, tkv, att, dt, bv, rawT, y_s, dwo_s, gx_s, dh, ssq, cl_s, sl_s, inv, mine, sall, mine2, mall, gpart, gall,
                 s_ring, r_ring, s_par, r_par, s_own, r_own, s_st, r_st, s_o, r_o, s_kv, r_kv, s_q, r_q, s_v, r_v, s_a, r_a, s_b, r_b, s_m, r_m, s_g, r_g,
                 s_ld, s_t, s_w, s_x, s_loc, s_out):
    me = lax.axis_index('sp')
    t_loc, d = x_hbm.shape
    t_all = t_loc * n
    z = me // 2
    c = lax.rem(me, 2)
    nz = n // 2
    mate = me + 1 - 2 * c
    up = lax.rem(z + 1, nz) * 2 + c
    down = lax.rem(z + nz - 1, nz) * 2 + c
    nd = d // HEAD
    half = HEAD // 2
    sub = t_loc // 4
    last = nz - 2
    ticks = 2 * (nz - 1)
    blk = 2 * t_loc
    nb = t_all // blk
    cexp = HEAD ** -0.5 * LOG2E
    scale = HEAD ** -0.5
    cw = tile.shape[2]
    nt = d // cw
    wr = wrow.shape[2]
    nw = d // wr
    cols = ds(me, HEAD)
    far = sorted(range(1, n), key=lambda e: -min(e, n - e))
    early = far[:2]
    alls = (h_all, gy_all)
    own_src = (hid, gy_ref)

    def peer(e):
        return lax.rem(me + e, n)

    def rows(i):
        return ds(i, t_loc)

    def hs(i):
        return ds(i, HEAD)

    def chip(s):
        k = nz // 2 - (s + 1) // 2
        return lax.rem(z + nz + jnp.where(lax.rem(s, 2) == 0, -k, k), nz)

    def piece(core, direction, s, u):
        bz = lax.rem(z + nz - 1 - s, nz) if direction == 0 else lax.rem(z + 1 + s, nz)
        return ds((bz * 2 + core) * 4 + 2 * direction + u, sub)

    def ring(a, direction, s, u):
        ref = alls[a]
        bz = lax.rem(z + nz - s, nz) if direction == 0 else lax.rem(z + s, nz)
        rs = ds((bz * 2 + c) * 4 + 2 * direction + u, sub)
        return remote(ref.at[rs, :], ref.at[rs, :], s_ring.at[a, direction, s, u], r_ring.at[a, direction, s, u], up if direction == 0 else down)

    def ring0(a, direction, u):
        rs = ds(me * 4 + 2 * direction + u, sub)
        return remote(own_src[a].at[pl.ds((2 * direction + u) * sub, sub), :], alls[a].at[rs, :], s_ring.at[a, direction, 0, u], r_ring.at[a, direction, 0, u], up if direction == 0 else down)

    def par(a, direction, s, u):
        rs = piece(c, direction, s, u)
        return remote(alls[a].at[rs, :], alls[a].at[rs, :], s_par.at[a, direction, s, u], r_par.at[a, direction, s, u], mate)

    def own_par(a):
        return remote(own_src[a], alls[a].at[rows(me), :], s_own.at[a], r_own.at[a], mate)

    def own_loc(a):
        return pltpu.make_async_copy(own_src[a], alls[a].at[rows(me), :], s_loc.at[a])

    def comm(a, t):
        s = t // 2
        u = lax.rem(t, 2)
        for direction in range(2):
            ring(a, direction, s, u).wait_recv()

            @pl.when(s < last)
            def _():
                ring(a, direction, s + 1, u).start()
            par(a, direction, s, u).start()

    def loads(a, t):
        s = t // 2
        u = lax.rem(t, 2)
        slot = lax.rem(t, 2)
        out = []
        for i, (core, direction) in enumerate(((c, 0), (c, 1), (1 - c, 0), (1 - c, 1))):
            out.append(pltpu.make_async_copy(alls[a].at[piece(core, direction, s, u), :], xbuf.at[slot, pl.ds(i * sub, sub), :], s_ld.at[slot, i]))
        return out

    def mate_load(a):
        return pltpu.make_async_copy(alls[a].at[rows(mate), :], xbuf.at[1], s_ld.at[1, 0])

    def spots(t):
        s = t // 2
        u = lax.rem(t, 2)
        return [piece(c, 0, s, u), piece(c, 1, s, u), piece(1 - c, 0, s, u), piece(1 - c, 1, s, u)]

    def gather(a, t, work, put):
        @pl.when(t < ticks)
        def _():
            with scope('comm'):
                comm(a, t)

        @pl.when(t == 0)
        def _():
            own_par(a).wait_recv()
            mate_load(a).start()
            put(work(own_src[a][...]), [rows(me)])

        @pl.when(t == 1)
        def _():
            mate_load(a).wait()
            put(work(xbuf[1]), [rows(mate)])

        @pl.when(t >= 2)
        def _():
            for cp in loads(a, t - 2):
                cp.wait()
            put(work(xbuf[lax.rem(t, 2)]), spots(t - 2))

        @pl.when((t >= 1) & (t < ticks + 1))
        def _():
            for direction in range(2):
                par(a, direction, (t - 1) // 2, lax.rem(t - 1, 2)).wait_recv()
            for cp in loads(a, t - 1):
                cp.start()

    def stat_tile(i, act):
        slot = lax.rem(i, 2)
        cs = ds(lax.rem(i, nt), cw)

        @pl.when(i < nt)
        def _():
            act(pltpu.make_async_copy(wq_ref.at[:, cs], wtile.at[slot], s_w.at[slot]))

        @pl.when(i >= nt)
        def _():
            act(pltpu.make_async_copy(wk_ref.at[:, cs], wtile.at[slot], s_w.at[slot]))

    def start(cp):
        cp.start()

    def wait(cp):
        cp.wait()

    def stat_step(i):
        stat_tile(i, wait)

        @pl.when(i + 1 < 2 * nt)
        def _():
            stat_tile(i + 1, start)
        r = dotf(hid[...], wtile[lax.rem(i, 2)], NN)
        w = i // nt
        qkl[w, :, ds(lax.rem(i, nt), cw)] = r
        acc = r[:, :HEAD] * r[:, :HEAD]
        for j in range(1, cw // HEAD):
            acc = acc + r[:, j * HEAD:(j + 1) * HEAD] * r[:, j * HEAD:(j + 1) * HEAD]
        ssq[w] = ssq[w] + acc

    def st_send(e):
        return remote(mine, sall.at[me], s_st.at[e], r_st.at[e], peer(e))

    sgn = jnp.where(lax.broadcasted_iota(jnp.int32, (1, HEAD), 1) < half, -1.0, 1.0).astype(f32)

    def stat_done():
        for w in range(2):
            iv = lax.rsqrt(jnp.sum(ssq[w], axis=1, keepdims=True) * (1.0 / d) + NORM_EPS)
            inv[w] = jnp.broadcast_to(iv, (t_loc, HEAD))
            mine[w:w + 1, :] = as_row(iv)
        mine[2:3, :] = pos_ref[...].astype(f32)
        for e in range(1, n):
            st_send(e).start()
        sall[me] = mine[...]
        ang = spread_col(pos_ref[...].astype(f32)) * fr_ref[0:1, :]
        cl_s[...] = jnp.cos(ang)
        sl_s[...] = jnp.sin(ang) * (-sgn)

    def spread_col(row):
        return jnp.broadcast_to(row, (HEAD, row.shape[1])).T

    def head_w(i):
        w = (wq_ref, wk_ref, wv_ref)[i]
        return pltpu.make_async_copy(w.at[:, cols], wh.at[:, pl.ds(i * HEAD, HEAD)], s_x.at[i])

    def wo_load():
        return pltpu.make_async_copy(wo_ref.at[cols, :], woh, s_x.at[3])

    with scope('begin'):
        barrier = pltpu.get_barrier_semaphore()
        for e in range(1, n):
            pl.semaphore_signal(barrier, inc=1, device_id={'sp': peer(e)}, device_id_type=MESH)
        first = [pltpu.make_async_copy(x_hbm, x_ref, s_x.at[4]), pltpu.make_async_copy(gy_hbm, gy_ref, s_x.at[5])]
        for cp in first:
            cp.start()
        for i in range(3):
            head_w(i).start()
        wo_load().start()
        stat_tile(0, start)
        first[0].wait()
        zero = jnp.zeros((t_loc, HEAD), f32)

        def sq_step(i, acc):
            xf = x_ref[:, hs(i)].astype(f32)
            return acc + xf * xf

        x_inv = lax.rsqrt(jnp.sum(lax.fori_loop(0, nd, sq_step, zero), axis=1, keepdims=True) * (1.0 / d) + NORM_EPS)

        def hid_step(i):
            hid[:, hs(i)] = (x_ref[:, hs(i)].astype(f32) * x_inv * g_ref[2:3, hs(i)]).astype(bf16)

        loop(0, nd, hid_step)
        mine[...] = jnp.zeros_like(mine)
        mine2[...] = jnp.zeros_like(mine2)
        ssq[...] = jnp.zeros_like(ssq)
        first[1].wait()
        own_loc(1).start()
        pl.semaphore_wait(barrier, n - 1)
    for u in range(2):
        for direction in range(2):
            ring0(0, direction, u).start()
    own_par(0).start()
    own_par(1).start()
    own_loc(0).start()
    for i in range(3):
        head_w(i).wait()
    wo_load().wait()

    def qkv_work(xv):
        return dotf(xv, wh[...], NN)

    def qkv_put(r, where):
        step = r.shape[0] // len(where)
        for i, rs in enumerate(where):
            for w in range(3):
                raw[w, rs, :] = r[i * step:(i + 1) * step, w * HEAD:(w + 1) * HEAD]

    spt = 2 * nt // 4

    def x_tick(t):
        gather(0, t, qkv_work, qkv_put)

        @pl.when(t == 2 * last - 1)
        def _():
            for u in range(2):
                for direction in range(2):
                    ring0(1, direction, u).start()

        @pl.when(t < 4)
        def _():
            with scope('stat'):
                loop(t * spt, (t + 1) * spt, stat_step)

        @pl.when(t == 4)
        def _():
            with scope('statdone'):
                stat_done()

    with scope('gather_x'):
        loop(0, ticks + 2, x_tick)
        for e in range(1, n):
            st_send(e).wait()

    def finish(j):
        rs = rows(j)
        st = sall[j]
        ang = spread_col(st[2:3, :]) * fr_ref[0:1, :]
        co = jnp.cos(ang)
        si = jnp.sin(ang)
        csT[0, :, rs] = co.T[:half, :]
        csT[1, :, rs] = si.T[:half, :]
        si = si * sgn
        for w, dst in enumerate((q_s, k_s)):
            hat = raw[w, rs, :] * spread_col(st[w:w + 1, :])
            hatT[w, :, rs] = hat.T
            hat = hat * g_ref[w:w + 1, cols]
            dst[rs, :] = (hat * co + pltpu.roll(hat, half, 1) * si).astype(bf16)
        v_s[rs, :] = raw[2, rs, :].astype(bf16)

    def attend(j):
        qs = ds(j, blk)
        q = q_s[qs, :]

        def unit(kb, carry, masked):
            m, l, acc = carry
            ks = ds(kb, blk)
            s = dotf(q, k_s[ks, :], NT)
            if masked:
                r = lax.broadcasted_iota(jnp.int32, (blk, blk), 0)
                cc = lax.broadcasted_iota(jnp.int32, (blk, blk), 1)
                s = jnp.where(r >= cc, s, -1e30)
            mn = jnp.maximum(m, jnp.max(s, axis=1, keepdims=True))
            al = jnp.exp2((m - mn) * cexp)
            p = jnp.exp2((s - mn) * cexp)
            l = l * al + jnp.sum(p, axis=1, keepdims=True)
            acc = acc * al + dotf(p.astype(bf16), v_s[ks, :], NN)
            return mn, l, acc

        init = (jnp.full((blk, 1), -1e30, f32), jnp.zeros((blk, 1), f32), jnp.zeros((blk, HEAD), f32))
        carry = lax.fori_loop(0, j, functools.partial(unit, masked=False), init)
        m, l, acc = unit(j, carry, True)
        o = acc / l
        raw[2, qs, :] = o
        o_s[qs, :] = o.astype(bf16)
        lse[0:1, qs] = as_row(m * cexp + jnp.log2(l))

    def o_send(e):
        to = peer(e)
        return remote(o_s.at[rows(to), :], att.at[:, cols], s_o.at[e], r_o.at[e], to)

    def do_work(xv):
        return dotf(xv, woh[...], NT).astype(bf16)

    def do_put(r, where):
        step = r.shape[0] // len(where)
        for i, rs in enumerate(where):
            do_s[rs, :] = r[i * step:(i + 1) * step]

    fpt = n // 4

    def y_tick(t):
        gather(1, t, do_work, do_put)

        @pl.when(t < 4)
        def _():
            with scope('finish'):
                loop(t * fpt, (t + 1) * fpt, finish)

        @pl.when((t >= 4) & (t < 4 + nb))
        def _():
            with scope('attend'):
                attend(t - 4)

        @pl.when(t == 4 + nb)
        def _():
            for e in far:
                o_send(e).start()

    with scope('gather_y'):
        loop(0, ticks + 2, y_tick)

    def gy_copy(t):
        return pltpu.make_async_copy(gy_all.at[:, ds(t, cw)], tile.at[lax.rem(t, 2)], s_t.at[lax.rem(t, 2)])

    def h_copy(t):
        return pltpu.make_async_copy(h_all.at[:, ds(lax.rem(t, nt), cw)], tile.at[lax.rem(t, 2)], s_t.at[lax.rem(t, 2)])

    def h2_copy(t):
        return pltpu.make_async_copy(h_all.at[:, ds(chip(t), cw)], tile.at[lax.rem(t, 2)], s_t.at[lax.rem(t, 2)])

    def wo_copy(t):
        return pltpu.make_async_copy(wo_ref.at[:, ds(t, cw)], wtile.at[lax.rem(t, 2)], s_w.at[lax.rem(t, 2)])

    def q_send(e):
        to = peer(e)
        return remote(dq_s.at[rows(to), :], tq.at[:, cols], s_q.at[e], r_q.at[e], to)

    def kv_send(to):
        e = lax.rem(to + n - me, n)
        return remote(dkv.at[to], tkv.at[:, :, cols], s_kv.at[e], r_kv.at[e], to)

    own_loc(0).wait()
    own_loc(1).wait()
    gy_copy(0).start()
    wo_copy(0).start()
    att[:, cols] = o_s[rows(me), :]
    raw[0] = jnp.zeros((t_all, HEAD), f32)

    def delta(j):
        qs = ds(j, blk)
        dl[0:1, qs] = as_row(jnp.sum(raw[2, qs, :] * do_s[qs, :].astype(f32), axis=1, keepdims=True))

    with scope('delta'):
        loop(0, nb, delta)

    def bwd_step(s):
        kb = chip(s)
        ks = ds(kb, blk)
        k = k_s[ks, :]
        v = v_s[ks, :]

        def unit(qb, carry, masked):
            dk, dv = carry
            qs = ds(qb, blk)
            q = q_s[qs, :]
            do = do_s[qs, :]
            p = jnp.exp2(dotf(k, q, NT) * cexp - lse[0:1, qs])
            if masked:
                r = lax.broadcasted_iota(jnp.int32, (blk, blk), 0)
                cc = lax.broadcasted_iota(jnp.int32, (blk, blk), 1)
                p = jnp.where(cc >= r, p, 0.0)
            g = (p * (dotf(v, do, NT) - dl[0:1, qs])).astype(bf16)
            dv = dv + dotf(p.astype(bf16), do, NN)
            dk = dk + dotf(g, q, NN)
            raw[0, qs, :] = raw[0, qs, :] + dotf(g, k, TN)
            return dk, dv

        zk = jnp.zeros((blk, HEAD), f32)
        carry = unit(kb, (zk, zk), True)
        dk, dv = lax.fori_loop(kb + 1, nb, functools.partial(unit, masked=False), carry)
        dk = (dk * scale).astype(bf16)
        dv = dv.astype(bf16)
        for u in range(2):
            dkv[2 * kb + u, 0] = dk[u * t_loc:(u + 1) * t_loc]
            dkv[2 * kb + u, 1] = dv[u * t_loc:(u + 1) * t_loc]

        @pl.when(kb != z)
        def _():
            for u in range(2):
                kv_send(2 * kb + u).start()

        @pl.when(kb == z)
        def _():
            kv_send(mate).start()

    with scope('bwd'):
        loop(0, nb, bwd_step)
        dq_s[...] = (raw[0] * scale).astype(bf16)
    for e in far:
        q_send(e).start()
    tq[:, cols] = dq_s[rows(me), :]
    tkv[:, :, cols] = dkv[me]

    def flip_o(i):
        dt[:, rows(i)] = o_s[rows(i), :].T

    def flip_v(i):
        dt[:, rows(i)] = dkv[i, 1].T

    def dwo_step(t):
        gy_copy(t).wait()

        @pl.when(t + 1 < nt)
        def _():
            gy_copy(t + 1).start()

        @pl.when(t + 1 == nt)
        def _():
            h_copy(t + 1).start()
        dwo_s[:, ds(t, cw)] = dotf(dt[...], tile[lax.rem(t, 2)], NN)

    def dwv_step(t):
        h_copy(t).wait()

        @pl.when(t + 1 < 2 * nt)
        def _():
            h_copy(t + 1).start()

        @pl.when(t + 1 == 2 * nt)
        def _():
            h2_copy(0).start()
        r = dotf(dt[...], tile[lax.rem(t, 2)], NN)
        for u in range(cw // HEAD):
            bv[(t - nt) * (cw // HEAD) + u] = r[:, u * HEAD:(u + 1) * HEAD].T

    def y_step(t):
        wo_copy(t).wait()

        @pl.when(t + 1 < nt)
        def _():
            wo_copy(t + 1).start()
        cs = ds(t, cw)
        y_s[:, cs] = (x_ref[:, cs].astype(f32) + dotf(att[...], wtile[lax.rem(t, 2)], NN)).astype(bf16)

    def v_send(e):
        to = peer(e)
        return remote(bv.at[to], dwv_out.at[:, cols], s_v.at[e], r_v.at[e], to)

    def out(i):
        src, dst = ((y_s, y_out), (dwo_s, dwo_out), (gx_s, gx_out), (bv.at[me], dwv_out.at[:, cols]),
                    (raw.at[1, rows_f(0, me), :], dwq_out.at[:, cols]), (raw.at[1, rows_f(1, me), :], dwk_out.at[:, cols]))[i]
        return pltpu.make_async_copy(src, dst, s_out.at[i])

    def rows_f(w, to):
        return ds(w * n + to, HEAD)

    with scope('dwo'):
        loop(0, n, flip_o)
        loop(0, nt, dwo_step)
        out(1).start()
    with scope('dwv'):
        loop(0, n, flip_v)
        loop(nt, 2 * nt, dwv_step)
        out(3).start()
    for e in early:
        v_send(e).start()
    with scope('y'):
        for e in range(1, n):
            o_send(e).wait()
        loop(0, nt, y_step)
        out(0).start()

    def w_copies(t):
        slot = lax.rem(t, 2)
        return [pltpu.make_async_copy(w.at[ds(t, wr), :], wrow.at[slot, i], s_x.at[4 + 3 * slot + i]) for i, w in enumerate((wq_ref, wk_ref, wv_ref))]

    for cp in w_copies(0):
        cp.start()
    with scope('waitkv'):
        for e in range(1, n):
            kv_send(peer(e)).wait()
    with scope('waitq'):
        for e in range(1, n):
            q_send(e).wait()

    cl = cl_s[...]
    sl = sl_s[...]

    def back_rope(a):
        a = a.astype(f32)
        return a * cl + pltpu.roll(a, half, 1) * sl

    def mean_step(i, carry):
        a, b = carry
        a = a + back_rope(tq[:, hs(i)]) * g_ref[0:1, hs(i)] * qkl[0, :, hs(i)]
        b = b + back_rope(tkv[0, :, hs(i)]) * g_ref[1:2, hs(i)] * qkl[1, :, hs(i)]
        return a, b

    def m_send(e):
        return remote(mine2, mall.at[me], s_m.at[e], r_m.at[e], peer(e))

    with scope('mean'):
        a, b = lax.fori_loop(0, nd, mean_step, (zero, zero))
        mq = jnp.sum(a, axis=1, keepdims=True) * inv[0] * (1.0 / d)
        mk = jnp.sum(b, axis=1, keepdims=True) * inv[1] * (1.0 / d)
        mine2[0:1, :] = mq.T[0:1, :]
        mine2[1:2, :] = mk.T[0:1, :]
    for e in range(1, n):
        m_send(e).start()
    for e in far:
        if e not in early:
            v_send(e).start()
    mall[me] = mine2[...]

    def loc_step(i):
        tq[:, hs(i)] = (inv[0] * (back_rope(tq[:, hs(i)]) * g_ref[0:1, hs(i)] - qkl[0, :, hs(i)] * inv[0] * mq)).astype(bf16)
        tkv[0, :, hs(i)] = (inv[1] * (back_rope(tkv[0, :, hs(i)]) * g_ref[1:2, hs(i)] - qkl[1, :, hs(i)] * inv[1] * mk)).astype(bf16)

    with scope('mwait'):
        for e in range(1, n):
            m_send(e).wait()

    gcol = [g_ref[w:w + 1, cols] for w in range(2)]
    gcol = [spread_col(g)[:, 0:1] for g in gcol]

    def head_step(j, carry):
        js = rows(j)
        ct = csT[0, :, js]
        sn = csT[1, :, js]
        res = []
        for w, src in enumerate((dq_s[js, :], dkv[j, 0])):
            t = src.astype(f32).T
            p, r = t[:half], t[half:]
            t = jnp.concatenate([p * ct + r * sn, r * ct - p * sn], axis=0)
            hat = hatT[w, :, js]
            res.append(carry[w] + t * hat)
            rawT[w * HEAD:(w + 1) * HEAD, js] = (sall[j, w:w + 1, :] * (t * gcol[w] - hat * mall[j, w:w + 1, :])).astype(bf16)
        return tuple(res)

    with scope('head'):
        zt = jnp.zeros((HEAD, t_loc), f32)
        sums = lax.fori_loop(0, n, head_step, (zt, zt))
        for w in range(2):
            gg_ref[w] = jnp.broadcast_to(jnp.sum(sums[w], axis=1, keepdims=True), (HEAD, HEAD)).T[0:8, :]

    def a_send(to):
        e = lax.rem(to + n - me, n)
        return remote(raw.at[1, rows_f(0, to), :], dwq_out.at[:, cols], s_a.at[e], r_a.at[e], to)

    def b_send(to):
        e = lax.rem(to + n - me, n)
        return remote(raw.at[1, rows_f(1, to), :], dwk_out.at[:, cols], s_b.at[e], r_b.at[e], to)

    def dw_step(t):
        h2_copy(t).wait()

        @pl.when(t + 1 < nt)
        def _():
            h2_copy(t + 1).start()
        nn = chip(t)
        r = dotf(rawT[...], tile[lax.rem(t, 2)], NN)
        for u in range(cw // HEAD):
            to = nn * (cw // HEAD) + u
            for w in range(2):
                raw[1, rows_f(w, to), :] = r[w * HEAD:(w + 1) * HEAD, u * HEAD:(u + 1) * HEAD].T

            @pl.when(to != me)
            def _():
                a_send(to).start()
                b_send(to).start()

    with scope('dw'):
        loop(0, nt, dw_step)
    out(4).start()
    out(5).start()
    with scope('loc'):
        loop(0, nd, loc_step)

    def dh_step(t):
        for cp in w_copies(t):
            cp.wait()

        @pl.when(t + 1 < nw)
        def _():
            for cp in w_copies(t + 1):
                cp.start()
        slot = lax.rem(t, 2)
        r = dotf(tq[...], wrow[slot, 0], NT) + dotf(tkv[0], wrow[slot, 1], NT) + dotf(tkv[1], wrow[slot, 2], NT)
        dh[:, ds(t, wr)] = r.astype(bf16).astype(f32)

    with scope('dh'):
        loop(0, nw, dh_step)

    def mx_step(i, acc):
        return acc + dh[:, hs(i)] * g_ref[2:3, hs(i)] * x_ref[:, hs(i)].astype(f32)

    def g_send(e):
        return remote(gpart.at[peer(e)], gall.at[me], s_g.at[e], r_g.at[e], peer(e))

    with scope('gx'):
        mx = jnp.sum(lax.fori_loop(0, nd, mx_step, zero), axis=1, keepdims=True) * x_inv * (1.0 / d)

        def gx_step(i):
            xh = x_ref[:, hs(i)].astype(f32) * x_inv
            dhh = dh[:, hs(i)]
            gpart[i] = jnp.broadcast_to(jnp.sum(dhh * xh, axis=0, keepdims=True), (8, HEAD))
            gx_s[:, hs(i)] = (gy_ref[:, hs(i)].astype(f32) + x_inv * (dhh * g_ref[2:3, hs(i)] - xh * mx)).astype(bf16)

        loop(0, nd, gx_step)
        out(2).start()
    with scope('end_v'):
        for e in range(1, n):
            g_send(e).start()
        gall[me] = gpart[me]
        for e in range(1, n):
            v_send(e).wait()
    with scope('end_g'):
        for e in range(1, n):
            g_send(e).wait()
        gn_ref[...] = jnp.sum(gall[...], axis=0)

        def drain(i):
            s = i // 2
            u = lax.rem(i, 2)
            for a in range(2):
                for direction in range(2):
                    ring(a, direction, s, u).wait_send()
                    par(a, direction, s, u).wait_send()

        loop(0, ticks, drain)
        for a in range(2):
            own_par(a).wait_send()
        for i in range(6):
            out(i).wait()
    with scope('end_ab'):
        for e in range(1, n):
            a_send(peer(e)).wait()
            b_send(peer(e)).wait()


def block(n, x, gy, pos, gains, freq, wq, wk, wv, wo):
    t_loc, d = x.shape
    t_all = t_loc * n
    vm = pl.BlockSpec(memory_space=pltpu.VMEM)
    hb = pl.BlockSpec(memory_space=pl.ANY)
    S = jax.ShapeDtypeStruct
    V = pltpu.VMEM
    sem = pltpu.SemaphoreType.DMA
    hd = (t_all, HEAD)
    tok = (t_loc, d)
    nz = n // 2
    return pl.pallas_call(functools.partial(block_kernel, n),
        in_specs=[hb] * 2 + [vm] * 3 + [hb] * 4,
        out_specs=[hb, hb, vm, hb, hb, hb, hb, vm, hb, hb],
        out_shape=[S(tok, bf16), S(tok, bf16), S((8, d // n), f32)] + [S((d // n, d), f32)] * 4 + [S((2, 8, HEAD), f32), S((t_all, d), bf16), S((t_all, d), bf16)],
        scratch_shapes=[V(tok, bf16), V(tok, bf16), V(tok, bf16), V((d, 3 * HEAD), bf16), V((HEAD, d), bf16), V((3,) + hd, f32), V((2,) + tok, bf16), V((2, d, 2 * HEAD), bf16), V((2, t_all, 2 * HEAD), bf16), V((2, 3, 2 * HEAD, d), bf16),
            V((2,) + tok, f32), V((2, HEAD, t_all), f32), V((2, HEAD // 2, t_all), f32)] + [V(hd, bf16)] * 5 + [V((8, t_all), f32)] * 2
        + [V(hd, bf16), V((n, 2, t_loc, HEAD), bf16), V(tok, bf16), V((2,) + tok, bf16), V(tok, bf16), V((HEAD, t_all), bf16), V((n, d // n, HEAD), f32), V((2 * HEAD, t_all), bf16), V(tok, bf16), V((HEAD, d), f32), V(tok, bf16), V(tok, f32),
            V((2, t_loc, HEAD), f32), V((t_loc, HEAD), f32), V((t_loc, HEAD), f32), V((2, t_loc, HEAD), f32), V((8, t_loc), f32), V((n, 8, t_loc), f32), V((8, t_loc), f32), V((n, 8, t_loc), f32), V((n, 8, d // n), f32), V((n, 8, d // n), f32)]
        + [sem((2, 2, nz - 1, 2))] * 4 + [sem((2,))] * 2 + [sem((n,))] * 18
        + [sem((2, 4)), sem((2,)), sem((2,)), sem((10,)), sem((2,)), sem((6,))],
        compiler_params=pltpu.CompilerParams(collective_id=1, has_side_effects=True, vmem_limit_bytes=67043328), name='block')(x, gy, pos, gains, freq, wq, wk, wv, wo)


def copy_kernel(*refs):
    k = (len(refs) - 1) // 3
    src, dst, buf, si, so = list(refs[:k - 1]), refs[k - 1:2 * k - 1], refs[2 * k - 1:3 * k - 1], refs[-2], refs[-1]
    src[k - 3:] = [src[k - 3].at[0:1, :], src[k - 2].at[0, 0:1, :], src[k - 2].at[1, 0:1, :]]
    ins = [pltpu.make_async_copy(src[i], buf[i], si.at[i]) for i in range(k)]
    outs = [pltpu.make_async_copy(buf[i], dst[i], so.at[i]) for i in range(k)]
    for cp in ins:
        cp.start()
    for i in range(k):
        ins[i].wait()
        outs[i].start()
    for cp in outs:
        cp.wait()


def copy_out(arrays):
    hb = pl.BlockSpec(memory_space=pl.ANY)
    shapes = [(a.shape, a.dtype) for a in arrays[:-2]] + [((1, HEAD), f32)] * 3
    k = len(shapes)
    return pl.pallas_call(copy_kernel, in_specs=[hb] * len(arrays), out_specs=[hb] * k, out_shape=[jax.ShapeDtypeStruct(*a) for a in shapes],
        scratch_shapes=[pltpu.VMEM(*a) for a in shapes] + [pltpu.SemaphoreType.DMA((k,))] * 2, name='copy_out')(*arrays)


def solution(mesh):
    n = mesh.shape['sp']

    def device_step(x_in, grad_y, positions, g_norm, wq, wk, wv, wo, gq, gk):
        gains = jnp.concatenate([gq, gk, g_norm]).astype(f32).reshape(3, -1)
        half = HEAD // 2
        inv_freq = ROPE_BASE ** (-np.arange(half) * (2.0 / HEAD))
        freq = jnp.asarray(np.tile(inv_freq, (8, 2)), f32)
        y, gx, gn, dwq, dwk, dwv, dwo, gg, _, _ = block(n, x_in[0], grad_y[0], positions, gains, freq, wq, wk, wv, wo)
        y, gx, dwq, dwk, dwv, dwo, gn, ggq, ggk = copy_out([y, gx, dwq, dwk, dwv, dwo, gn, gg])
        return (y[None], gx[None], gn[0], dwq, dwk, dwv, dwo, ggq[0], ggk[0])

    seq_spec = P('dp', 'sp', None)
    rep2, rep1 = P(None, None), P(None)
    row_spec, vec_spec = P(('dp', 'sp'), None), P(('dp', 'sp'))
    return jax.shard_map(device_step, mesh=mesh, in_specs=(seq_spec, seq_spec, P('dp', 'sp'), rep1, rep2, rep2, rep2, rep2, rep1, rep1), out_specs=(seq_spec, seq_spec, vec_spec, row_spec, row_spec, row_spec, row_spec, vec_spec, vec_spec), check_vma=False)
```

time: 1240 us -> 357 us (0.29)
  matrix products: 490 us -> 0 us
  Pallas kernels: 0 us -> 353 us
  waiting for transfers between devices: 268 us -> 0 us
  other arithmetic: 154 us -> 0.72 us
  local copies, waits for them, and re-layouts: 138 us -> 0.63 us
  blocking collectives: 118 us -> 0 us
  starting transfers between devices: 39.7 us -> 0 us
  between operations: 15.2 us -> 0.81 us
    dot_general x236 -> x0, matrix products: 490 us -> none  [the longest x32 122 us: block_step(): jnp.einsum('bhqk,bqhd->bkhd', ds_bf, q_blk, preferred_element_type=jnp.fl...]
    pallas_call x0 -> x2, Pallas kernels: none -> 353 us  [the longest x1 347 us: block(): pl.pallas_call(functools.partial(block_kernel, n), in_specs=[hb] * 2 + [v...]
    reduce_scatter x4 -> x0, waiting for transfers between devices: 181 us -> none  [sum_rows(): return lax.psum_scatter(partial_sum, 'sp', scatter_dimension=0, tiled=True)]
    unnamed x10 -> x0, other arithmetic: 93 us -> none
    all_to_all x6 -> x0, waiting for transfers between devices: 86.5 us -> none  [the longest x1 26.1 us: device_step(): q_all = to_heads(q_loc)]
    while x194 -> x0, local copies, waits for them, and re-layouts: 79.6 us -> none
    all_to_all x2 -> x0, blocking collectives: 74.8 us -> none  [the longest x1 37.5 us: device_step(): d_v = to_tokens(dv_acc.astype(jnp.bfloat16))]
    unnamed x1 -> x0, blocking collectives: 43.4 us -> none
  transfers between devices with their start and end apart: 10 -> 0, of which waited for: 6 -> 0; matrix products, arithmetic and copies ran while one was open for 24% -> 0% of each run, Pallas kernels for 0% -> 0%
where the time goes in v3:
time: 357 us; the launch traced here: 355 us
  Pallas kernels  353 us (99%)
    pallas_call x1, Pallas kernels, block(): pl.pallas_call(functools.partial(block_kernel, n), in_specs=[hb] * 2 + [v...  347 us

profile of v3, /device:TPU:21, one launch (start us, length us, event | category | flops | bytes accessed | tf_op | source)
XLA Modules:
  0.0 354.8 jit_solution(5564382851612769737)
XLA Ops:
  0.6 0.7 maximum_convert_fusion
  1.4 0.6 reshape.22.g_ref
  2.0 347.1 %block.1 = (bf16[256,2048]{1,0:T(8,128)(2,1)}, bf16[256,2048]{1,0:T(8,128)(2,1)}, f32[8,128]{1,0:T(8,128)}, f32[128,2048]{1,0:T(8,128)}, f32[128,2048]{1,0:T(8,1...) custom-call(bf16[256,2048]{1,0:T(8,128)(2,1)} %bitcast.7, ...), custom_call_target="tpu_custom_call" | custom-call | tf_op jit(solution)/shard_map/block/pallas_call | solution.py:720
  349.1 5.5 %copy_out.1 = (bf16[256,2048]{1,0:T(8,128)(2,1)}, bf16[256,2048]{1,0:T(8,128)(2,1)}, f32[128,2048]{1,0:T(8,128)}, f32[128,2048]{1,0:T(8,128)}, f32[128,2048]{1,0...) custom-call(bf16[256,2048]{1,0:T(8,128)(2,1)} %get-tuple-element.26.refs_0_, ...), custom_call_target="tpu_custom_call" | custom-call | tf_op jit(solution)/shard_map/copy_out/pallas_call | solution.py:752

commit v4 on v3

v4 whole, which is shorter than its diff:
```python
import contextlib
import functools
import jax
import jax.numpy as jnp
import numpy as np
from jax import lax
from jax.experimental import pallas as pl
from jax.experimental.pallas import tpu as pltpu
from jax.sharding import PartitionSpec as P

HEAD = 128
NORM_EPS = 1e-5
ROPE_BASE = 10000.0
LOG2E = 1.4426950408889634
f32 = jnp.float32
bf16 = jnp.bfloat16
MESH = pl.DeviceIdType.MESH
NN = (((1,), (0,)), ((), ()))
NT = (((1,), (1,)), ((), ()))
TN = (((0,), (0,)), ((), ()))
PROF = 0
scope = jax.named_scope if PROF else (lambda name: contextlib.nullcontext())


def dotf(a, b, dims):
    return lax.dot_general(a, b, dims, preferred_element_type=f32)


def remote(src, dst, ss, rs, to):
    return pltpu.make_async_remote_copy(src_ref=src, dst_ref=dst, send_sem=ss, recv_sem=rs, device_id={'sp': to}, device_id_type=MESH)


def ds(i, size):
    return pl.ds(pl.multiple_of(i * size, size), size)


def settle(ref, *sems):
    for sem in sems:
        pltpu.make_async_copy(ref, ref, sem).wait()


def as_row(col):
    return jnp.broadcast_to(col, (col.shape[0], HEAD)).T[0:1, :]


def loop(lo, hi, body):
    def step(i, carry):
        body(i)
        return carry
    lax.fori_loop(lo, hi, step, 0)


def block_kernel(n, x_hbm, gy_hbm, pos_ref, gq_ref, gk_ref, gn1_ref, fr_ref, wq_ref, wk_ref, wv_ref, wo_ref,
                 y_out, gx_out, gall, dwq_out, dwk_out, dwv_out, dwo_out, gg_out, h_all, gy_all,
                 x_ref, gy_ref, g_ref, hid, wh, woh, raw, xbuf, wtile, tile, wrow, qkl, hatT, csT, q_s, k_s, v_s, do_s, o_s, lse, dl,
                 dq_s, dkv, tq, tkv, att, dt, bv, rawT, y_s, dwo_s, gx_s, dh, ssq, cl_s, sl_s, inv, xinv, mine, sall, mine2, mall, pm, pall, gpart, gg_s,
                 s_ring, r_ring, s_par, r_par, r_own, s_st, r_st, s_o, r_o, s_kv, r_kv, s_q, r_q, s_v, r_v, s_a, r_a, s_b, r_b, s_m, r_m, s_g, r_g, s_p, r_p,
                 s_ld, s_t, s_w, s_x, s_wr, s_loc, s_out):
    me = lax.axis_index('sp')
    t_loc, d = x_hbm.shape
    t_all = t_loc * n
    z = me // 2
    c = lax.rem(me, 2)
    nz = n // 2
    mate = me + 1 - 2 * c
    up = lax.rem(z + 1, nz) * 2 + c
    down = lax.rem(z + nz - 1, nz) * 2 + c
    nd = d // HEAD
    half = HEAD // 2
    sub = t_loc // 4
    last = nz - 2
    ticks = 2 * (nz - 1)
    blk = 2 * t_loc
    nb = t_all // blk
    cexp = HEAD ** -0.5 * LOG2E
    scale = HEAD ** -0.5
    cw = tile.shape[2]
    nt = d // cw
    wr = wrow.shape[2]
    nw = d // wr
    cols = ds(me, HEAD)
    far = sorted(range(1, n), key=lambda e: -min(e, n - e))
    alls = (h_all, gy_all)
    own_src = (hid, gy_ref)

    def peer(e):
        return lax.rem(me + e, n)

    def rows(i):
        return ds(i, t_loc)

    def hs(i):
        return ds(i, HEAD)

    def chip(s):
        k = nz // 2 - (s + 1) // 2
        return lax.rem(z + nz + jnp.where(lax.rem(s, 2) == 0, -k, k), nz)

    def piece(core, direction, s, u):
        bz = lax.rem(z + nz - 1 - s, nz) if direction == 0 else lax.rem(z + 1 + s, nz)
        return ds((bz * 2 + core) * 4 + 2 * direction + u, sub)

    def ring(a, direction, s, u):
        ref = alls[a]
        bz = lax.rem(z + nz - s, nz) if direction == 0 else lax.rem(z + s, nz)
        rs = ds((bz * 2 + c) * 4 + 2 * direction + u, sub)
        return remote(ref.at[rs, :], ref.at[rs, :], s_ring.at[a], r_ring.at[a, direction, s, u], up if direction == 0 else down)

    def ring0(a, direction, u):
        rs = ds(me * 4 + 2 * direction + u, sub)
        return remote(own_src[a].at[pl.ds((2 * direction + u) * sub, sub), :], alls[a].at[rs, :], s_ring.at[a], r_ring.at[a, direction, 0, u], up if direction == 0 else down)

    def par(a, direction, s, u):
        rs = piece(c, direction, s, u)
        return remote(alls[a].at[rs, :], alls[a].at[rs, :], s_par.at[a], r_par.at[a, 2 * s + u], mate)

    def own_par(a):
        return remote(own_src[a], alls[a].at[rows(me), :], s_par.at[a], r_own.at[a], mate)

    def own_loc(a):
        return pltpu.make_async_copy(own_src[a], alls[a].at[rows(me), :], s_loc.at[0])

    def comm(a, t):
        s = t // 2
        u = lax.rem(t, 2)
        for direction in range(2):
            ring(a, direction, s, u).wait_recv()

            @pl.when(s < last)
            def _():
                ring(a, direction, s + 1, u).start()
            par(a, direction, s, u).start()

    def loads(a, t):
        s = t // 2
        u = lax.rem(t, 2)
        slot = lax.rem(t, 2)
        out = []
        for i, (core, direction) in enumerate(((c, 0), (c, 1), (1 - c, 0), (1 - c, 1))):
            out.append(pltpu.make_async_copy(alls[a].at[piece(core, direction, s, u), :], xbuf.at[slot, pl.ds(i * sub, sub), :], s_ld.at[slot]))
        return out

    def mate_load(a):
        return pltpu.make_async_copy(alls[a].at[rows(mate), :], xbuf.at[1], s_ld.at[1])

    def spots(t):
        s = t // 2
        u = lax.rem(t, 2)
        return [piece(c, 0, s, u), piece(c, 1, s, u), piece(1 - c, 0, s, u), piece(1 - c, 1, s, u)]

    def gather(a, t, work, put):
        @pl.when(t < ticks)
        def _():
            with scope('comm'):
                comm(a, t)

        @pl.when(t == 0)
        def _():
            own_par(a).wait_recv()
            mate_load(a).start()
            put(work(own_src[a][...]), [rows(me)])

        @pl.when(t == 1)
        def _():
            mate_load(a).wait()
            put(work(xbuf[1]), [rows(mate)])

        @pl.when(t >= 2)
        def _():
            settle(xbuf.at[lax.rem(t, 2)], s_ld.at[lax.rem(t, 2)])
            put(work(xbuf[lax.rem(t, 2)]), spots(t - 2))

        @pl.when((t >= 1) & (t < ticks + 1))
        def _():
            settle(alls[a].at[pl.ds(0, 2 * sub), :], r_par.at[a, t - 1])
            for cp in loads(a, t - 1):
                cp.start()

    def stat_tile(i, act):
        slot = lax.rem(i, 2)
        cs = ds(lax.rem(i, nt), cw)

        @pl.when(i < nt)
        def _():
            act(pltpu.make_async_copy(wq_ref.at[:, cs], wtile.at[slot], s_w.at[slot]))

        @pl.when(i >= nt)
        def _():
            act(pltpu.make_async_copy(wk_ref.at[:, cs], wtile.at[slot], s_w.at[slot]))

    def start(cp):
        cp.start()

    def wait(cp):
        cp.wait()

    def stat_step(i):
        stat_tile(i, wait)

        @pl.when(i + 1 < 2 * nt)
        def _():
            stat_tile(i + 1, start)
        r = dotf(hid[...], wtile[lax.rem(i, 2)], NN)
        w = i // nt
        qkl[w, :, ds(lax.rem(i, nt), cw)] = r
        acc = r[:, :HEAD] * r[:, :HEAD]
        for j in range(1, cw // HEAD):
            acc = acc + r[:, j * HEAD:(j + 1) * HEAD] * r[:, j * HEAD:(j + 1) * HEAD]
        ssq[w] = ssq[w] + acc

    def st_send(e):
        return remote(mine.at[pl.ds(0, 3)], sall.at[me, pl.ds(0, 3)], s_st.at[0], r_st.at[0], peer(e))

    sgn = jnp.where(lax.broadcasted_iota(jnp.int32, (1, HEAD), 1) < half, -1.0, 1.0).astype(f32)

    def stat_done():
        for w in range(2):
            iv = lax.rsqrt(jnp.sum(ssq[w], axis=1, keepdims=True) * (1.0 / d) + NORM_EPS)
            inv[w] = jnp.broadcast_to(iv, (t_loc, HEAD))
            mine[w:w + 1, :] = as_row(iv)
        mine[2:3, :] = pos_ref[...].astype(f32)
        for e in range(1, n):
            st_send(e).start()
        sall[me, 0:3, :] = mine[0:3, :]
        ang = spread_col(pos_ref[...].astype(f32)) * fr_ref[0:1, :]
        cl_s[...] = jnp.cos(ang)
        sl_s[...] = jnp.sin(ang) * (-sgn)

    def spread_col(row):
        return jnp.broadcast_to(row, (HEAD, row.shape[1])).T

    def head_w(i):
        w = (wq_ref, wk_ref, wv_ref)[i]
        return pltpu.make_async_copy(w.at[:, cols], wh.at[:, pl.ds(i * HEAD, HEAD)], s_x.at[0])

    def wo_load():
        return pltpu.make_async_copy(wo_ref.at[cols, :], woh, s_x.at[1])

    with scope('begin'):
        barrier = pltpu.get_barrier_semaphore()
        for e in range(1, n):
            pl.semaphore_signal(barrier, inc=1, device_id={'sp': peer(e)}, device_id_type=MESH)
        def x_piece(p):
            rs = pl.ds(p * sub, sub)
            return pltpu.make_async_copy(x_hbm.at[rs, :], x_ref.at[rs, :], s_x.at[2 + p])

        gy_load = pltpu.make_async_copy(gy_hbm, gy_ref, s_x.at[6])
        for p in (0, 2, 1, 3):
            x_piece(p).start()
        gy_load.start()
        for i in range(3):
            head_w(i).start()
        wo_load().start()
        stat_tile(0, start)
        for w, src in enumerate((gq_ref, gk_ref, gn1_ref)):
            g_ref[w:w + 1, :] = src[...].astype(f32).reshape(1, d)
        def norm_piece(p):
            rs = pl.ds(p * sub, sub)
            x_piece(p).wait()

            def sq_step(i, acc):
                xf = x_ref[rs, hs(i)].astype(f32)
                return acc + xf * xf

            acc = lax.fori_loop(0, nd, sq_step, jnp.zeros((sub, HEAD), f32))
            xi = lax.rsqrt(jnp.sum(acc, axis=1, keepdims=True) * (1.0 / d) + NORM_EPS)
            xinv[rs, :] = jnp.broadcast_to(xi, (sub, HEAD))

            def hid_step(i):
                hid[rs, hs(i)] = (x_ref[rs, hs(i)].astype(f32) * xi * g_ref[2:3, hs(i)]).astype(bf16)

            loop(0, nd, hid_step)

        norm_piece(0)
        norm_piece(2)
        pl.semaphore_wait(barrier, n - 1)
        ring0(0, 0, 0).start()
        ring0(0, 1, 0).start()
        norm_piece(1)
        ring0(0, 0, 1).start()
        norm_piece(3)
        ring0(0, 1, 1).start()
        zero = jnp.zeros((t_loc, HEAD), f32)
        ssq[...] = jnp.zeros_like(ssq)
        gy_load.wait()
        own_loc(1).start()
    own_par(0).start()
    own_par(1).start()
    own_loc(0).start()
    settle(wh, s_x.at[0])
    wo_load().wait()

    hb = t_loc // 2

    def finish(s):
        for direction in range(2):
            bz = lax.rem(z + nz - 1 - s, nz) if direction == 0 else lax.rem(z + 1 + s, nz)

            def one(core):
                b = bz * 2 + core
                rs = ds(b * 2 + direction, hb)
                st = sall[b, 0:3, direction * hb:(direction + 1) * hb]
                ang = spread_col(st[2:3, :]) * fr_ref[0:1, :]
                co = jnp.cos(ang)
                si = jnp.sin(ang)
                csT[0, :, rs] = co.T[:half, :]
                csT[1, :, rs] = si.T[:half, :]
                si = si * sgn
                for w, dst in enumerate((q_s, k_s)):
                    hat = raw[w, rs, :] * spread_col(st[w:w + 1, :])
                    hatT[w, :, rs] = hat.T
                    hat = hat * g_ref[w:w + 1, cols]
                    dst[rs, :] = (hat * co + pltpu.roll(hat, half, 1) * si).astype(bf16)
                v_s[rs, :] = raw[2, rs, :].astype(bf16)

            loop(0, 2, one)

    def qkv_work(xv):
        return dotf(xv, wh[...], NN)

    def qkv_put(r, where):
        step = r.shape[0] // len(where)
        for i, rs in enumerate(where):
            for w in range(3):
                raw[w, rs, :] = r[i * step:(i + 1) * step, w * HEAD:(w + 1) * HEAD]

    spt = 2 * nt // 4

    def x_tick(t):
        gather(0, t, qkv_work, qkv_put)

        @pl.when(t == 2 * last - 1)
        def _():
            for u in range(2):
                for direction in range(2):
                    ring0(1, direction, u).start()

        @pl.when(t < 4)
        def _():
            with scope('stat'):
                loop(t * spt, (t + 1) * spt, stat_step)

        @pl.when(t == 4)
        def _():
            with scope('statdone'):
                stat_done()

        @pl.when(t == 6)
        def _():
            settle(sall.at[pl.ds(0, n - 1), pl.ds(0, 3)], s_st.at[0], r_st.at[0])

        @pl.when(((t >= 6) & (t <= 11)) | (t == 13))
        def _():
            with scope('finish'):
                finish(jnp.where(t == 13, last - 1, t - 7))

    with scope('gather_x'):
        loop(0, ticks + 2, x_tick)

    def attend(j):
        qs = ds(j, blk)
        q = q_s[qs, :]

        def unit(kb, carry, masked):
            m, l, acc = carry
            ks = ds(kb, blk)
            s = dotf(q, k_s[ks, :], NT)
            if masked:
                r = lax.broadcasted_iota(jnp.int32, (blk, blk), 0)
                cc = lax.broadcasted_iota(jnp.int32, (blk, blk), 1)
                s = jnp.where(r >= cc, s, -1e30)
            mn = jnp.maximum(m, jnp.max(s, axis=1, keepdims=True))
            al = jnp.exp2((m - mn) * cexp)
            p = jnp.exp2((s - mn) * cexp)
            l = l * al + jnp.sum(p, axis=1, keepdims=True)
            acc = acc * al + dotf(p.astype(bf16), v_s[ks, :], NN)
            return mn, l, acc

        init = (jnp.full((blk, 1), -1e30, f32), jnp.zeros((blk, 1), f32), jnp.zeros((blk, HEAD), f32))
        carry = lax.fori_loop(0, j, functools.partial(unit, masked=False), init)
        m, l, acc = unit(j, carry, True)
        o = acc / l
        raw[2, qs, :] = o
        o_s[qs, :] = o.astype(bf16)
        lse[0:1, qs] = as_row(m * cexp + jnp.log2(l))

    def o_send(e):
        to = peer(e)
        return remote(o_s.at[rows(to), :], att.at[:, cols], s_o.at[0], r_o.at[0], to)

    def do_work(xv):
        return dotf(xv, woh[...], NT).astype(bf16)

    def do_put(r, where):
        step = r.shape[0] // len(where)
        for i, rs in enumerate(where):
            do_s[rs, :] = r[i * step:(i + 1) * step]

    def y_tick(t):
        gather(1, t, do_work, do_put)

        @pl.when(t == 0)
        def _():
            with scope('finish'):
                finish(last)
        lo = jnp.where(t == 0, 0, jnp.where(t <= 4, t + 1, jnp.where(t <= 6, 6, 7)))
        hi = jnp.where(t == 0, 2, jnp.where(t <= 4, t + 2, jnp.where(t == 5, 6, jnp.where(t == 8, 8, 7))))
        with scope('attend'):
            loop(lo, hi, attend)

        @pl.when(t == ticks - 2)
        def _():
            for e in far:
                o_send(e).start()

    with scope('gather_y'):
        loop(0, ticks + 2, y_tick)

    def gy_copy(t):
        return pltpu.make_async_copy(gy_all.at[:, ds(t, cw)], tile.at[lax.rem(t, 2)], s_t.at[lax.rem(t, 2)])

    def h_copy(t):
        return pltpu.make_async_copy(h_all.at[:, ds(lax.rem(t, nt), cw)], tile.at[lax.rem(t, 2)], s_t.at[lax.rem(t, 2)])

    def h2_copy(t):
        return pltpu.make_async_copy(h_all.at[:, ds(chip(t), cw)], tile.at[lax.rem(t, 2)], s_t.at[lax.rem(t, 2)])

    def wo_copy(t):
        return pltpu.make_async_copy(wo_ref.at[:, ds(t, cw)], wtile.at[lax.rem(t, 2)], s_w.at[lax.rem(t, 2)])

    def q_send(e):
        to = peer(e)
        return remote(dq_s.at[rows(to), :], tq.at[:, cols], s_q.at[0], r_q.at[0], to)

    def kv_send(to):
        return remote(dkv.at[to], tkv.at[:, :, cols], s_kv.at[0], r_kv.at[0], to)

    settle(h_all.at[pl.ds(0, 2 * t_loc), :], s_loc.at[0])
    gy_copy(0).start()
    wo_copy(0).start()
    att[:, cols] = o_s[rows(me), :]
    raw[0] = jnp.zeros((t_all, HEAD), f32)

    def delta(j):
        qs = ds(j, blk)
        dl[0:1, qs] = as_row(jnp.sum(raw[2, qs, :] * do_s[qs, :].astype(f32), axis=1, keepdims=True))

    with scope('delta'):
        loop(0, nb, delta)

    def bwd_step(s):
        kb = chip(s)
        ks = ds(kb, blk)
        k = k_s[ks, :]
        v = v_s[ks, :]

        def unit(qb, carry, masked):
            dk, dv = carry
            qs = ds(qb, blk)
            q = q_s[qs, :]
            do = do_s[qs, :]
            p = jnp.exp2(dotf(k, q, NT) * cexp - lse[0:1, qs])
            if masked:
                r = lax.broadcasted_iota(jnp.int32, (blk, blk), 0)
                cc = lax.broadcasted_iota(jnp.int32, (blk, blk), 1)
                p = jnp.where(cc >= r, p, 0.0)
            g = (p * (dotf(v, do, NT) - dl[0:1, qs])).astype(bf16)
            dv = dv + dotf(p.astype(bf16), do, NN)
            dk = dk + dotf(g, q, NN)
            raw[0, qs, :] = raw[0, qs, :] + dotf(g, k, TN)
            return dk, dv

        zk = jnp.zeros((blk, HEAD), f32)
        carry = unit(kb, (zk, zk), True)
        dk, dv = lax.fori_loop(kb + 1, nb, functools.partial(unit, masked=False), carry)
        dk = (dk * scale).astype(bf16)
        dv = dv.astype(bf16)
        for u in range(2):
            dkv[2 * kb + u, 0] = dk[u * t_loc:(u + 1) * t_loc]
            dkv[2 * kb + u, 1] = dv[u * t_loc:(u + 1) * t_loc]

        @pl.when(kb != z)
        def _():
            for u in range(2):
                kv_send(2 * kb + u).start()

        @pl.when(kb == z)
        def _():
            kv_send(mate).start()

    with scope('bwd'):
        loop(0, nb, bwd_step)
        dq_s[...] = (raw[0] * scale).astype(bf16)
    gcol = [spread_col(g_ref[w:w + 1, cols])[:, 0:1] for w in range(2)]

    def unroped(src, js):
        ct = csT[0, :, js]
        sn = csT[1, :, js]
        t = src.astype(f32).T
        p, r = t[:half], t[half:]
        return jnp.concatenate([p * ct + r * sn, r * ct - p * sn], axis=0)

    def share_step(j, carry):
        js = rows(j)
        res = []
        for w, src in enumerate((dq_s[js, :], dkv[j, 0])):
            th = unroped(src, js) * hatT[w, :, js]
            res.append(carry[w] + th)
            pm[j, w:w + 1, :] = jnp.sum(th * gcol[w], axis=0, keepdims=True)
        return tuple(res)

    def p_send(e):
        to = peer(e)
        return remote(pm.at[to, pl.ds(0, 2)], pall.at[me, pl.ds(0, 2)], s_p.at[0], r_p.at[0], to)

    with scope('share'):
        zt = jnp.zeros((HEAD, t_loc), f32)
        sums = lax.fori_loop(0, n, share_step, (zt, zt))
    for e in far:
        p_send(e).start()
    for e in far:
        q_send(e).start()
    pall[me, 0:2, :] = pm[me, 0:2, :]
    for w in range(2):
        gg_s[w] = jnp.broadcast_to(jnp.sum(sums[w], axis=1, keepdims=True), (HEAD, HEAD)).T[0:8, :]
    tq[:, cols] = dq_s[rows(me), :]
    tkv[:, :, cols] = dkv[me]

    def flip_o(i):
        dt[:, rows(i)] = o_s[rows(i), :].T

    def flip_v(i):
        dt[:, rows(i)] = dkv[i, 1].T

    def dwo_step(t):
        gy_copy(t).wait()

        @pl.when(t + 1 < nt)
        def _():
            gy_copy(t + 1).start()

        @pl.when(t + 1 == nt)
        def _():
            h_copy(t + 1).start()
        dwo_s[:, ds(t, cw)] = dotf(dt[...], tile[lax.rem(t, 2)], NN)

    def dwv_step(t):
        h_copy(t).wait()

        @pl.when(t + 1 < 2 * nt)
        def _():
            h_copy(t + 1).start()

        @pl.when(t + 1 == 2 * nt)
        def _():
            h2_copy(0).start()
        r = dotf(dt[...], tile[lax.rem(t, 2)], NN)
        for u in range(cw // HEAD):
            bv[(t - nt) * (cw // HEAD) + u] = r[:, u * HEAD:(u + 1) * HEAD].T

    def y_step(t):
        wo_copy(t).wait()

        @pl.when(t + 1 < nt)
        def _():
            wo_copy(t + 1).start()
        cs = ds(t, cw)
        y_s[:, cs] = (x_ref[:, cs].astype(f32) + dotf(att[...], wtile[lax.rem(t, 2)], NN)).astype(bf16)

    def v_send(e):
        to = peer(e)
        return remote(bv.at[to], dwv_out.at[:, cols], s_v.at[0], r_v.at[0], to)

    def out(i):
        src, dst, k = ((y_s, y_out, 0), (dwo_s, dwo_out, 1), (gx_s, gx_out, 0), (bv.at[me], dwv_out.at[:, cols], 2),
                       (raw.at[1, rows_f(0, me), :], dwq_out.at[:, cols], 2), (raw.at[1, rows_f(1, me), :], dwk_out.at[:, cols], 2),
                       (gg_s, gg_out, 3), (gpart.at[me], gall.at[me], 4))[i]
        return pltpu.make_async_copy(src, dst, s_out.at[k])

    def rows_f(w, to):
        return ds(w * n + to, HEAD)

    with scope('dwo'):
        loop(0, n, flip_o)
        loop(0, nt, dwo_step)
        out(1).start()

    def m_send(e):
        return remote(mine2.at[pl.ds(0, 2)], mall.at[me, pl.ds(0, 2)], s_m.at[0], r_m.at[0], peer(e))

    with scope('dwv'):
        loop(0, n, flip_v)
        loop(nt, 2 * nt, dwv_step)
        out(3).start()
    with scope('pwait'):
        settle(pall.at[pl.ds(0, n - 1), pl.ds(0, 2)], s_p.at[0], r_p.at[0])
        tot = pall[0, 0:2, :]
        for j in range(1, n):
            tot = tot + pall[j, 0:2, :]
        mine2[0:2, :] = tot * (1.0 / d)
    for e in far:
        m_send(e).start()
    mall[me, 0:2, :] = mine2[0:2, :]
    for e in far:
        v_send(e).start()
    with scope('y'):
        settle(att.at[pl.ds(0, t_loc - t_loc // n), :], s_o.at[0], r_o.at[0])
        loop(0, nt, y_step)
        out(0).start()

    def w_copies(t):
        slot = lax.rem(t, 2)
        return [pltpu.make_async_copy(w.at[ds(t, wr), :], wrow.at[slot, i], s_wr.at[slot]) for i, w in enumerate((wq_ref, wk_ref, wv_ref))]

    for cp in w_copies(0):
        cp.start()
    cl = cl_s[...]
    sl = sl_s[...]

    def back_rope(a):
        a = a.astype(f32)
        return a * cl + pltpu.roll(a, half, 1) * sl

    def loc_step(i):
        tq[:, hs(i)] = (inv[0] * (back_rope(tq[:, hs(i)]) * g_ref[0:1, hs(i)] - qkl[0, :, hs(i)] * inv[0] * mq)).astype(bf16)
        tkv[0, :, hs(i)] = (inv[1] * (back_rope(tkv[0, :, hs(i)]) * g_ref[1:2, hs(i)] - qkl[1, :, hs(i)] * inv[1] * mk)).astype(bf16)

    with scope('mwait'):
        settle(mall.at[pl.ds(0, n - 1), pl.ds(0, 2)], s_m.at[0], r_m.at[0])

    def head_step(j):
        js = rows(j)
        for w, src in enumerate((dq_s[js, :], dkv[j, 0])):
            rawT[w * HEAD:(w + 1) * HEAD, js] = (sall[j, w:w + 1, :] * (unroped(src, js) * gcol[w] - hatT[w, :, js] * mall[j, w:w + 1, :])).astype(bf16)

    with scope('head'):
        loop(0, n, head_step)

    def a_send(to):
        return remote(raw.at[1, rows_f(0, to), :], dwq_out.at[:, cols], s_a.at[0], r_a.at[0], to)

    def b_send(to):
        return remote(raw.at[1, rows_f(1, to), :], dwk_out.at[:, cols], s_b.at[0], r_b.at[0], to)

    def dw_step(t):
        h2_copy(t).wait()

        @pl.when(t + 1 < nt)
        def _():
            h2_copy(t + 1).start()
        nn = chip(t)
        r = dotf(rawT[...], tile[lax.rem(t, 2)], NN)
        for u in range(cw // HEAD):
            to = nn * (cw // HEAD) + u
            for w in range(2):
                raw[1, rows_f(w, to), :] = r[w * HEAD:(w + 1) * HEAD, u * HEAD:(u + 1) * HEAD].T

            @pl.when(to != me)
            def _():
                a_send(to).start()
                b_send(to).start()

    with scope('dw'):
        loop(0, nt, dw_step)
    out(4).start()
    out(5).start()
    with scope('waitkv'):
        settle(tkv.at[:, pl.ds(0, t_loc - t_loc // n), :], s_kv.at[0], r_kv.at[0])
    with scope('waitq'):
        settle(tq.at[pl.ds(0, t_loc - t_loc // n), :], s_q.at[0], r_q.at[0])

    mq = spread_col(mine2[0:1, :])
    mk = spread_col(mine2[1:2, :])
    with scope('loc'):
        loop(0, nd, loc_step)

    def dh_step(t):
        settle(wrow.at[lax.rem(t, 2)], s_wr.at[lax.rem(t, 2)])

        @pl.when(t + 1 < nw)
        def _():
            for cp in w_copies(t + 1):
                cp.start()
        slot = lax.rem(t, 2)
        r = dotf(tq[...], wrow[slot, 0], NT) + dotf(tkv[0], wrow[slot, 1], NT) + dotf(tkv[1], wrow[slot, 2], NT)
        dh[:, ds(t, wr)] = r.astype(bf16).astype(f32)

    with scope('dh'):
        loop(0, nw, dh_step)

    def mx_step(i, acc):
        return acc + dh[:, hs(i)] * g_ref[2:3, hs(i)] * x_ref[:, hs(i)].astype(f32)

    def g_send(e):
        return remote(gpart.at[peer(e), pl.ds(0, 1)], gall.at[me, pl.ds(0, 1)], s_g.at[0], r_g.at[0], peer(e))

    with scope('gx'):
        mx = jnp.sum(lax.fori_loop(0, nd, mx_step, zero), axis=1, keepdims=True) * (1.0 / d) * xinv[...]

        def gx_step(i):
            xh = x_ref[:, hs(i)].astype(f32) * xinv[...]
            dhh = dh[:, hs(i)]
            gpart[i] = jnp.broadcast_to(jnp.sum(dhh * xh, axis=0, keepdims=True), (8, HEAD))
            gx_s[:, hs(i)] = (gy_ref[:, hs(i)].astype(f32) + xinv[...] * (dhh * g_ref[2:3, hs(i)] - xh * mx)).astype(bf16)

        loop(0, nd, gx_step)
        out(2).start()
    for e in far:
        g_send(e).start()
    out(7).start()
    out(6).start()
    with scope('end_drain'):
        for a in range(2):
            settle(alls[a].at[pl.ds(0, (nz - 1) * t_loc), :], s_ring.at[a])
            settle(alls[a].at[pl.ds(0, nz * t_loc), :], s_par.at[a])
        settle(tkv, s_out.at[0])
        settle(dwo_s, s_out.at[1])
        settle(bv.at[pl.ds(0, 3)], s_out.at[2])
        settle(gg_s, s_out.at[3])
        settle(gpart.at[0], s_out.at[4])
    most = pl.ds(0, HEAD - HEAD // n)
    with scope('end_v'):
        settle(dwv_out.at[most, :], s_v.at[0], r_v.at[0])
    with scope('end_a'):
        settle(dwq_out.at[most, :], s_a.at[0], r_a.at[0])
    with scope('end_b'):
        settle(dwk_out.at[most, :], s_b.at[0], r_b.at[0])
    with scope('end_g'):
        settle(gall.at[pl.ds(0, n - 1), pl.ds(0, 1)], s_g.at[0], r_g.at[0])


def block(n, x, gy, pos, gq, gk, gn, freq, wq, wk, wv, wo):
    t_loc, d = x.shape
    t_all = t_loc * n
    vm = pl.BlockSpec(memory_space=pltpu.VMEM)
    hb = pl.BlockSpec(memory_space=pl.ANY)
    S = jax.ShapeDtypeStruct
    V = pltpu.VMEM
    sem = pltpu.SemaphoreType.DMA
    hd = (t_all, HEAD)
    tok = (t_loc, d)
    nz = n // 2
    return pl.pallas_call(functools.partial(block_kernel, n),
        in_specs=[hb] * 2 + [vm] * 5 + [hb] * 4,
        out_specs=[hb] * 10,
        out_shape=[S(tok, bf16), S(tok, bf16), S((n, 8, d // n), f32)] + [S((d // n, d), f32)] * 4 + [S((2, 8, HEAD), f32), S((t_all, d), bf16), S((t_all, d), bf16)],
        scratch_shapes=[V(tok, bf16), V(tok, bf16), V((8, d), f32), V(tok, bf16), V((d, 3 * HEAD), bf16), V((HEAD, d), bf16), V((3,) + hd, f32), V((2,) + tok, bf16), V((2, d, 2 * HEAD), bf16), V((2, t_all, 2 * HEAD), bf16), V((2, 3, 2 * HEAD, d), bf16),
            V((2,) + tok, f32), V((2, HEAD, t_all), f32), V((2, HEAD // 2, t_all), f32)] + [V(hd, bf16)] * 5 + [V((8, t_all), f32)] * 2
        + [V(hd, bf16), V((n, 2, t_loc, HEAD), bf16), V(tok, bf16), V((2,) + tok, bf16), V(tok, bf16), V((HEAD, t_all), bf16), V((n, d // n, HEAD), f32), V((2 * HEAD, t_all), bf16), V(tok, bf16), V((HEAD, d), f32), V(tok, bf16), V(tok, f32),
            V((2, t_loc, HEAD), f32), V((t_loc, HEAD), f32), V((t_loc, HEAD), f32), V((2, t_loc, HEAD), f32), V((t_loc, HEAD), f32), V((8, t_loc), f32), V((n, 8, t_loc), f32), V((8, t_loc), f32), V((n, 8, t_loc), f32), V((n, 8, t_loc), f32), V((n, 8, t_loc), f32), V((n, 8, d // n), f32), V((2, 8, HEAD), f32)]
        + [sem((2,)), sem((2, 2, nz - 1, 2)), sem((2,)), sem((2, 2 * (nz - 1))), sem((2,))] + [sem((1,))] * 20
        + [sem((2,)), sem((2,)), sem((2,)), sem((7,)), sem((2,)), sem((1,)), sem((5,))],
        compiler_params=pltpu.CompilerParams(collective_id=1, has_side_effects=True, vmem_limit_bytes=67043328), name='block')(x, gy, pos, gq, gk, gn, freq, wq, wk, wv, wo)


def copy_kernel(*refs):
    k = (len(refs) - 2) // 3
    src, dst, buf, si, so = list(refs[:k - 1]), refs[k - 1:2 * k - 1], refs[2 * k - 1:3 * k - 1], refs[-2], refs[-1]
    parts = src[k - 3]
    src[k - 3:] = [parts, src[k - 2].at[0, 0:1, :], src[k - 2].at[1, 0:1, :]]
    buf = list(buf)
    total = buf[k - 3]
    buf[k - 3] = refs[-3]
    ins = [pltpu.make_async_copy(src[i], buf[i], si.at[i]) for i in range(k)]
    outs = [pltpu.make_async_copy(buf[i], dst[i], so.at[i]) if i != k - 3 else None for i in range(k)]
    for cp in ins:
        cp.start()
    outs[k - 3] = pltpu.make_async_copy(total, dst[k - 3], so.at[k - 3])
    for i in range(k):
        ins[i].wait()
        if i == k - 3:
            total[...] = jnp.sum(refs[-3][:, 0:1, :], axis=0)
        outs[i].start()
    for cp in outs:
        cp.wait()


def copy_out(arrays):
    hb = pl.BlockSpec(memory_space=pl.ANY)
    shapes = [(a.shape, a.dtype) for a in arrays[:-2]] + [((1, HEAD), f32)] * 3
    k = len(shapes)
    return pl.pallas_call(copy_kernel, in_specs=[hb] * len(arrays), out_specs=[hb] * k, out_shape=[jax.ShapeDtypeStruct(*a) for a in shapes],
        scratch_shapes=[pltpu.VMEM(*a) for a in shapes] + [pltpu.VMEM(arrays[-2].shape, f32)] + [pltpu.SemaphoreType.DMA((k,))] * 2, name='copy_out')(*arrays)


def solution(mesh):
    n = mesh.shape['sp']

    def device_step(x_in, grad_y, positions, g_norm, wq, wk, wv, wo, gq, gk):
        half = HEAD // 2
        inv_freq = ROPE_BASE ** (-np.arange(half) * (2.0 / HEAD))
        freq = jnp.asarray(np.tile(inv_freq, (8, 2)), f32)
        y, gx, gn, dwq, dwk, dwv, dwo, gg, _, _ = block(n, x_in[0], grad_y[0], positions, gq, gk, g_norm, freq, wq, wk, wv, wo)
        y, gx, dwq, dwk, dwv, dwo, gn, ggq, ggk = copy_out([y, gx, dwq, dwk, dwv, dwo, gn, gg])
        return (y[None], gx[None], gn[0], dwq, dwk, dwv, dwo, ggq[0], ggk[0])

    seq_spec = P('dp', 'sp', None)
    rep2, rep1 = P(None, None), P(None)
    row_spec, vec_spec = P(('dp', 'sp'), None), P(('dp', 'sp'))
    return jax.shard_map(device_step, mesh=mesh, in_specs=(seq_spec, seq_spec, P('dp', 'sp'), rep1, rep2, rep2, rep2, rep2, rep1, rep1), out_specs=(seq_spec, seq_spec, vec_spec, row_spec, row_spec, row_spec, row_spec, vec_spec, vec_spec), check_vma=False)
```

time: 357 us -> 345 us (0.966)
  Pallas kernels: 353 us -> 343 us
    pallas_call x1, Pallas kernels: 347 us -> 337 us  [block(): pl.pallas_call(functools.partial(block_kernel, n), in_specs=[hb] * 2 + [v...]
where the time goes in v4:
time: 345 us; the launch traced here: 343 us
  Pallas kernels  343 us (99%)
    pallas_call x1, Pallas kernels, block(): pl.pallas_call(functools.partial(block_kernel, n), in_specs=[hb] * 2 + [v...  337 us

profile of v4, /device:TPU:21, one launch (start us, length us, event | category | flops | bytes accessed | tf_op | source)
XLA Modules:
  0.0 343.4 jit_solution(5075505490039798289)
XLA Ops:
  0.6 337.1 %block.1 = (bf16[256,2048]{1,0:T(8,128)(2,1)}, bf16[256,2048]{1,0:T(8,128)(2,1)}, f32[16,8,128]{2,1,0:T(8,128)}, f32[128,2048]{1,0:T(8,128)}, f32[128,2048]{1,0:...) custom-call(bf16[256,2048]{1,0:T(8,128)(2,1)} %bitcast.7, ...), custom_call_target="tpu_custom_call" | custom-call | tf_op jit(solution)/shard_map/block/pallas_call | solution.py:743
  337.7 5.5 %copy_out.1 = (bf16[256,2048]{1,0:T(8,128)(2,1)}, bf16[256,2048]{1,0:T(8,128)(2,1)}, f32[128,2048]{1,0:T(8,128)}, f32[128,2048]{1,0:T(8,128)}, f32[128,2048]{1,0...) custom-call(bf16[256,2048]{1,0:T(8,128)(2,1)} %get-tuple-element.26.refs_0_, ...), custom_call_target="tpu_custom_call" | custom-call | tf_op jit(solution)/shard_map/copy_out/pallas_call | solution.py:782

commit v5 on v4

--- a/solution.py
+++ b/solution.py
@@ -50,12 +50,12 @@
     lax.fori_loop(lo, hi, step, 0)
 
 
-def block_kernel(n, x_hbm, gy_hbm, pos_ref, gq_ref, gk_ref, gn1_ref, fr_ref, wq_ref, wk_ref, wv_ref, wo_ref,
+def block_kernel(n, x_hbm, gy_hbm, pos_hbm, gq_hbm, gk_hbm, gn1_hbm, fr_hbm, wq_ref, wk_ref, wv_ref, wo_ref,
                  y_out, gx_out, gall, dwq_out, dwk_out, dwv_out, dwo_out, gg_out, h_all, gy_all,
-                 x_ref, gy_ref, g_ref, hid, wh, woh, raw, xbuf, wtile, tile, wrow, qkl, hatT, csT, q_s, k_s, v_s, do_s, o_s, lse, dl,
+                 pos_ref, gq_ref, gk_ref, gn1_ref, fr_ref, x_ref, gy_ref, g_ref, hid, wh, woh, raw, xbuf, wtile, tile, wrow, qkl, hatT, csT, q_s, k_s, v_s, do_s, o_s, lse, dl,
                  dq_s, dkv, tq, tkv, att, dt, bv, rawT, y_s, dwo_s, gx_s, dh, ssq, cl_s, sl_s, inv, xinv, mine, sall, mine2, mall, pm, pall, gpart, gg_s,
                  s_ring, r_ring, s_par, r_par, r_own, s_st, r_st, s_o, r_o, s_kv, r_kv, s_q, r_q, s_v, r_v, s_a, r_a, s_b, r_b, s_m, r_m, s_g, r_g, s_p, r_p,
-                 s_ld, s_t, s_w, s_x, s_wr, s_loc, s_out):
+                 s_ld, s_t, s_w, s_x, s_wr, s_loc, s_out, s_in):
     me = lax.axis_index('sp')
     t_loc, d = x_hbm.shape
     t_all = t_loc * n
@@ -81,7 +81,7 @@
     cols = ds(me, HEAD)
     far = sorted(range(1, n), key=lambda e: -min(e, n - e))
     alls = (h_all, gy_all)
-    own_src = (hid, gy_ref)
+    own_src = (hid, gy_hbm)
 
     def peer(e):
         return lax.rem(me + e, n)
@@ -115,10 +115,10 @@
         return remote(alls[a].at[rs, :], alls[a].at[rs, :], s_par.at[a], r_par.at[a, 2 * s + u], mate)
 
     def own_par(a):
-        return remote(own_src[a], alls[a].at[rows(me), :], s_par.at[a], r_own.at[a], mate)
+        return remote((hid, gy_ref)[a], alls[a].at[rows(me), :], s_par.at[a], r_own.at[a], mate)
 
     def own_loc(a):
-        return pltpu.make_async_copy(own_src[a], alls[a].at[rows(me), :], s_loc.at[0])
+        return pltpu.make_async_copy((hid, gy_ref)[a], alls[a].at[rows(me), :], s_loc.at[0])
 
     def comm(a, t):
         s = t // 2
@@ -149,7 +149,7 @@
         return [piece(c, 0, s, u), piece(c, 1, s, u), piece(1 - c, 0, s, u), piece(1 - c, 1, s, u)]
 
     def gather(a, t, work, put):
-        @pl.when(t < ticks)
+        @pl.when((t >= a) & (t < ticks))
         def _():
             with scope('comm'):
                 comm(a, t)
@@ -158,7 +158,7 @@
         def _():
             own_par(a).wait_recv()
             mate_load(a).start()
-            put(work(own_src[a][...]), [rows(me)])
+            put(work((hid, gy_ref)[a][...]), [rows(me)])
 
         @pl.when(t == 1)
         def _():
@@ -219,8 +219,6 @@
             inv[w] = jnp.broadcast_to(iv, (t_loc, HEAD))
             mine[w:w + 1, :] = as_row(iv)
         mine[2:3, :] = pos_ref[...].astype(f32)
-        for e in range(1, n):
-            st_send(e).start()
         sall[me, 0:3, :] = mine[0:3, :]
         ang = spread_col(pos_ref[...].astype(f32)) * fr_ref[0:1, :]
         cl_s[...] = jnp.cos(ang)
@@ -238,22 +236,31 @@
 
     with scope('begin'):
         barrier = pltpu.get_barrier_semaphore()
-        for e in range(1, n):
-            pl.semaphore_signal(barrier, inc=1, device_id={'sp': peer(e)}, device_id_type=MESH)
+        for to in (up, down, mate):
+            pl.semaphore_signal(barrier, inc=1, device_id={'sp': to}, device_id_type=MESH)
+
         def x_piece(p):
             rs = pl.ds(p * sub, sub)
             return pltpu.make_async_copy(x_hbm.at[rs, :], x_ref.at[rs, :], s_x.at[2 + p])
 
-        gy_load = pltpu.make_async_copy(gy_hbm, gy_ref, s_x.at[6])
+        smalls = [pltpu.make_async_copy(src, dst, s_in.at[i]) for i, (src, dst) in enumerate(((gn1_hbm, gn1_ref), (gq_hbm, gq_ref), (gk_hbm, gk_ref), (pos_hbm, pos_ref), (fr_hbm, fr_ref)))]
+        smalls[0].start()
         for p in (0, 2, 1, 3):
             x_piece(p).start()
+        for cp in smalls[1:]:
+            cp.start()
+        gy_load = pltpu.make_async_copy(gy_hbm, gy_ref, s_x.at[6])
         gy_load.start()
         for i in range(3):
             head_w(i).start()
         wo_load().start()
         stat_tile(0, start)
-        for w, src in enumerate((gq_ref, gk_ref, gn1_ref)):
-            g_ref[w:w + 1, :] = src[...].astype(f32).reshape(1, d)
+        pl.semaphore_wait(barrier, 3)
+        ring0(1, 0, 0).start()
+        ring0(1, 1, 0).start()
+        smalls[0].wait()
+        g_ref[2:3, :] = gn1_ref[...].astype(f32).reshape(1, d)
+
         def norm_piece(p):
             rs = pl.ds(p * sub, sub)
             x_piece(p).wait()
@@ -271,15 +278,13 @@
 
             loop(0, nd, hid_step)
 
-        norm_piece(0)
-        norm_piece(2)
-        pl.semaphore_wait(barrier, n - 1)
-        ring0(0, 0, 0).start()
-        ring0(0, 1, 0).start()
-        norm_piece(1)
-        ring0(0, 0, 1).start()
-        norm_piece(3)
-        ring0(0, 1, 1).start()
+        for p in (0, 2, 1, 3):
+            norm_piece(p)
+            ring0(0, p // 2, p % 2).start()
+        for cp in smalls[1:]:
+            cp.wait()
+        for w, src in enumerate((gq_ref, gk_ref)):
+            g_ref[w:w + 1, :] = src[...].astype(f32).reshape(1, d)
         zero = jnp.zeros((t_loc, HEAD), f32)
         ssq[...] = jnp.zeros_like(ssq)
         gy_load.wait()
@@ -331,9 +336,9 @@
 
         @pl.when(t == 2 * last - 1)
         def _():
-            for u in range(2):
-                for direction in range(2):
-                    ring0(1, direction, u).start()
+            for direction in range(2):
+                ring0(1, direction, 1).start()
+            comm(1, 0)
 
         @pl.when(t < 4)
         def _():
@@ -345,14 +350,18 @@
             with scope('statdone'):
                 stat_done()
 
-        @pl.when(t == 6)
+        @pl.when(t == 8)
+        def _():
+            for e in far:
+                st_send(e).start()
+
+        @pl.when(t == 10)
         def _():
             settle(sall.at[pl.ds(0, n - 1), pl.ds(0, 3)], s_st.at[0], r_st.at[0])
-
-        @pl.when(((t >= 6) & (t <= 11)) | (t == 13))
-        def _():
-            with scope('finish'):
-                finish(jnp.where(t == 13, last - 1, t - 7))
+        lo = jnp.where(t == 10, -1, jnp.where(t == 11, 1, jnp.where(t >= 12, t - 9, 0)))
+        hi = jnp.where(t == 10, 1, jnp.where(t == 11, 3, jnp.where((t >= 12) & (t <= 14), t - 8, -1)))
+        with scope('finish'):
+            loop(lo, hi, finish)
 
     with scope('gather_x'):
         loop(0, ticks + 2, x_tick)
@@ -399,18 +408,25 @@
     def y_tick(t):
         gather(1, t, do_work, do_put)
 
-        @pl.when(t == 0)
+        @pl.when(t == 1)
         def _():
             with scope('finish'):
                 finish(last)
+        t = t - 1
         lo = jnp.where(t == 0, 0, jnp.where(t <= 4, t + 1, jnp.where(t <= 6, 6, 7)))
         hi = jnp.where(t == 0, 2, jnp.where(t <= 4, t + 2, jnp.where(t == 5, 6, jnp.where(t == 8, 8, 7))))
+        hi = jnp.where(t < 0, 0, hi)
         with scope('attend'):
             loop(lo, hi, attend)
 
+        @pl.when(t == ticks - 3)
+        def _():
+            for e in far[-5:]:
+                o_send(e).start()
+
         @pl.when(t == ticks - 2)
         def _():
-            for e in far:
+            for e in far[:-5]:
                 o_send(e).start()
 
     with scope('gather_y'):
@@ -661,9 +677,7 @@
                 b_send(to).start()
 
     with scope('dw'):
-        loop(0, nt, dw_step)
-    out(4).start()
-    out(5).start()
+        loop(0, nt // 2, dw_step)
     with scope('waitkv'):
         settle(tkv.at[:, pl.ds(0, t_loc - t_loc // n), :], s_kv.at[0], r_kv.at[0])
     with scope('waitq'):
@@ -709,6 +723,10 @@
         g_send(e).start()
     out(7).start()
     out(6).start()
+    with scope('dw2'):
+        loop(nt // 2, nt, dw_step)
+        out(4).start()
+        out(5).start()
     with scope('end_drain'):
         for a in range(2):
             settle(alls[a].at[pl.ds(0, (nz - 1) * t_loc), :], s_ring.at[a])
@@ -732,7 +750,6 @@
 def block(n, x, gy, pos, gq, gk, gn, freq, wq, wk, wv, wo):
     t_loc, d = x.shape
     t_all = t_loc * n
-    vm = pl.BlockSpec(memory_space=pltpu.VMEM)
     hb = pl.BlockSpec(memory_space=pl.ANY)
     S = jax.ShapeDtypeStruct
     V = pltpu.VMEM
@@ -741,15 +758,15 @@
     tok = (t_loc, d)
     nz = n // 2
     return pl.pallas_call(functools.partial(block_kernel, n),
-        in_specs=[hb] * 2 + [vm] * 5 + [hb] * 4,
+        in_specs=[hb] * 11,
         out_specs=[hb] * 10,
         out_shape=[S(tok, bf16), S(tok, bf16), S((n, 8, d // n), f32)] + [S((d // n, d), f32)] * 4 + [S((2, 8, HEAD), f32), S((t_all, d), bf16), S((t_all, d), bf16)],
-        scratch_shapes=[V(tok, bf16), V(tok, bf16), V((8, d), f32), V(tok, bf16), V((d, 3 * HEAD), bf16), V((HEAD, d), bf16), V((3,) + hd, f32), V((2,) + tok, bf16), V((2, d, 2 * HEAD), bf16), V((2, t_all, 2 * HEAD), bf16), V((2, 3, 2 * HEAD, d), bf16),
+        scratch_shapes=[V((1, t_loc), jnp.int32), V((d,), bf16), V((d,), bf16), V((d,), bf16), V((8, HEAD), f32), V(tok, bf16), V(tok, bf16), V((8, d), f32), V(tok, bf16), V((d, 3 * HEAD), bf16), V((HEAD, d), bf16), V((3,) + hd, f32), V((2,) + tok, bf16), V((2, d, 2 * HEAD), bf16), V((2, t_all, 2 * HEAD), bf16), V((2, 3, 2 * HEAD, d), bf16),
             V((2,) + tok, f32), V((2, HEAD, t_all), f32), V((2, HEAD // 2, t_all), f32)] + [V(hd, bf16)] * 5 + [V((8, t_all), f32)] * 2
         + [V(hd, bf16), V((n, 2, t_loc, HEAD), bf16), V(tok, bf16), V((2,) + tok, bf16), V(tok, bf16), V((HEAD, t_all), bf16), V((n, d // n, HEAD), f32), V((2 * HEAD, t_all), bf16), V(tok, bf16), V((HEAD, d), f32), V(tok, bf16), V(tok, f32),
             V((2, t_loc, HEAD), f32), V((t_loc, HEAD), f32), V((t_loc, HEAD), f32), V((2, t_loc, HEAD), f32), V((t_loc, HEAD), f32), V((8, t_loc), f32), V((n, 8, t_loc), f32), V((8, t_loc), f32), V((n, 8, t_loc), f32), V((n, 8, t_loc), f32), V((n, 8, t_loc), f32), V((n, 8, d // n), f32), V((2, 8, HEAD), f32)]
         + [sem((2,)), sem((2, 2, nz - 1, 2)), sem((2,)), sem((2, 2 * (nz - 1))), sem((2,))] + [sem((1,))] * 20
-        + [sem((2,)), sem((2,)), sem((2,)), sem((7,)), sem((2,)), sem((1,)), sem((5,))],
+        + [sem((2,)), sem((2,)), sem((2,)), sem((7,)), sem((2,)), sem((1,)), sem((5,)), sem((5,))],
         compiler_params=pltpu.CompilerParams(collective_id=1, has_side_effects=True, vmem_limit_bytes=67043328), name='block')(x, gy, pos, gq, gk, gn, freq, wq, wk, wv, wo)
 
 

time: 345 us -> 340 us (0.986)
  Pallas kernels: 343 us -> 337 us
    pallas_call x1, Pallas kernels: 337 us -> 332 us  [block(): pl.pallas_call(functools.partial(block_kernel, n), in_specs=[hb] * 11, ou...]
where the time goes in v5:
time: 340 us; the launch traced here: 338 us
  Pallas kernels  337 us (99%)
    pallas_call x1, Pallas kernels, block(): pl.pallas_call(functools.partial(block_kernel, n), in_specs=[hb] * 11, ou...  332 us

profile of v5, /device:TPU:21, one launch (start us, length us, event | category | flops | bytes accessed | tf_op | source)
XLA Modules:
  0.0 338.1 jit_solution(6319166917551521287)
XLA Ops:
  0.6 331.7 %block.1 = (bf16[256,2048]{1,0:T(8,128)(2,1)}, bf16[256,2048]{1,0:T(8,128)(2,1)}, f32[16,8,128]{2,1,0:T(8,128)}, f32[128,2048]{1,0:T(8,128)}, f32[128,2048]{1,0:...) custom-call(bf16[256,2048]{1,0:T(8,128)(2,1)} %bitcast.7, ...), custom_call_target="tpu_custom_call" | custom-call | tf_op jit(solution)/shard_map/block/pallas_call | solution.py:760
  332.4 5.5 %copy_out.1 = (bf16[256,2048]{1,0:T(8,128)(2,1)}, bf16[256,2048]{1,0:T(8,128)(2,1)}, f32[128,2048]{1,0:T(8,128)}, f32[128,2048]{1,0:T(8,128)}, f32[128,2048]{1,0...) custom-call(bf16[256,2048]{1,0:T(8,128)(2,1)} %get-tuple-element.26.refs_0_, ...), custom_call_target="tpu_custom_call" | custom-call | tf_op jit(solution)/shard_map/copy_out/pallas_call | solution.py:799

commit v6 on v5

--- a/solution.py
+++ b/solution.py
@@ -52,10 +52,10 @@
 
 def block_kernel(n, x_hbm, gy_hbm, pos_hbm, gq_hbm, gk_hbm, gn1_hbm, fr_hbm, wq_ref, wk_ref, wv_ref, wo_ref,
                  y_out, gx_out, gall, dwq_out, dwk_out, dwv_out, dwo_out, gg_out, h_all, gy_all,
-                 pos_ref, gq_ref, gk_ref, gn1_ref, fr_ref, x_ref, gy_ref, g_ref, hid, wh, woh, raw, xbuf, wtile, tile, wrow, qkl, hatT, csT, q_s, k_s, v_s, do_s, o_s, lse, dl,
-                 dq_s, dkv, tq, tkv, att, dt, bv, rawT, y_s, dwo_s, gx_s, dh, ssq, cl_s, sl_s, inv, xinv, mine, sall, mine2, mall, pm, pall, gpart, gg_s,
+                 pos_ref, gq_ref, gk_ref, gn1_ref, fr_ref, x_ref, gy_ref, g_ref, hid, wh, woh, raw, xbuf, wtile, tile, wrow, qkl, hatT, csT, q_s, k_s, v_s, do_s, o_s, lse, ld2,
+                 dq_s, dkv, tq, tkv, att, rawT, dh, cl_s, sl_s, inv, xinv, mine, sall, mine2, mall, pm, pall, gpart, gg_s, k2, v2, q2, do2, o2, dq2, dkv2,
                  s_ring, r_ring, s_par, r_par, r_own, s_st, r_st, s_o, r_o, s_kv, r_kv, s_q, r_q, s_v, r_v, s_a, r_a, s_b, r_b, s_m, r_m, s_g, r_g, s_p, r_p,
-                 s_ld, s_t, s_w, s_x, s_wr, s_loc, s_out, s_in):
+                 s_ld, s_t, s_w, s_x, s_wr, s_loc, s_out, s_in, s_r2, s_hu, s_o2, r_o2, s_q2, r_q2, s_kv2, r_kv2, s_ld2, r_ld2):
     me = lax.axis_index('sp')
     t_loc, d = x_hbm.shape
     t_all = t_loc * n
@@ -83,6 +83,21 @@
     alls = (h_all, gy_all)
     own_src = (hid, gy_hbm)
 
+    again = lax.rem(me, 4) == 0
+    sent = lax.rem(me, 4) != 0
+    n_sent = n - n // 4
+    msg = t_loc // n
+
+    def h2(i):
+        return c * (n // 2) + 4 * i
+
+    def w2(act):
+        for i in range(2):
+            act(pltpu.make_async_copy(wk_ref.at[:, hs(h2(i))], wtile.at[0, :, pl.ds(i * HEAD, HEAD)], s_r2.at[0]))
+            act(pltpu.make_async_copy(wv_ref.at[:, hs(h2(i))], wtile.at[1, :, pl.ds(i * HEAD, HEAD)], s_r2.at[0]))
+            act(pltpu.make_async_copy(wq_ref.at[:, hs(h2(i))], tile.at[0, pl.ds(0, d), pl.ds(i * HEAD, HEAD)], s_r2.at[1]))
+            act(pltpu.make_async_copy(wo_ref.at[hs(h2(i)), :], wrow.at[0, 0, pl.ds(i * HEAD, HEAD), :], s_r2.at[2]))
+
     def peer(e):
         return lax.rem(me + e, n)
 
@@ -206,7 +221,7 @@
         acc = r[:, :HEAD] * r[:, :HEAD]
         for j in range(1, cw // HEAD):
             acc = acc + r[:, j * HEAD:(j + 1) * HEAD] * r[:, j * HEAD:(j + 1) * HEAD]
-        ssq[w] = ssq[w] + acc
+        inv[w] = inv[w] + acc
 
     def st_send(e):
         return remote(mine.at[pl.ds(0, 3)], sall.at[me, pl.ds(0, 3)], s_st.at[0], r_st.at[0], peer(e))
@@ -215,7 +230,7 @@
 
     def stat_done():
         for w in range(2):
-            iv = lax.rsqrt(jnp.sum(ssq[w], axis=1, keepdims=True) * (1.0 / d) + NORM_EPS)
+            iv = lax.rsqrt(jnp.sum(inv[w], axis=1, keepdims=True) * (1.0 / d) + NORM_EPS)
             inv[w] = jnp.broadcast_to(iv, (t_loc, HEAD))
             mine[w:w + 1, :] = as_row(iv)
         mine[2:3, :] = pos_ref[...].astype(f32)
@@ -286,7 +301,7 @@
         for w, src in enumerate((gq_ref, gk_ref)):
             g_ref[w:w + 1, :] = src[...].astype(f32).reshape(1, d)
         zero = jnp.zeros((t_loc, HEAD), f32)
-        ssq[...] = jnp.zeros_like(ssq)
+        inv[...] = jnp.zeros_like(inv)
         gy_load.wait()
         own_loc(1).start()
     own_par(0).start()
@@ -354,6 +369,7 @@
         def _():
             for e in far:
                 st_send(e).start()
+            w2(start)
 
         @pl.when(t == 10)
         def _():
@@ -397,13 +413,66 @@
         to = peer(e)
         return remote(o_s.at[rows(to), :], att.at[:, cols], s_o.at[0], r_o.at[0], to)
 
+    def h_unit(u):
+        return pltpu.make_async_copy(h_all.at[rows(u), :], wrow.at[1, lax.rem(u, 2)], s_hu.at[lax.rem(u, 2)])
+
+    def kv_unit(u):
+        h_unit(u).wait()
+
+        @pl.when(u < n - 1)
+        def _():
+            h_unit(u + 1).start()
+        xv = wrow[1, lax.rem(u, 2)]
+        rs = rows(u)
+        st = sall[u, 0:3, :]
+        ang = spread_col(st[2:3, :]) * fr_ref[0:1, :]
+        co = jnp.cos(ang)
+        si = jnp.sin(ang) * sgn
+
+        def turned(r, w, i):
+            hat = r[:, i * HEAD:(i + 1) * HEAD] * spread_col(st[w:w + 1, :]) * g_ref[w:w + 1, hs(h2(i))]
+            return (hat * co + pltpu.roll(hat, half, 1) * si).astype(bf16)
+
+        @pl.when(u < 2 * z + 2)
+        def _():
+            rk = dotf(xv, wtile[0], NN)
+            rv = dotf(xv, wtile[1], NN).astype(bf16)
+            for i in range(2):
+                k2[i, rs, :] = turned(rk, 1, i)
+                v2[i, rs, :] = rv[:, i * HEAD:(i + 1) * HEAD]
+
+        @pl.when(u >= 2 * z)
+        def _():
+            rq = dotf(xv, tile[0, 0:d, :], NN)
+            for i in range(2):
+                @pl.when(u < 2 * z + 2)
+                def _():
+                    q2[i, rows(u - 2 * z), :] = turned(rq, 0, i)
+
+                @pl.when(u >= 2 * z + 2)
+                def _():
+                    k2[i, rs, :] = turned(rq, 0, i)
+
+    def do_again(gv, core):
+        r = dotf(gv, wrow[0, 0], NT).astype(bf16)
+        for i in range(2):
+            do2[i, rows(core), :] = r[:, i * HEAD:(i + 1) * HEAD]
+
     def do_work(xv):
-        return dotf(xv, woh[...], NT).astype(bf16)
+        return dotf(xv, woh[...], NT).astype(bf16), xv
 
     def do_put(r, where):
+        r, xv = r
         step = r.shape[0] // len(where)
         for i, rs in enumerate(where):
             do_s[rs, :] = r[i * step:(i + 1) * step]
+        if len(where) == 4:
+            w = dotf(xv, wrow[0, 0], NT).astype(bf16)
+            for j, rs in enumerate(where):
+                @pl.when(rs.start >= 2 * t_loc * (z + 1))
+                def _():
+                    for i in range(2):
+                        v2[i, rs, :] = w[j * step:(j + 1) * step, i * HEAD:(i + 1) * HEAD]
 
     def y_tick(t):
         gather(1, t, do_work, do_put)
@@ -419,15 +488,32 @@
         with scope('attend'):
             loop(lo, hi, attend)
 
-        @pl.when(t == ticks - 3)
+        @pl.when((t == ticks - 3) & sent)
         def _():
             for e in far[-5:]:
                 o_send(e).start()
 
-        @pl.when(t == ticks - 2)
+        @pl.when((t == ticks - 2) & sent)
         def _():
             for e in far[:-5]:
                 o_send(e).start()
+
+        @pl.when(t == -1)
+        def _():
+            settle(wrow.at[0, 0], s_r2.at[2])
+            do_again(gy_ref[...], c)
+            settle(h_all.at[pl.ds(0, 2 * t_loc), :], s_loc.at[0])
+            h_unit(0).start()
+            settle(wtile, s_r2.at[0])
+            settle(tile.at[0, pl.ds(0, d), :], s_r2.at[1])
+
+        @pl.when(t == 0)
+        def _():
+            do_again(xbuf[1], 1 - c)
+        first = jnp.where(t == 1, 0, jnp.where(t == 2, 1, jnp.where(t == 5, 2, jnp.where(t == 7, 5, jnp.where(t == 9, 8, jnp.where(t == 10, 11, jnp.where(t == 11, 14, 16)))))))
+        count = jnp.where((t == 1) | (t == 2), 1, jnp.where((t == 5) | (t == 7) | (t == 9) | (t == 10), 3, jnp.where(t == 11, 2, 0)))
+        with scope('again_kv'):
+            loop(first, first + count, kv_unit)
 
     with scope('gather_y'):
         loop(0, ticks + 2, y_tick)
@@ -451,18 +537,43 @@
     def kv_send(to):
         return remote(dkv.at[to], tkv.at[:, :, cols], s_kv.at[0], r_kv.at[0], to)
 
-    settle(h_all.at[pl.ds(0, 2 * t_loc), :], s_loc.at[0])
     gy_copy(0).start()
     wo_copy(0).start()
-    att[:, cols] = o_s[rows(me), :]
+    settle(h_all.at[pl.ds(0, (nz - 1) * t_loc), :], s_ring.at[0])
+    settle(h_all.at[pl.ds(0, nz * t_loc), :], s_par.at[0])
+
+    @pl.when(sent)
+    def _():
+        att[:, cols] = o_s[rows(me), :]
     raw[0] = jnp.zeros((t_all, HEAD), f32)
 
     def delta(j):
         qs = ds(j, blk)
-        dl[0:1, qs] = as_row(jnp.sum(raw[2, qs, :] * do_s[qs, :].astype(f32), axis=1, keepdims=True))
+        lse[1:2, qs] = as_row(jnp.sum(raw[2, qs, :] * do_s[qs, :].astype(f32), axis=1, keepdims=True))
 
     with scope('delta'):
         loop(0, nb, delta)
+
+    home = me // (n // 2)
+    slot2 = lax.rem(me, n // 2) // 4
+    mine_too = again & (home == c)
+
+    def ld_send(k):
+        to = lax.rem(z + k, nz) * 2 + home
+        return remote(lse.at[pl.ds(0, 2)], ld2.at[slot2, pl.ds(0, 2)], s_ld2.at[0], r_ld2.at[0], to)
+
+    @pl.when(again)
+    def _():
+        for k in (4, 3, 5, 2, 6, 1, 7):
+            ld_send(k).start()
+
+    @pl.when(again & (home != c))
+    def _():
+        ld_send(0).start()
+
+    @pl.when(mine_too)
+    def _():
+        ld2[slot2, 0:2, :] = lse[0:2, :]
 
     def bwd_step(s):
         kb = chip(s)
@@ -480,7 +591,7 @@
                 r = lax.broadcasted_iota(jnp.int32, (blk, blk), 0)
                 cc = lax.broadcasted_iota(jnp.int32, (blk, blk), 1)
                 p = jnp.where(cc >= r, p, 0.0)
-            g = (p * (dotf(v, do, NT) - dl[0:1, qs])).astype(bf16)
+            g = (p * (dotf(v, do, NT) - lse[1:2, qs])).astype(bf16)
             dv = dv + dotf(p.astype(bf16), do, NN)
             dk = dk + dotf(g, q, NN)
             raw[0, qs, :] = raw[0, qs, :] + dotf(g, k, TN)
@@ -495,12 +606,12 @@
             dkv[2 * kb + u, 0] = dk[u * t_loc:(u + 1) * t_loc]
             dkv[2 * kb + u, 1] = dv[u * t_loc:(u + 1) * t_loc]
 
-        @pl.when(kb != z)
+        @pl.when((kb != z) & sent)
         def _():
             for u in range(2):
                 kv_send(2 * kb + u).start()
 
-        @pl.when(kb == z)
+        @pl.when((kb == z) & sent)
         def _():
             kv_send(mate).start()
 
@@ -534,19 +645,22 @@
         sums = lax.fori_loop(0, n, share_step, (zt, zt))
     for e in far:
         p_send(e).start()
-    for e in far:
-        q_send(e).start()
+    @pl.when(sent)
+    def _():
+        for e in far:
+            q_send(e).start()
+        tq[:, cols] = dq_s[rows(me), :]
+        tkv[:, :, cols] = dkv[me]
+
     pall[me, 0:2, :] = pm[me, 0:2, :]
     for w in range(2):
         gg_s[w] = jnp.broadcast_to(jnp.sum(sums[w], axis=1, keepdims=True), (HEAD, HEAD)).T[0:8, :]
-    tq[:, cols] = dq_s[rows(me), :]
-    tkv[:, :, cols] = dkv[me]
 
     def flip_o(i):
-        dt[:, rows(i)] = o_s[rows(i), :].T
+        rawT[0:HEAD, rows(i)] = o_s[rows(i), :].T
 
     def flip_v(i):
-        dt[:, rows(i)] = dkv[i, 1].T
+        rawT[0:HEAD, rows(i)] = dkv[i, 1].T
 
     def dwo_step(t):
         gy_copy(t).wait()
@@ -558,7 +672,9 @@
         @pl.when(t + 1 == nt)
         def _():
             h_copy(t + 1).start()
-        dwo_s[:, ds(t, cw)] = dotf(dt[...], tile[lax.rem(t, 2)], NN)
+        r = dotf(rawT[0:HEAD, :], tile[lax.rem(t, 2)], NN)
+        for u in range(cw // HEAD):
+            raw[2, hs(n + t * (cw // HEAD) + u), :] = r[:, u * HEAD:(u + 1) * HEAD]
 
     def dwv_step(t):
         h_copy(t).wait()
@@ -570,9 +686,9 @@
         @pl.when(t + 1 == 2 * nt)
         def _():
             h2_copy(0).start()
-        r = dotf(dt[...], tile[lax.rem(t, 2)], NN)
+        r = dotf(rawT[0:HEAD, :], tile[lax.rem(t, 2)], NN)
         for u in range(cw // HEAD):
-            bv[(t - nt) * (cw // HEAD) + u] = r[:, u * HEAD:(u + 1) * HEAD].T
+            raw[2, hs((t - nt) * (cw // HEAD) + u), :] = r[:, u * HEAD:(u + 1) * HEAD].T
 
     def y_step(t):
         wo_copy(t).wait()
@@ -581,14 +697,14 @@
         def _():
             wo_copy(t + 1).start()
         cs = ds(t, cw)
-        y_s[:, cs] = (x_ref[:, cs].astype(f32) + dotf(att[...], wtile[lax.rem(t, 2)], NN)).astype(bf16)
+        hid[:, cs] = (x_ref[:, cs].astype(f32) + dotf(att[...], wtile[lax.rem(t, 2)], NN)).astype(bf16)
 
     def v_send(e):
         to = peer(e)
-        return remote(bv.at[to], dwv_out.at[:, cols], s_v.at[0], r_v.at[0], to)
+        return remote(raw.at[2, hs(to), :], dwv_out.at[:, cols], s_v.at[0], r_v.at[0], to)
 
     def out(i):
-        src, dst, k = ((y_s, y_out, 0), (dwo_s, dwo_out, 1), (gx_s, gx_out, 0), (bv.at[me], dwv_out.at[:, cols], 2),
+        src, dst, k = ((hid, y_out, 0), None, (xbuf.at[0], gx_out, 0), (raw.at[2, hs(me), :], dwv_out.at[:, cols], 2),
                        (raw.at[1, rows_f(0, me), :], dwq_out.at[:, cols], 2), (raw.at[1, rows_f(1, me), :], dwk_out.at[:, cols], 2),
                        (gg_s, gg_out, 3), (gpart.at[me], gall.at[me], 4))[i]
         return pltpu.make_async_copy(src, dst, s_out.at[k])
@@ -599,7 +715,8 @@
     with scope('dwo'):
         loop(0, n, flip_o)
         loop(0, nt, dwo_step)
-        out(1).start()
+        for j in range(n):
+            pltpu.make_async_copy(raw.at[2, pl.ds((n + j) * HEAD, HEAD), :], dwo_out.at[:, pl.ds(j * HEAD, HEAD)], s_out.at[1]).start()
 
     def m_send(e):
         return remote(mine2.at[pl.ds(0, 2)], mall.at[me, pl.ds(0, 2)], s_m.at[0], r_m.at[0], peer(e))
@@ -619,10 +736,108 @@
     mall[me, 0:2, :] = mine2[0:2, :]
     for e in far:
         v_send(e).start()
-    with scope('y'):
-        settle(att.at[pl.ds(0, t_loc - t_loc // n), :], s_o.at[0], r_o.at[0])
-        loop(0, nt, y_step)
-        out(0).start()
+    def got(buf, s_sem, r_sem):
+        @pl.when(sent)
+        def _():
+            settle(buf.at[pl.ds(0, (n - 1) * msg), :], s_sem.at[0])
+            settle(buf.at[pl.ds(0, (n_sent - 1) * msg), :], r_sem.at[0])
+
+        @pl.when(again)
+        def _():
+            settle(buf.at[pl.ds(0, n_sent * msg), :], r_sem.at[0])
+
+    def o2_send(i):
+        return remote(o2.at[i, rows(1 - c), :], att.at[:, hs(h2(i))], s_o2.at[0], r_o2.at[0], mate)
+
+    def q2_send(i):
+        return remote(dq2.at[i, rows(1 - c), :], tq.at[:, hs(h2(i))], s_q2.at[0], r_q2.at[0], mate)
+
+    def again_head(i):
+        q = q2[i]
+        do = do2[i]
+        r0 = lax.broadcasted_iota(jnp.int32, (blk, blk), 0)
+        c0 = lax.broadcasted_iota(jnp.int32, (blk, blk), 1)
+
+        def unit(kb, carry, masked):
+            m, l, acc = carry
+            ks = ds(kb, blk)
+            s = dotf(q, k2[i, ks, :], NT)
+            if masked:
+                s = jnp.where(r0 >= c0, s, -1e30)
+            mn = jnp.maximum(m, jnp.max(s, axis=1, keepdims=True))
+            al = jnp.exp2((m - mn) * cexp)
+            p = jnp.exp2((s - mn) * cexp)
+            l = l * al + jnp.sum(p, axis=1, keepdims=True)
+            acc = acc * al + dotf(p.astype(bf16), v2[i, ks, :], NN)
+            return mn, l, acc
+
+        init = (jnp.full((blk, 1), -1e30, f32), jnp.zeros((blk, 1), f32), jnp.zeros((blk, HEAD), f32))
+        m, l, acc = unit(z, lax.fori_loop(0, z, functools.partial(unit, masked=False), init), True)
+        o = acc / l
+        o2[i] = o.astype(bf16)
+        ls = m * cexp + jnp.log2(l)
+        de = jnp.sum(o * do.astype(f32), axis=1, keepdims=True)
+
+        def unit2(kb, dq, masked):
+            ks = ds(kb, blk)
+            k = k2[i, ks, :]
+            p = jnp.exp2(dotf(q, k, NT) * cexp - ls)
+            if masked:
+                p = jnp.where(r0 >= c0, p, 0.0)
+            g = (p * (dotf(do, v2[i, ks, :], NT) - de)).astype(bf16)
+            return dq + dotf(g, k, NN)
+
+        dq = unit2(z, lax.fori_loop(0, z, functools.partial(unit2, masked=False), jnp.zeros((blk, HEAD), f32)), True)
+        dq2[i] = (dq * scale).astype(bf16)
+
+        k = k2[i, ds(z, blk), :]
+        v = v2[i, ds(z, blk), :]
+
+        def unit3(carry, qq, dd, qb, masked):
+            dk, dv = carry
+            qs = ds(qb, blk)
+            p = jnp.exp2(dotf(k, qq, NT) * cexp - ld2[i, 0:1, qs])
+            if masked:
+                p = jnp.where(c0 >= r0, p, 0.0)
+            g = (p * (dotf(v, dd, NT) - ld2[i, 1:2, qs])).astype(bf16)
+            return dk + dotf(g, qq, NN), dv + dotf(p.astype(bf16), dd, NN)
+
+        def later(qb, carry):
+            qs = ds(qb, blk)
+            return unit3(carry, k2[i, qs, :], v2[i, qs, :], qb, False)
+
+        zk = jnp.zeros((blk, HEAD), f32)
+        dk, dv = lax.fori_loop(z + 1, nb, later, unit3((zk, zk), q, do, z, True))
+        dkv2[i, 0] = (dk * scale).astype(bf16)
+        dkv2[i, 1] = dv.astype(bf16)
+        for w in range(2):
+            tkv[w, :, hs(h2(i))] = dkv2[i, w, rows(c), :]
+        att[:, hs(h2(i))] = o2[i, rows(c), :]
+        tq[:, hs(h2(i))] = dq2[i, rows(c), :]
+
+    def kv2_send(i):
+        return remote(dkv2.at[i, :, rows(1 - c), :], tkv.at[:, :, hs(h2(i))], s_kv2.at[0], r_kv2.at[0], mate)
+
+    pair = ld2.at[pl.ds(0, 1), pl.ds(0, 2)]
+    with scope('ldwait'):
+        @pl.when(mine_too)
+        def _():
+            settle(pair, r_ld2.at[0])
+            settle(ld2.at[:, pl.ds(0, nz - 1)], s_ld2.at[0])
+
+        @pl.when(jnp.logical_not(mine_too))
+        def _():
+            settle(ld2.at[:, pl.ds(0, 2)], r_ld2.at[0])
+
+        @pl.when(again & (home != c))
+        def _():
+            settle(ld2.at[:, pl.ds(0, nz)], s_ld2.at[0])
+    with scope('again'):
+        loop(0, 2, again_head)
+        for i in range(2):
+            o2_send(i).start()
+            q2_send(i).start()
+            kv2_send(i).start()
 
     def w_copies(t):
         slot = lax.rem(t, 2)
@@ -679,9 +894,18 @@
     with scope('dw'):
         loop(0, nt // 2, dw_step)
     with scope('waitkv'):
-        settle(tkv.at[:, pl.ds(0, t_loc - t_loc // n), :], s_kv.at[0], r_kv.at[0])
+        @pl.when(sent)
+        def _():
+            settle(tkv.at[:, pl.ds(0, (n - 1) * msg), :], s_kv.at[0])
+            settle(tkv.at[:, pl.ds(0, (n_sent - 1) * msg), :], r_kv.at[0])
+
+        @pl.when(again)
+        def _():
+            settle(tkv.at[:, pl.ds(0, n_sent * msg), :], r_kv.at[0])
+        settle(tkv.at[:, pl.ds(0, 2 * msg), :], s_kv2.at[0], r_kv2.at[0])
     with scope('waitq'):
-        settle(tq.at[pl.ds(0, t_loc - t_loc // n), :], s_q.at[0], r_q.at[0])
+        got(tq, s_q, r_q)
+        settle(tq.at[pl.ds(0, 2 * msg), :], s_q2.at[0], r_q2.at[0])
 
     mq = spread_col(mine2[0:1, :])
     mk = spread_col(mine2[1:2, :])
@@ -715,7 +939,7 @@
             xh = x_ref[:, hs(i)].astype(f32) * xinv[...]
             dhh = dh[:, hs(i)]
             gpart[i] = jnp.broadcast_to(jnp.sum(dhh * xh, axis=0, keepdims=True), (8, HEAD))
-            gx_s[:, hs(i)] = (gy_ref[:, hs(i)].astype(f32) + xinv[...] * (dhh * g_ref[2:3, hs(i)] - xh * mx)).astype(bf16)
+            xbuf[0, :, hs(i)] = (gy_ref[:, hs(i)].astype(f32) + xinv[...] * (dhh * g_ref[2:3, hs(i)] - xh * mx)).astype(bf16)
 
         loop(0, nd, gx_step)
         out(2).start()
@@ -727,13 +951,17 @@
         loop(nt // 2, nt, dw_step)
         out(4).start()
         out(5).start()
+    with scope('y'):
+        got(att, s_o, r_o)
+        settle(att.at[pl.ds(0, 2 * msg), :], s_o2.at[0], r_o2.at[0])
+        loop(0, nt, y_step)
+        out(0).start()
     with scope('end_drain'):
-        for a in range(2):
-            settle(alls[a].at[pl.ds(0, (nz - 1) * t_loc), :], s_ring.at[a])
-            settle(alls[a].at[pl.ds(0, nz * t_loc), :], s_par.at[a])
+        settle(gy_all.at[pl.ds(0, (nz - 1) * t_loc), :], s_ring.at[1])
+        settle(gy_all.at[pl.ds(0, nz * t_loc), :], s_par.at[1])
         settle(tkv, s_out.at[0])
-        settle(dwo_s, s_out.at[1])
-        settle(bv.at[pl.ds(0, 3)], s_out.at[2])
+        settle(raw.at[2, pl.ds(0, n * HEAD), :], s_out.at[1])
+        settle(raw.at[2, pl.ds(0, 3 * HEAD), :], s_out.at[2])
         settle(gg_s, s_out.at[3])
         settle(gpart.at[0], s_out.at[4])
     most = pl.ds(0, HEAD - HEAD // n)
@@ -762,11 +990,11 @@
         out_specs=[hb] * 10,
         out_shape=[S(tok, bf16), S(tok, bf16), S((n, 8, d // n), f32)] + [S((d // n, d), f32)] * 4 + [S((2, 8, HEAD), f32), S((t_all, d), bf16), S((t_all, d), bf16)],
         scratch_shapes=[V((1, t_loc), jnp.int32), V((d,), bf16), V((d,), bf16), V((d,), bf16), V((8, HEAD), f32), V(tok, bf16), V(tok, bf16), V((8, d), f32), V(tok, bf16), V((d, 3 * HEAD), bf16), V((HEAD, d), bf16), V((3,) + hd, f32), V((2,) + tok, bf16), V((2, d, 2 * HEAD), bf16), V((2, t_all, 2 * HEAD), bf16), V((2, 3, 2 * HEAD, d), bf16),
-            V((2,) + tok, f32), V((2, HEAD, t_all), f32), V((2, HEAD // 2, t_all), f32)] + [V(hd, bf16)] * 5 + [V((8, t_all), f32)] * 2
-        + [V(hd, bf16), V((n, 2, t_loc, HEAD), bf16), V(tok, bf16), V((2,) + tok, bf16), V(tok, bf16), V((HEAD, t_all), bf16), V((n, d // n, HEAD), f32), V((2 * HEAD, t_all), bf16), V(tok, bf16), V((HEAD, d), f32), V(tok, bf16), V(tok, f32),
-            V((2, t_loc, HEAD), f32), V((t_loc, HEAD), f32), V((t_loc, HEAD), f32), V((2, t_loc, HEAD), f32), V((t_loc, HEAD), f32), V((8, t_loc), f32), V((n, 8, t_loc), f32), V((8, t_loc), f32), V((n, 8, t_loc), f32), V((n, 8, t_loc), f32), V((n, 8, t_loc), f32), V((n, 8, d // n), f32), V((2, 8, HEAD), f32)]
+            V((2,) + tok, f32), V((2, HEAD, t_all), f32), V((2, HEAD // 2, t_all), f32)] + [V(hd, bf16)] * 5 + [V((8, t_all), f32), V((2, 8, t_all), f32)]
+        + [V(hd, bf16), V((n, 2, t_loc, HEAD), bf16), V(tok, bf16), V((2,) + tok, bf16), V(tok, bf16), V((2 * HEAD, t_all), bf16), V(tok, f32),
+            V((t_loc, HEAD), f32), V((t_loc, HEAD), f32), V((2, t_loc, HEAD), f32), V((t_loc, HEAD), f32), V((8, t_loc), f32), V((n, 8, t_loc), f32), V((8, t_loc), f32), V((n, 8, t_loc), f32), V((n, 8, t_loc), f32), V((n, 8, t_loc), f32), V((n, 8, d // n), f32), V((2, 8, HEAD), f32)] + [V((2, t_all, HEAD), bf16)] * 2 + [V((2, 2 * t_loc, HEAD), bf16)] * 4 + [V((2, 2, 2 * t_loc, HEAD), bf16)]
         + [sem((2,)), sem((2, 2, nz - 1, 2)), sem((2,)), sem((2, 2 * (nz - 1))), sem((2,))] + [sem((1,))] * 20
-        + [sem((2,)), sem((2,)), sem((2,)), sem((7,)), sem((2,)), sem((1,)), sem((5,)), sem((5,))],
+        + [sem((2,)), sem((2,)), sem((2,)), sem((7,)), sem((2,)), sem((1,)), sem((5,)), sem((5,)), sem((3,)), sem((2,))] + [sem((1,))] * 8,
         compiler_params=pltpu.CompilerParams(collective_id=1, has_side_effects=True, vmem_limit_bytes=67043328), name='block')(x, gy, pos, gq, gk, gn, freq, wq, wk, wv, wo)
 
 

time: 340 us -> 326 us (0.959)
  Pallas kernels: 337 us -> 323 us
    pallas_call x1, Pallas kernels: 332 us -> 317 us  [block(): pl.pallas_call(functools.partial(block_kernel, n), in_specs=[hb] * 11, ou...]
where the time goes in v6:
time: 326 us; the launch traced here: 324 us
  Pallas kernels  323 us (99%)
    pallas_call x1, Pallas kernels, block(): pl.pallas_call(functools.partial(block_kernel, n), in_specs=[hb] * 11, ou...  317 us

profile of v6, /device:TPU:21, one launch (start us, length us, event | category | flops | bytes accessed | tf_op | source)
XLA Modules:
  0.0 323.6 jit_solution(17263426535289485147)
XLA Ops:
  0.6 317.2 %block.1 = (bf16[256,2048]{1,0:T(8,128)(2,1)}, bf16[256,2048]{1,0:T(8,128)(2,1)}, f32[16,8,128]{2,1,0:T(8,128)}, f32[128,2048]{1,0:T(8,128)}, f32[128,2048]{1,0:...) custom-call(bf16[256,2048]{1,0:T(8,128)(2,1)} %bitcast.7, ...), custom_call_target="tpu_custom_call" | custom-call | tf_op jit(solution)/shard_map/block/pallas_call | solution.py:988
  317.9 5.5 %copy_out.1 = (bf16[256,2048]{1,0:T(8,128)(2,1)}, bf16[256,2048]{1,0:T(8,128)(2,1)}, f32[128,2048]{1,0:T(8,128)}, f32[128,2048]{1,0:T(8,128)}, f32[128,2048]{1,0...) custom-call(bf16[256,2048]{1,0:T(8,128)(2,1)} %get-tuple-element.26.refs_0_, ...), custom_call_target="tpu_custom_call" | custom-call | tf_op jit(solution)/shard_map/copy_out/pallas_call | solution.py:1027

commit v7 on v6

--- a/solution.py
+++ b/solution.py
@@ -55,7 +55,7 @@
                  pos_ref, gq_ref, gk_ref, gn1_ref, fr_ref, x_ref, gy_ref, g_ref, hid, wh, woh, raw, xbuf, wtile, tile, wrow, qkl, hatT, csT, q_s, k_s, v_s, do_s, o_s, lse, ld2,
                  dq_s, dkv, tq, tkv, att, rawT, dh, cl_s, sl_s, inv, xinv, mine, sall, mine2, mall, pm, pall, gpart, gg_s, k2, v2, q2, do2, o2, dq2, dkv2,
                  s_ring, r_ring, s_par, r_par, r_own, s_st, r_st, s_o, r_o, s_kv, r_kv, s_q, r_q, s_v, r_v, s_a, r_a, s_b, r_b, s_m, r_m, s_g, r_g, s_p, r_p,
-                 s_ld, s_t, s_w, s_x, s_wr, s_loc, s_out, s_in, s_r2, s_hu, s_o2, r_o2, s_q2, r_q2, s_kv2, r_kv2, s_ld2, r_ld2):
+                 s_ld, s_t, s_w, s_x, s_wr, s_loc, s_out, s_in, s_r2, s_hu, s_o2, r_o2, s_q2, r_q2, s_kv2, r_kv2, s_ld2, r_ld2, s_w4):
     me = lax.axis_index('sp')
     t_loc, d = x_hbm.shape
     t_all = t_loc * n
@@ -83,13 +83,22 @@
     alls = (h_all, gy_all)
     own_src = (hid, gy_hbm)
 
-    again = lax.rem(me, 4) == 0
-    sent = lax.rem(me, 4) != 0
+    again = c == 0
+    sent = c == 1
     n_sent = n - n // 4
     msg = t_loc // n
 
     def h2(i):
-        return c * (n // 2) + 4 * i
+        return 2 * lax.rem(z, 2) + c * (n // 2) + 4 * i
+
+    def to_send(to):
+        return sent | (lax.rem(to // 2 + z, 2) == 1)
+
+    def send_all(make, es):
+        for e in es:
+            @pl.when(to_send(peer(e)))
+            def _():
+                make(e).start()
 
     def w2(act):
         for i in range(2):
@@ -488,15 +497,13 @@
         with scope('attend'):
             loop(lo, hi, attend)
 
-        @pl.when((t == ticks - 3) & sent)
-        def _():
-            for e in far[-5:]:
-                o_send(e).start()
-
-        @pl.when((t == ticks - 2) & sent)
-        def _():
-            for e in far[:-5]:
-                o_send(e).start()
+        @pl.when(t == ticks - 3)
+        def _():
+            send_all(o_send, far[-5:])
+
+        @pl.when(t == ticks - 2)
+        def _():
+            send_all(o_send, far[:-5])
 
         @pl.when(t == -1)
         def _():
@@ -527,8 +534,11 @@
     def h2_copy(t):
         return pltpu.make_async_copy(h_all.at[:, ds(chip(t), cw)], tile.at[lax.rem(t, 2)], s_t.at[lax.rem(t, 2)])
 
-    def wo_copy(t):
-        return pltpu.make_async_copy(wo_ref.at[:, ds(t, cw)], wtile.at[lax.rem(t, 2)], s_w.at[lax.rem(t, 2)])
+    hw = d // 2
+
+    def wo_half(h):
+        k = lax.rem(h, 2)
+        return pltpu.make_async_copy(wo_ref.at[ds(k, hw), ds(h // 2, cw)], wtile.at[lax.rem(h // 2, 2), ds(k, hw), :], s_w4.at[lax.rem(h, 4)])
 
     def q_send(e):
         to = peer(e)
@@ -538,7 +548,8 @@
         return remote(dkv.at[to], tkv.at[:, :, cols], s_kv.at[0], r_kv.at[0], to)
 
     gy_copy(0).start()
-    wo_copy(0).start()
+    for h in range(4):
+        wo_half(h).start()
     settle(h_all.at[pl.ds(0, (nz - 1) * t_loc), :], s_ring.at[0])
     settle(h_all.at[pl.ds(0, nz * t_loc), :], s_par.at[0])
 
@@ -554,8 +565,8 @@
     with scope('delta'):
         loop(0, nb, delta)
 
-    home = me // (n // 2)
-    slot2 = lax.rem(me, n // 2) // 4
+    home = z // (nz // 2)
+    slot2 = lax.rem(z // 2, 2)
     mine_too = again & (home == c)
 
     def ld_send(k):
@@ -564,7 +575,7 @@
 
     @pl.when(again)
     def _():
-        for k in (4, 3, 5, 2, 6, 1, 7):
+        for k in (4, 2, 6):
             ld_send(k).start()
 
     @pl.when(again & (home != c))
@@ -606,7 +617,7 @@
             dkv[2 * kb + u, 0] = dk[u * t_loc:(u + 1) * t_loc]
             dkv[2 * kb + u, 1] = dv[u * t_loc:(u + 1) * t_loc]
 
-        @pl.when((kb != z) & sent)
+        @pl.when((kb != z) & to_send(2 * kb))
         def _():
             for u in range(2):
                 kv_send(2 * kb + u).start()
@@ -645,10 +656,10 @@
         sums = lax.fori_loop(0, n, share_step, (zt, zt))
     for e in far:
         p_send(e).start()
+    send_all(q_send, far)
+
     @pl.when(sent)
     def _():
-        for e in far:
-            q_send(e).start()
         tq[:, cols] = dq_s[rows(me), :]
         tkv[:, :, cols] = dkv[me]
 
@@ -691,13 +702,17 @@
             raw[2, hs((t - nt) * (cw // HEAD) + u), :] = r[:, u * HEAD:(u + 1) * HEAD].T
 
     def y_step(t):
-        wo_copy(t).wait()
-
-        @pl.when(t + 1 < nt)
-        def _():
-            wo_copy(t + 1).start()
         cs = ds(t, cw)
-        hid[:, cs] = (x_ref[:, cs].astype(f32) + dotf(att[...], wtile[lax.rem(t, 2)], NN)).astype(bf16)
+        acc = x_ref[:, cs].astype(f32)
+        for k in range(2):
+            h = 2 * t + k
+            wo_half(h).wait()
+            acc = acc + dotf(att[:, k * hw:(k + 1) * hw], wtile[lax.rem(t, 2), k * hw:(k + 1) * hw, :], NN)
+
+            @pl.when(h + 4 < 2 * nt)
+            def _():
+                wo_half(h + 4).start()
+        hid[:, cs] = acc.astype(bf16)
 
     def v_send(e):
         to = peer(e)
@@ -744,6 +759,7 @@
 
         @pl.when(again)
         def _():
+            settle(buf.at[pl.ds(0, n // 2 * msg), :], s_sem.at[0])
             settle(buf.at[pl.ds(0, n_sent * msg), :], r_sem.at[0])
 
     def o2_send(i):
@@ -823,7 +839,7 @@
         @pl.when(mine_too)
         def _():
             settle(pair, r_ld2.at[0])
-            settle(ld2.at[:, pl.ds(0, nz - 1)], s_ld2.at[0])
+            settle(ld2.at[:, pl.ds(0, nz // 2 - 1)], s_ld2.at[0])
 
         @pl.when(jnp.logical_not(mine_too))
         def _():
@@ -831,13 +847,13 @@
 
         @pl.when(again & (home != c))
         def _():
-            settle(ld2.at[:, pl.ds(0, nz)], s_ld2.at[0])
-    with scope('again'):
-        loop(0, 2, again_head)
-        for i in range(2):
-            o2_send(i).start()
-            q2_send(i).start()
-            kv2_send(i).start()
+            settle(ld2.at[:, pl.ds(0, nz // 2)], s_ld2.at[0])
+    def again_both(i):
+        again_head(i)
+        o2_send(i).start()
+        q2_send(i).start()
+        kv2_send(i).start()
+
 
     def w_copies(t):
         slot = lax.rem(t, 2)
@@ -856,16 +872,10 @@
         tq[:, hs(i)] = (inv[0] * (back_rope(tq[:, hs(i)]) * g_ref[0:1, hs(i)] - qkl[0, :, hs(i)] * inv[0] * mq)).astype(bf16)
         tkv[0, :, hs(i)] = (inv[1] * (back_rope(tkv[0, :, hs(i)]) * g_ref[1:2, hs(i)] - qkl[1, :, hs(i)] * inv[1] * mk)).astype(bf16)
 
-    with scope('mwait'):
-        settle(mall.at[pl.ds(0, n - 1), pl.ds(0, 2)], s_m.at[0], r_m.at[0])
-
     def head_step(j):
         js = rows(j)
         for w, src in enumerate((dq_s[js, :], dkv[j, 0])):
             rawT[w * HEAD:(w + 1) * HEAD, js] = (sall[j, w:w + 1, :] * (unroped(src, js) * gcol[w] - hatT[w, :, js] * mall[j, w:w + 1, :])).astype(bf16)
-
-    with scope('head'):
-        loop(0, n, head_step)
 
     def a_send(to):
         return remote(raw.at[1, rows_f(0, to), :], dwq_out.at[:, cols], s_a.at[0], r_a.at[0], to)
@@ -891,8 +901,20 @@
                 a_send(to).start()
                 b_send(to).start()
 
-    with scope('dw'):
-        loop(0, nt // 2, dw_step)
+    def phase(i):
+        with scope('again'):
+            again_both(i)
+
+        @pl.when(i == 0)
+        def _():
+            with scope('mwait'):
+                settle(mall.at[pl.ds(0, n - 1), pl.ds(0, 2)], s_m.at[0], r_m.at[0])
+            with scope('head'):
+                loop(0, n, head_step)
+            with scope('dw'):
+                loop(0, nt - 2, dw_step)
+
+    loop(0, 2, phase)
     with scope('waitkv'):
         @pl.when(sent)
         def _():
@@ -901,6 +923,7 @@
 
         @pl.when(again)
         def _():
+            settle(tkv.at[:, pl.ds(0, n // 2 * msg), :], s_kv.at[0])
             settle(tkv.at[:, pl.ds(0, n_sent * msg), :], r_kv.at[0])
         settle(tkv.at[:, pl.ds(0, 2 * msg), :], s_kv2.at[0], r_kv2.at[0])
     with scope('waitq'):
@@ -948,7 +971,7 @@
     out(7).start()
     out(6).start()
     with scope('dw2'):
-        loop(nt // 2, nt, dw_step)
+        loop(nt - 2, nt, dw_step)
         out(4).start()
         out(5).start()
     with scope('y'):
@@ -994,7 +1017,7 @@
         + [V(hd, bf16), V((n, 2, t_loc, HEAD), bf16), V(tok, bf16), V((2,) + tok, bf16), V(tok, bf16), V((2 * HEAD, t_all), bf16), V(tok, f32),
             V((t_loc, HEAD), f32), V((t_loc, HEAD), f32), V((2, t_loc, HEAD), f32), V((t_loc, HEAD), f32), V((8, t_loc), f32), V((n, 8, t_loc), f32), V((8, t_loc), f32), V((n, 8, t_loc), f32), V((n, 8, t_loc), f32), V((n, 8, t_loc), f32), V((n, 8, d // n), f32), V((2, 8, HEAD), f32)] + [V((2, t_all, HEAD), bf16)] * 2 + [V((2, 2 * t_loc, HEAD), bf16)] * 4 + [V((2, 2, 2 * t_loc, HEAD), bf16)]
         + [sem((2,)), sem((2, 2, nz - 1, 2)), sem((2,)), sem((2, 2 * (nz - 1))), sem((2,))] + [sem((1,))] * 20
-        + [sem((2,)), sem((2,)), sem((2,)), sem((7,)), sem((2,)), sem((1,)), sem((5,)), sem((5,)), sem((3,)), sem((2,))] + [sem((1,))] * 8,
+        + [sem((2,)), sem((2,)), sem((2,)), sem((7,)), sem((2,)), sem((1,)), sem((5,)), sem((5,)), sem((3,)), sem((2,))] + [sem((1,))] * 8 + [sem((4,))],
         compiler_params=pltpu.CompilerParams(collective_id=1, has_side_effects=True, vmem_limit_bytes=67043328), name='block')(x, gy, pos, gq, gk, gn, freq, wq, wk, wv, wo)
 
 

time: 326 us -> 325 us (level)
  no operation moved by 1% of the time
where the time goes in v7:
time: 325 us; the launch traced here: 323 us
  Pallas kernels  322 us (99%)
    pallas_call x1, Pallas kernels, block(): pl.pallas_call(functools.partial(block_kernel, n), in_specs=[hb] * 11, ou...  317 us

profile of v7, /device:TPU:21, one launch (start us, length us, event | category | flops | bytes accessed | tf_op | source)
XLA Modules:
  0.0 323.2 jit_solution(18308175780063028424)
XLA Ops:
  0.6 316.9 %block.1 = (bf16[256,2048]{1,0:T(8,128)(2,1)}, bf16[256,2048]{1,0:T(8,128)(2,1)}, f32[16,8,128]{2,1,0:T(8,128)}, f32[128,2048]{1,0:T(8,128)}, f32[128,2048]{1,0:...) custom-call(bf16[256,2048]{1,0:T(8,128)(2,1)} %bitcast.7, ...), custom_call_target="tpu_custom_call" | custom-call | tf_op jit(solution)/shard_map/block/pallas_call | solution.py:1011
  317.5 5.5 %copy_out.1 = (bf16[256,2048]{1,0:T(8,128)(2,1)}, bf16[256,2048]{1,0:T(8,128)(2,1)}, f32[128,2048]{1,0:T(8,128)}, f32[128,2048]{1,0:T(8,128)}, f32[128,2048]{1,0...) custom-call(bf16[256,2048]{1,0:T(8,128)(2,1)} %get-tuple-element.26.refs_0_, ...), custom_call_target="tpu_custom_call" | custom-call | tf_op jit(solution)/shard_map/copy_out/pallas_call | solution.py:1050

commit v8 on v7

--- a/solution.py
+++ b/solution.py
@@ -85,14 +85,15 @@
 
     again = c == 0
     sent = c == 1
-    n_sent = n - n // 4
     msg = t_loc // n
 
     def h2(i):
-        return 2 * lax.rem(z, 2) + c * (n // 2) + 4 * i
+        off = jnp.where(i == 0, nz // 2, jnp.where(c == 0, 2, nz - 2))
+        return lax.rem(z + off, nz) * 2 + jnp.where(i == 0, c, 0)
 
     def to_send(to):
-        return sent | (lax.rem(to // 2 + z, 2) == 1)
+        gap = lax.rem(to // 2 + nz - z, nz)
+        return (gap != nz // 2) & (sent | ((gap != 2) & (gap != nz - 2)))
 
     def send_all(make, es):
         for e in es:
@@ -553,9 +554,7 @@
     settle(h_all.at[pl.ds(0, (nz - 1) * t_loc), :], s_ring.at[0])
     settle(h_all.at[pl.ds(0, nz * t_loc), :], s_par.at[0])
 
-    @pl.when(sent)
-    def _():
-        att[:, cols] = o_s[rows(me), :]
+    att[:, cols] = o_s[rows(me), :]
     raw[0] = jnp.zeros((t_all, HEAD), f32)
 
     def delta(j):
@@ -565,29 +564,19 @@
     with scope('delta'):
         loop(0, nb, delta)
 
-    home = z // (nz // 2)
-    slot2 = lax.rem(z // 2, 2)
-    mine_too = again & (home == c)
-
-    def ld_send(k):
-        to = lax.rem(z + k, nz) * 2 + home
-        return remote(lse.at[pl.ds(0, 2)], ld2.at[slot2, pl.ds(0, 2)], s_ld2.at[0], r_ld2.at[0], to)
+    def ld_send(gap, core, slot):
+        to = lax.rem(z + gap, nz) * 2 + core
+        return remote(lse.at[pl.ds(0, 2)], ld2.at[slot, pl.ds(0, 2)], s_ld2.at[0], r_ld2.at[0], to)
+
+    ld_send(nz // 2, c, 0).start()
 
     @pl.when(again)
     def _():
-        for k in (4, 2, 6):
-            ld_send(k).start()
-
-    @pl.when(again & (home != c))
-    def _():
-        ld_send(0).start()
-
-    @pl.when(mine_too)
-    def _():
-        ld2[slot2, 0:2, :] = lse[0:2, :]
+        ld_send(nz - 2, 0, 1).start()
+        ld_send(2, 1, 1).start()
 
     def bwd_step(s):
-        kb = chip(s)
+        kb = chip(lax.rem(s + 1, nz))
         ks = ds(kb, blk)
         k = k_s[ks, :]
         v = v_s[ks, :]
@@ -622,7 +611,7 @@
             for u in range(2):
                 kv_send(2 * kb + u).start()
 
-        @pl.when((kb == z) & sent)
+        @pl.when(kb == z)
         def _():
             kv_send(mate).start()
 
@@ -658,10 +647,8 @@
         p_send(e).start()
     send_all(q_send, far)
 
-    @pl.when(sent)
-    def _():
-        tq[:, cols] = dq_s[rows(me), :]
-        tkv[:, :, cols] = dkv[me]
+    tq[:, cols] = dq_s[rows(me), :]
+    tkv[:, :, cols] = dkv[me]
 
     pall[me, 0:2, :] = pm[me, 0:2, :]
     for w in range(2):
@@ -752,15 +739,15 @@
     for e in far:
         v_send(e).start()
     def got(buf, s_sem, r_sem):
+        settle(buf.at[pl.ds(0, (n - 5) * msg), :], r_sem.at[0])
+
         @pl.when(sent)
         def _():
-            settle(buf.at[pl.ds(0, (n - 1) * msg), :], s_sem.at[0])
-            settle(buf.at[pl.ds(0, (n_sent - 1) * msg), :], r_sem.at[0])
+            settle(buf.at[pl.ds(0, (n - 3) * msg), :], s_sem.at[0])
 
         @pl.when(again)
         def _():
-            settle(buf.at[pl.ds(0, n // 2 * msg), :], s_sem.at[0])
-            settle(buf.at[pl.ds(0, n_sent * msg), :], r_sem.at[0])
+            settle(buf.at[pl.ds(0, (n - 7) * msg), :], s_sem.at[0])
 
     def o2_send(i):
         return remote(o2.at[i, rows(1 - c), :], att.at[:, hs(h2(i))], s_o2.at[0], r_o2.at[0], mate)
@@ -836,18 +823,16 @@
 
     pair = ld2.at[pl.ds(0, 1), pl.ds(0, 2)]
     with scope('ldwait'):
-        @pl.when(mine_too)
-        def _():
-            settle(pair, r_ld2.at[0])
-            settle(ld2.at[:, pl.ds(0, nz // 2 - 1)], s_ld2.at[0])
-
-        @pl.when(jnp.logical_not(mine_too))
-        def _():
-            settle(ld2.at[:, pl.ds(0, 2)], r_ld2.at[0])
-
-        @pl.when(again & (home != c))
-        def _():
-            settle(ld2.at[:, pl.ds(0, nz // 2)], s_ld2.at[0])
+        settle(ld2.at[:, pl.ds(0, 2)], r_ld2.at[0])
+
+        @pl.when(sent)
+        def _():
+            settle(pair, s_ld2.at[0])
+
+        @pl.when(again)
+        def _():
+            settle(ld2.at[:, pl.ds(0, 3)], s_ld2.at[0])
+
     def again_both(i):
         again_head(i)
         o2_send(i).start()
@@ -916,15 +901,15 @@
 
     loop(0, 2, phase)
     with scope('waitkv'):
+        settle(tkv.at[:, pl.ds(0, (n - 5) * msg), :], r_kv.at[0])
+
         @pl.when(sent)
         def _():
-            settle(tkv.at[:, pl.ds(0, (n - 1) * msg), :], s_kv.at[0])
-            settle(tkv.at[:, pl.ds(0, (n_sent - 1) * msg), :], r_kv.at[0])
+            settle(tkv.at[:, pl.ds(0, (n - 3) * msg), :], s_kv.at[0])
 
         @pl.when(again)
         def _():
-            settle(tkv.at[:, pl.ds(0, n // 2 * msg), :], s_kv.at[0])
-            settle(tkv.at[:, pl.ds(0, n_sent * msg), :], r_kv.at[0])
+            settle(tkv.at[:, pl.ds(0, (n - 7) * msg), :], s_kv.at[0])
         settle(tkv.at[:, pl.ds(0, 2 * msg), :], s_kv2.at[0], r_kv2.at[0])
     with scope('waitq'):
         got(tq, s_q, r_q)

time: 325 us -> 324 us (level)
  no operation moved by 1% of the time
where the time goes in v8:
time: 324 us; the launch traced here: 322 us
  Pallas kernels  322 us (99%)
    pallas_call x1, Pallas kernels, block(): pl.pallas_call(functools.partial(block_kernel, n), in_specs=[hb] * 11, ou...  316 us

profile of v8, /device:TPU:21, one launch (start us, length us, event | category | flops | bytes accessed | tf_op | source)
XLA Modules:
  0.0 322.4 jit_solution(10908107582296978476)
XLA Ops:
  0.6 316.1 %block.1 = (bf16[256,2048]{1,0:T(8,128)(2,1)}, bf16[256,2048]{1,0:T(8,128)(2,1)}, f32[16,8,128]{2,1,0:T(8,128)}, f32[128,2048]{1,0:T(8,128)}, f32[128,2048]{1,0:...) custom-call(bf16[256,2048]{1,0:T(8,128)(2,1)} %bitcast.7, ...), custom_call_target="tpu_custom_call" | custom-call | tf_op jit(solution)/shard_map/block/pallas_call | solution.py:996
  316.7 5.5 %copy_out.1 = (bf16[256,2048]{1,0:T(8,128)(2,1)}, bf16[256,2048]{1,0:T(8,128)(2,1)}, f32[128,2048]{1,0:T(8,128)}, f32[128,2048]{1,0:T(8,128)}, f32[128,2048]{1,0...) custom-call(bf16[256,2048]{1,0:T(8,128)(2,1)} %get-tuple-element.26.refs_0_, ...), custom_call_target="tpu_custom_call" | custom-call | tf_op jit(solution)/shard_map/copy_out/pallas_call | solution.py:1035
